TPU v7x, 768 devices: a whole 4x8x12 slice. The times are simulated.
768 devices in a mesh: gx: 16 (over y, z_hi), gy: 4 (over x), gz: 12 (over z_lo, core).
Axes of the slice: x: 4, y: 8, z: 12 (z_hi: 2, z_lo: 6; z = z_hi * 6 + z_lo), core: 2. Of those that a mesh axis runs over, the one named last changes fastest.
Arguments:
- pressure_now: float32 [256, 128, 1536], P('gx', 'gy', 'gz'), may hold values from -6 to 6
- pressure_before: float32 [256, 128, 1536], P('gx', 'gy', 'gz'), may hold values from -6 to 6
- region_code: int32 [256, 128, 1536], P('gx', 'gy', 'gz'), may hold values from 0 to 7
- velocity: float32 [8], replicated, may hold values from 0.2 to 0.42
- wavelet: float32 [6, 16], replicated, may hold values from -6 to 6
- source_cell: int32 [16], replicated, may hold values from 0 to 50331647
Outputs:
- pressure: float32 [256, 128, 1536], P('gx', 'gy', 'gz')
- previous: float32 [256, 128, 1536], P('gx', 'gy', 'gz')
Inputs may be any that keep to these rules, and one draw needn't show every extreme that they name: source_cell[s] is the flat index x * 128 * 1536 + y * 1536 + z of a grid cell; sources may share a cell.
All inputs are finite; a program needn't handle non-finite values.
Results may differ from a plain program's by a relative error of at most 0.00002.
Values sent between devices are 32-bit elements; how exact they have to be, the bound alone decides.
No kernel may reach another device: no remote copies, remote signals or barrier semaphores. Data moves between devices by JAX's collectives and lax.ppermute only.
A program may use at most 32 MiB of HBM per device.

v0:
```python
import jax
import jax.numpy as jnp
from jax import lax
from jax.experimental import pallas as pl
from jax.experimental.pallas import tpu as pltpu
from jax.sharding import PartitionSpec as P


STEPS = 6
CENTRE = -205.0 / 72.0
WEIGHTS = (8.0 / 5.0, -1.0 / 5.0, 8.0 / 315.0, -1.0 / 560.0)
HALO = 4
DEEP = HALO * STEPS
VMEM = pl.BlockSpec(memory_space=pltpu.VMEM)


def extra(step):
    return DEEP - HALO * (step + 1)


def matmul(a, b, contract):
    return lax.dot_general(
        a, b, (contract, ((), ())), precision=lax.Precision.HIGHEST, preferred_element_type=jnp.float32
    )


def chosen(columns, nz):
    row = lax.broadcasted_iota(jnp.int32, (2 * columns, nz), 0)
    lane = lax.broadcasted_iota(jnp.int32, (2 * columns, nz), 1)
    wanted = jnp.where(row < columns, row, row + nz - 2 * columns)
    return jnp.where(lane == wanted, jnp.float32(1), jnp.float32(0))


def packed(rows, columns):
    return matmul(chosen(columns, rows.shape[1]), rows, ((1,), (1,)))


def unpacked(block, columns, nz):
    return matmul(block, chosen(columns, nz), ((0,), (0,)))


def pack_faces(field, columns, pair, y_low, y_high, rows):
    _, nx, ny, nz = field.shape
    odd = lax.axis_index("gx") % 2
    inner = (1 - odd) * (nx - HALO)
    outer = odd * (nx - HALO)
    face = HALO * ny
    for place, first in ((0, inner), (face + 2 * columns, outer)):
        pair[place : place + face, :] = field[0, pl.ds(first, HALO)].reshape(face, nz)
        if columns:
            pair[place + face : place + face + 2 * columns, :] = packed(
                field[1, pl.ds(first, HALO)].reshape(face, nz), columns
            )
    for y_face, y in ((y_low, 0), (y_high, ny - HALO)):
        for x in range(nx):
            y_face[HALO * x : HALO * (x + 1), :] = field[0, x, y : y + HALO, :]
        if columns:
            for x in range(nx):
                rows[HALO * x : HALO * (x + 1), :] = field[1, x, y : y + HALO, :]
            y_face[HALO * nx : HALO * nx + 2 * columns, 0 : HALO * nx] = packed(rows[...], columns)


def first_kernel(velocity_in, now_in, before_in, codes_in, rate, z_low, z_high, velocity, now, before, codes, arrived):
    nx, ny, nz = now.shape
    regions = velocity.shape[0]
    copies = [
        pltpu.make_async_copy(source, target, arrived.at[n])
        for n, (source, target) in enumerate(
            ((velocity_in, velocity), (codes_in, codes), (now_in, now), (before_in, before))
        )
    ]
    for copy in copies:
        copy.start()
    copies[0].wait()
    copies[1].wait()
    squares = [velocity[r] * velocity[r] for r in range(regions)]
    for x in range(nx):
        code = codes[x]
        value = jnp.full(code.shape, squares[0], jnp.float32)
        for r in range(1, regions):
            value = jnp.where(code == r, squares[r], value)
        rate[x] = value
    copies[2].wait()
    copies[3].wait()
    for place, field in enumerate((now, before, rate)):
        both = packed(field[...].reshape(nx * ny, nz), DEEP)
        z_low[place * DEEP : (place + 1) * DEEP, :] = both[0:DEEP]
        z_high[place * DEEP : (place + 1) * DEEP, :] = both[DEEP : 2 * DEEP]


def widen_kernel(now, before, rate, from_low, from_high, wide_now, wide_before, wide_rate, pair, y_low, y_high, rows):
    nx, ny, nz = now.shape
    for place, (field, wide) in enumerate(((now, wide_now), (before, wide_before), (rate, wide_rate))):
        wide[0] = field[...]
        part = slice(place * DEEP, (place + 1) * DEEP)
        block = jnp.concatenate([from_high[part, :], from_low[part, :]], axis=0)
        wide[1] = unpacked(block, DEEP, nz).reshape(nx, ny, nz)
    pack_faces(wide_now, extra(0), pair, y_low, y_high, rows)


def part_one(step, now, before, rate, cells, amounts, y_low, y_high, *rest):
    following, wide = rest[0], rest[-1]
    columns = extra(step)
    tiles = 2 if columns else 1
    _, nx, ny, nz = now.shape
    for t in range(tiles):
        for place, y_face in ((8 - HALO, y_low), (8 + ny, y_high)):
            if t == 0:
                face = y_face[0 : HALO * nx, :]
            else:
                face = unpacked(y_face[HALO * nx : HALO * nx + 2 * columns, 0 : HALO * nx], columns, nz)
            for x in range(nx):
                wide[t, x, place : place + HALO, :] = face[HALO * x : HALO * (x + 1), :]
        for x in range(nx):
            wide[t, x, 8 : 8 + ny, :] = now[t, x]
    both = jnp.concatenate([now[0].reshape(nx * ny, nz), now[1].reshape(nx * ny, nz)], axis=1)
    i = lax.broadcasted_iota(jnp.int32, (2 * nz, tiles * nz), 0)
    j = lax.broadcasted_iota(jnp.int32, (2 * nz, tiles * nz), 1)
    distance = jnp.abs(i - j)
    distance = jnp.minimum(distance, 2 * nz - distance)
    band = jnp.zeros(distance.shape, jnp.float32)
    for k, weight in enumerate(WEIGHTS, 1):
        band = jnp.where(distance == k, jnp.float32(weight), band)
    along_z = matmul(both, band, ((1,), (0,)))
    for t in range(tiles):
        mine = along_z[:, t * nz : (t + 1) * nz].reshape(nx, ny, nz)
        for x in range(nx):
            here = now[t, x]
            total = jnp.float32(3.0 * CENTRE) * here + mine[x]
            for k, weight in enumerate(WEIGHTS, 1):
                around = wide[t, x, 8 + k : 8 + k + ny, :] + wide[t, x, 8 - k : 8 - k + ny, :]
                if x + k < nx:
                    around = around + now[t, x + k]
                if x - k >= 0:
                    around = around + now[t, x - k]
                total = total + jnp.float32(weight) * around
            value = 2.0 * here - before[t, x] + rate[t, x] * total
            if tiles == 2:
                following[t, x] = value
            else:
                following[x] = value
    if tiles == 1:
        rest[1][...] = now[0]

    @pl.when(jnp.max(cells[...]) >= 0)
    def _():
        lanes = lax.broadcasted_iota(jnp.int32, (1, nz), 1)
        numbers = [jnp.max(cells[s : s + 1, :]) for s in range(cells.shape[0])]
        for s, number in enumerate(numbers):

            @pl.when((number >= 0) & (number < tiles * nx * ny * nz))
            def _():
                line_of = number // nz
                y = line_of % ny
                x = line_of // ny % nx
                if tiles == 2:
                    here = following.at[line_of // (nx * ny), x]
                else:
                    here = following.at[x]
                row = here[pl.ds(y, 1), :]
                here[pl.ds(y, 1), :] = row + jnp.where(lanes == number % nz, amounts[s : s + 1, :], jnp.float32(0))


def part_two(step, partial, rate, inner, outer, following, *rest):
    columns = extra(step)
    tiles = 2 if columns else 1
    _, nx, ny, nz = rate.shape
    if tiles == 2:
        pair, y_low, y_high, halo, rows = rest
    else:
        (halo,) = rest
    odd = lax.axis_index("gx") % 2
    face = HALO * ny
    for block, first in ((inner, (1 - odd) * HALO), (outer, odd * HALO)):
        halo[0, pl.ds(first, HALO)] = block[0:face, :].reshape(HALO, ny, nz)
        if columns:
            halo[1, pl.ds(first, HALO)] = unpacked(block[face : face + 2 * columns, :], columns, nz).reshape(HALO, ny, nz)
    for t in range(tiles):
        for x in range(nx):
            total = None
            for k, weight in enumerate(WEIGHTS, 1):
                for at in (x - k, x + k):
                    if 0 <= at < nx:
                        continue
                    term = jnp.float32(weight) * halo[t, at + HALO if at < 0 else at - nx + HALO]
                    total = term if total is None else total + term
            value = partial[t, x] if tiles == 2 else partial[x]
            if total is not None:
                value = value + rate[t, x] * total
            if tiles == 2:
                following[t, x] = value
            else:
                following[x] = value

    if tiles == 2:
        pack_faces(following, extra(step + 1), pair, y_low, y_high, rows)


def arrays(*shapes):
    return tuple(jax.ShapeDtypeStruct(s, jnp.float32) for s in shapes)


def face_shapes(shape, columns):
    nx, ny, nz = shape
    return (
        (2 * (HALO * ny + 2 * columns), nz),
        (HALO * nx + 2 * columns, nz),
        (HALO * nx + 2 * columns, nz),
    )


def call(kernel, out, inputs, operands, scratch=()):
    return pl.pallas_call(
        kernel,
        out_shape=out,
        in_specs=inputs,
        out_specs=(VMEM,) * len(out),
        scratch_shapes=[pltpu.VMEM(s, jnp.float32) for s in scratch],
        compiler_params=pltpu.CompilerParams(vmem_limit_bytes=16 * 1024 * 1024),
        cost_estimate=pl.CostEstimate(flops=5000000, bytes_accessed=1500000, transcendentals=0),
    )(*operands)


def line(count):
    return [(i, i + 1) for i in range(count - 1)]


def back(pairs):
    return [(b, a) for a, b in pairs]


def exchange(faces, ny, columns):
    pair, y_low, y_high = faces
    half = HALO * ny + 2 * columns
    count = lax.axis_size("gx")
    swapped = lax.ppermute(pair, "gx", [(i, i ^ 1) for i in range(count)])
    up = line(lax.axis_size("gy"))
    from_y_low = lax.ppermute(y_high, "gy", up)
    from_y_high = lax.ppermute(y_low, "gy", back(up))
    onward = [(i, (i + 2 - 4 * (i % 2)) % count) for i in range(count)]
    outer = lax.ppermute(swapped[half:], "gx", onward)
    return swapped[:half], outer, from_y_low, from_y_high


def per_device(pressure_now, pressure_before, region_code, velocity, wavelet, source_cell):
    shape = pressure_now.shape
    nx, ny, nz = shape
    field = (2,) + shape
    rows = (HALO * nx, nz)
    grid_y = ny * lax.axis_size("gy")
    grid_z = nz * lax.axis_size("gz")
    x = source_cell // (grid_y * grid_z) - lax.axis_index("gx") * nx
    y = source_cell // grid_z % grid_y - lax.axis_index("gy") * ny
    z = source_cell % grid_z - lax.axis_index("gz") * nz
    inside = (x >= 0) & (x < nx) & (y >= 0) & (y < ny) & (z >= -DEEP) & (z < nz + DEEP)
    place = jnp.where(z < 0, z + 2 * nz, z)
    cells = jnp.where(inside, (((place // nz) * nx + x) * ny + y) * nz + place % nz, -1)
    cells = jnp.broadcast_to(cells[:, None], (cells.shape[0], nz))
    amounts = [jnp.broadcast_to(wavelet[step][:, None], (wavelet.shape[1], nz)) for step in range(STEPS)]

    deep = (3 * DEEP, nx * ny)
    in_hbm = pl.BlockSpec(memory_space=pltpu.HBM)
    rate, z_low, z_high = pl.pallas_call(
        first_kernel,
        out_shape=arrays(shape, deep, deep),
        in_specs=[in_hbm] * 4,
        out_specs=(VMEM,) * 3,
        scratch_shapes=[
            pltpu.SMEM(velocity.shape, jnp.float32),
            pltpu.VMEM(shape, jnp.float32),
            pltpu.VMEM(shape, jnp.float32),
            pltpu.VMEM(shape, jnp.int32),
            pltpu.SemaphoreType.DMA((4,)),
        ],
        compiler_params=pltpu.CompilerParams(vmem_limit_bytes=16 * 1024 * 1024),
        cost_estimate=pl.CostEstimate(flops=5000000, bytes_accessed=1500000, transcendentals=0),
        name="first",
    )(*(pltpu.with_memory_space_constraint(a, pltpu.HBM) for a in (velocity, pressure_now, pressure_before, region_code)))
    up = line(lax.axis_size("gz"))
    from_low = lax.ppermute(z_high, "gz", up)
    from_high = lax.ppermute(z_low, "gz", back(up))
    from_low, from_high, cells, *amounts = lax.optimization_barrier((from_low, from_high, cells, *amounts))
    current, before, rate, *faces = call(
        widen_kernel,
        arrays(field, field, field, *face_shapes(shape, extra(0))),
        [VMEM] * 5,
        (pressure_now, pressure_before, rate, from_low, from_high),
        scratch=[rows],
    )
    for step in range(STEPS):
        last = step == STEPS - 1
        inner, outer, y_low, y_high = exchange(faces, ny, extra(step))
        out = call(
            lambda *refs, step=step: part_one(step, *refs),
            arrays(shape, shape) if last else arrays(field),
            [VMEM] * 7,
            (current, before, rate, cells, amounts[step], y_low, y_high),
            scratch=[(2, nx, ny + 16, nz)],
        )
        partial = out[0]
        following, *faces = call(
            lambda *refs, step=step: part_two(step, *refs),
            arrays(shape) if last else arrays(field, *face_shapes(shape, extra(step + 1))),
            [VMEM] * 4,
            (partial, rate, inner, outer),
            scratch=[(2, 2 * HALO, ny, nz)] if last else [(2, 2 * HALO, ny, nz), rows],
        )
        before, current = (out[1], following) if last else (current, following)
    return current, before


def solution(mesh):
    field = P("gx", "gy", "gz")
    return jax.shard_map(
        per_device,
        mesh=mesh,
        in_specs=(field, field, field, P(), P(), P()),
        out_specs=(field, field),
        check_vma=False,
    )
```

profile of v0, /device:TPU:64, one launch (start us, length us, event | category | flops | bytes accessed | tf_op | source)
XLA Modules:
  0.0 201.9 jit_solution(5567599616595256157)
XLA Ops:
  0.7 2.1 %first.1 = (f32[16,32,128]{2,1,0:T(8,128)S(1)}, f32[72,512]{1,0:T(8,128)S(1)}, f32[72,512]{1,0:T(8,128)S(1)}) custom-call(f32[8]{0:T(128)} %velocity_in.1, f32[16,32,128]{2,1,0:T(8,128)} %now.1, f32[16,32,128]{2,1,0:T(8,128)} %before.1, s32[16,32,128]{2,1,0:T(8,128)} %codes_in.1), custom_call_target="tpu_custom_call" | custom-call | flops 5000000 | bytes 1500000 | tf_op jit(solution)/shard_map/first/pallas_call | solution.py:263
  2.7 1.9 collective-permute-start
  4.7 3.6 %collective-permute-start.1 = (f32[72,512]{1,0:T(8,128)S(1)}, f32[72,512]{1,0:T(8,128)S(1)}, u32[]{:S(2)}, u32[]{:S(2)}) collective-permute-start(f32[72,512]{1,0:T(8,128)S(1)} %get-tuple-element.44), channel_id=1, source_target_pairs={{1,0},{2,1},{3,2},{4,3},{5,4},{6,5},{7,6},{8,7},{9,8},{10,9},{11,1... | collective-permute-start | bytes 442376 | tf_op jit(solution)/shard_map/ppermute | solution.py:281
  8.3 0.7 copy-done.2
  9.0 0.7 copy-done.3
  9.7 1.2 collective-permute-done.1.from_high
  11.0 0.1 broadcast_in_dim.62.refs_4_
  11.0 0.1 broadcast_in_dim.50.refs_3_
  11.1 0.1 broadcast_in_dim.58.refs_4_
  11.5 1.3 shard_map.77
  12.8 14.2 %collective-permute-start.4 = (f32[336,128]{1,0:T(8,128)S(1)}, f32[336,128]{1,0:T(8,128)S(1)}, u32[]{:S(2)}, u32[]{:S(2)}) collective-permute-start(f32[336,128]{1,0:T(8,128)S(1)} %get-tuple-element.54), channel_id=1, source_target_pairs={{0,48},{48,0},{96,144},{144,96},{192,240},{240,192},{288,336},{336... | collective-permute-start | bytes 516104 | tf_op jit(solution)/shard_map/ppermute | solution.py:236
  27.0 11.5 %collective-permute-done.4 = f32[336,128]{1,0:T(8,128)S(1)} collective-permute-done((f32[336,128]{1,0:T(8,128)S(1)}, f32[336,128]{1,0:T(8,128)S(1)}, u32[]{:S(2)}, u32[]{:S(2)}) %collective-permute-start.4) | collective-permute-done | bytes 172064 | tf_op jit(solution)/shard_map/ppermute | solution.py:236
  38.5 3.5 %collective-permute-start.5 = (f32[168,128]{1,0:T(8,128)S(1)}, f32[168,128]{1,0:T(8,128)S(1)}, u32[]{:S(2)}, u32[]{:S(2)}) collective-permute-start(f32[168,128]{1,0:T(8,128)S(1)} %get-tuple-element.82), channel_id=1, source_target_pairs={{0,96},{48,720},{96,192},{144,48},{192,288},{240,144},{288,384},{3... | collective-permute-start | bytes 258056 | tf_op jit(solution)/shard_map/ppermute | solution.py:241
  42.0 3.4 %collective-permute-start.2 = (f32[104,128]{1,0:T(8,128)S(1)}, f32[104,128]{1,0:T(8,128)S(1)}, u32[]{:S(2)}, u32[]{:S(2)}) collective-permute-start(f32[104,128]{1,0:T(8,128)S(1)} %get-tuple-element.52), channel_id=1, source_target_pairs={{0,12},{12,24},{24,36},{1,13},{13,25},{25,37},{2,14},{14,26},{26,3... | collective-permute-start | bytes 159752 | tf_op jit(solution)/shard_map/ppermute | solution.py:238
  45.4 1.3 collective-permute-start.3
  46.7 0.6 collective-permute-done.2.refs_5_
  47.3 4.1 %collective-permute-done.3.refs_6_ = f32[104,128]{1,0:T(8,128)S(1)} collective-permute-done((f32[104,128]{1,0:T(8,128)S(1)}, f32[104,128]{1,0:T(8,128)S(1)}, u32[]{:S(2)}, u32[]{:S(2)}) %collective-permute-start.3) | collective-permute-done | bytes 53280 | tf_op jit(solution)/shard_map/ppermute | solution.py:239
  51.5 1.1 shard_map.78.refs_0_
  52.6 0.9 shard_map.79
  53.5 12.5 %collective-permute-start.8 = (f32[320,128]{1,0:T(8,128)S(1)}, f32[320,128]{1,0:T(8,128)S(1)}, u32[]{:S(2)}, u32[]{:S(2)}) collective-permute-start(f32[320,128]{1,0:T(8,128)S(1)} %get-tuple-element.59), channel_id=1, source_target_pairs={{0,48},{48,0},{96,144},{144,96},{192,240},{240,192},{288,336},{336... | collective-permute-start | bytes 491528 | tf_op jit(solution)/shard_map/ppermute | solution.py:236
  66.0 6.7 %collective-permute-done.8 = f32[320,128]{1,0:T(8,128)S(1)} collective-permute-done((f32[320,128]{1,0:T(8,128)S(1)}, f32[320,128]{1,0:T(8,128)S(1)}, u32[]{:S(2)}, u32[]{:S(2)}) %collective-permute-start.8) | collective-permute-done | bytes 163872 | tf_op jit(solution)/shard_map/ppermute | solution.py:236
  72.8 1.9 collective-permute-start.9
  74.7 3.4 %collective-permute-start.6 = (f32[96,128]{1,0:T(8,128)S(1)}, f32[96,128]{1,0:T(8,128)S(1)}, u32[]{:S(2)}, u32[]{:S(2)}) collective-permute-start(f32[96,128]{1,0:T(8,128)S(1)} %get-tuple-element.57), channel_id=1, source_target_pairs={{0,12},{12,24},{24,36},{1,13},{13,25},{25,37},{2,14},{14,26},{26,3... | collective-permute-start | bytes 147464 | tf_op jit(solution)/shard_map/ppermute | solution.py:238
  78.1 1.3 collective-permute-start.7
  79.4 0.4 collective-permute-done.6.refs_5_
  79.8 4.3 %collective-permute-done.7.refs_6_ = f32[96,128]{1,0:T(8,128)S(1)} collective-permute-done((f32[96,128]{1,0:T(8,128)S(1)}, f32[96,128]{1,0:T(8,128)S(1)}, u32[]{:S(2)}, u32[]{:S(2)}) %collective-permute-start.7) | collective-permute-done | bytes 49184 | tf_op jit(solution)/shard_map/ppermute | solution.py:239
  84.1 1.1 shard_map.80.refs_0_
  85.2 0.9 shard_map.81
  86.1 11.1 %collective-permute-start.12 = (f32[304,128]{1,0:T(8,128)S(1)}, f32[304,128]{1,0:T(8,128)S(1)}, u32[]{:S(2)}, u32[]{:S(2)}) collective-permute-start(f32[304,128]{1,0:T(8,128)S(1)} %get-tuple-element.64), channel_id=1, source_target_pairs={{0,48},{48,0},{96,144},{144,96},{192,240},{240,192},{288,336},{336... | collective-permute-start | bytes 466952 | tf_op jit(solution)/shard_map/ppermute | solution.py:236
  97.2 6.0 %collective-permute-done.12 = f32[304,128]{1,0:T(8,128)S(1)} collective-permute-done((f32[304,128]{1,0:T(8,128)S(1)}, f32[304,128]{1,0:T(8,128)S(1)}, u32[]{:S(2)}, u32[]{:S(2)}) %collective-permute-start.12) | collective-permute-done | bytes 155680 | tf_op jit(solution)/shard_map/ppermute | solution.py:236
  103.2 2.6 %collective-permute-start.13 = (f32[152,128]{1,0:T(8,128)S(1)}, f32[152,128]{1,0:T(8,128)S(1)}, u32[]{:S(2)}, u32[]{:S(2)}) collective-permute-start(f32[152,128]{1,0:T(8,128)S(1)} %get-tuple-element.86), channel_id=1, source_target_pairs={{0,96},{48,720},{96,192},{144,48},{192,288},{240,144},{288,384},{3... | collective-permute-start | bytes 233480 | tf_op jit(solution)/shard_map/ppermute | solution.py:241
  105.9 3.8 %collective-permute-start.10 = (f32[88,128]{1,0:T(8,128)S(1)}, f32[88,128]{1,0:T(8,128)S(1)}, u32[]{:S(2)}, u32[]{:S(2)}) collective-permute-start(f32[88,128]{1,0:T(8,128)S(1)} %get-tuple-element.62), channel_id=1, source_target_pairs={{0,12},{12,24},{24,36},{1,13},{13,25},{25,37},{2,14},{14,26},{26,3... | collective-permute-start | bytes 135176 | tf_op jit(solution)/shard_map/ppermute | solution.py:238
  109.7 1.3 collective-permute-start.11
  111.0 0.4 collective-permute-done.10.refs_5_
  111.4 4.2 %collective-permute-done.11.refs_6_ = f32[88,128]{1,0:T(8,128)S(1)} collective-permute-done((f32[88,128]{1,0:T(8,128)S(1)}, f32[88,128]{1,0:T(8,128)S(1)}, u32[]{:S(2)}, u32[]{:S(2)}) %collective-permute-start.11) | collective-permute-done | bytes 45088 | tf_op jit(solution)/shard_map/ppermute | solution.py:239
  115.6 1.1 shard_map.82.refs_0_
  116.8 0.9 shard_map.83
  117.6 9.1 %collective-permute-start.16 = (f32[288,128]{1,0:T(8,128)S(1)}, f32[288,128]{1,0:T(8,128)S(1)}, u32[]{:S(2)}, u32[]{:S(2)}) collective-permute-start(f32[288,128]{1,0:T(8,128)S(1)} %get-tuple-element.69), channel_id=1, source_target_pairs={{0,48},{48,0},{96,144},{144,96},{192,240},{240,192},{288,336},{336... | collective-permute-start | bytes 442376 | tf_op jit(solution)/shard_map/ppermute | solution.py:236
  126.7 4.5 %collective-permute-done.16 = f32[288,128]{1,0:T(8,128)S(1)} collective-permute-done((f32[288,128]{1,0:T(8,128)S(1)}, f32[288,128]{1,0:T(8,128)S(1)}, u32[]{:S(2)}, u32[]{:S(2)}) %collective-permute-start.16) | collective-permute-done | bytes 147488 | tf_op jit(solution)/shard_map/ppermute | solution.py:236
  131.3 3.7 %collective-permute-start.17 = (f32[144,128]{1,0:T(8,128)S(1)}, f32[144,128]{1,0:T(8,128)S(1)}, u32[]{:S(2)}, u32[]{:S(2)}) collective-permute-start(f32[144,128]{1,0:T(8,128)S(1)} %get-tuple-element.88), channel_id=1, source_target_pairs={{0,96},{48,720},{96,192},{144,48},{192,288},{240,144},{288,384},{3... | collective-permute-start | bytes 221192 | tf_op jit(solution)/shard_map/ppermute | solution.py:241
  135.0 2.2 %collective-permute-start.14 = (f32[80,128]{1,0:T(8,128)S(1)}, f32[80,128]{1,0:T(8,128)S(1)}, u32[]{:S(2)}, u32[]{:S(2)}) collective-permute-start(f32[80,128]{1,0:T(8,128)S(1)} %get-tuple-element.67), channel_id=1, source_target_pairs={{0,12},{12,24},{24,36},{1,13},{13,25},{25,37},{2,14},{14,26},{26,3... | collective-permute-start | bytes 122888 | tf_op jit(solution)/shard_map/ppermute | solution.py:238
  137.3 1.3 collective-permute-start.15
  138.6 0.4 collective-permute-done.14.refs_5_
  138.9 4.2 %collective-permute-done.15.refs_6_ = f32[80,128]{1,0:T(8,128)S(1)} collective-permute-done((f32[80,128]{1,0:T(8,128)S(1)}, f32[80,128]{1,0:T(8,128)S(1)}, u32[]{:S(2)}, u32[]{:S(2)}) %collective-permute-start.15) | collective-permute-done | bytes 40992 | tf_op jit(solution)/shard_map/ppermute | solution.py:239
  143.2 1.1 shard_map.84.refs_0_
  144.3 0.9 shard_map.85
  145.2 9.4 %collective-permute-start.20 = (f32[272,128]{1,0:T(8,128)S(1)}, f32[272,128]{1,0:T(8,128)S(1)}, u32[]{:S(2)}, u32[]{:S(2)}) collective-permute-start(f32[272,128]{1,0:T(8,128)S(1)} %get-tuple-element.74), channel_id=1, source_target_pairs={{0,48},{48,0},{96,144},{144,96},{192,240},{240,192},{288,336},{336... | collective-permute-start | bytes 417800 | tf_op jit(solution)/shard_map/ppermute | solution.py:236
  154.6 7.7 %collective-permute-done.20 = f32[272,128]{1,0:T(8,128)S(1)} collective-permute-done((f32[272,128]{1,0:T(8,128)S(1)}, f32[272,128]{1,0:T(8,128)S(1)}, u32[]{:S(2)}, u32[]{:S(2)}) %collective-permute-start.20) | collective-permute-done | bytes 139296 | tf_op jit(solution)/shard_map/ppermute | solution.py:236
  162.3 3.0 %collective-permute-start.21 = (f32[136,128]{1,0:T(8,128)S(1)}, f32[136,128]{1,0:T(8,128)S(1)}, u32[]{:S(2)}, u32[]{:S(2)}) collective-permute-start(f32[136,128]{1,0:T(8,128)S(1)} %get-tuple-element.90), channel_id=1, source_target_pairs={{0,96},{48,720},{96,192},{144,48},{192,288},{240,144},{288,384},{3... | collective-permute-start | bytes 208904 | tf_op jit(solution)/shard_map/ppermute | solution.py:241
  165.3 2.2 %collective-permute-start.18 = (f32[72,128]{1,0:T(8,128)S(1)}, f32[72,128]{1,0:T(8,128)S(1)}, u32[]{:S(2)}, u32[]{:S(2)}) collective-permute-start(f32[72,128]{1,0:T(8,128)S(1)} %get-tuple-element.72), channel_id=1, source_target_pairs={{0,12},{12,24},{24,36},{1,13},{13,25},{25,37},{2,14},{14,26},{26,3... | collective-permute-start | bytes 110600 | tf_op jit(solution)/shard_map/ppermute | solution.py:238
  167.5 1.5 collective-permute-start.19
  169.0 0.1 collective-permute-done.18.refs_5_
  169.2 4.2 %collective-permute-done.19.refs_6_ = f32[72,128]{1,0:T(8,128)S(1)} collective-permute-done((f32[72,128]{1,0:T(8,128)S(1)}, f32[72,128]{1,0:T(8,128)S(1)}, u32[]{:S(2)}, u32[]{:S(2)}) %collective-permute-start.19) | collective-permute-done | bytes 36896 | tf_op jit(solution)/shard_map/ppermute | solution.py:239
  173.4 1.1 shard_map.86.refs_0_
  174.5 0.5 shard_map.87
  175.0 7.9 %collective-permute-start.24 = (f32[256,128]{1,0:T(8,128)S(1)}, f32[256,128]{1,0:T(8,128)S(1)}, u32[]{:S(2)}, u32[]{:S(2)}) collective-permute-start(f32[256,128]{1,0:T(8,128)S(1)} %get-tuple-element.80), channel_id=1, source_target_pairs={{0,48},{48,0},{96,144},{144,96},{192,240},{240,192},{288,336},{336... | collective-permute-start | bytes 393224 | tf_op jit(solution)/shard_map/ppermute | solution.py:236
  182.9 5.3 %collective-permute-done.24 = f32[256,128]{1,0:T(8,128)S(1)} collective-permute-done((f32[256,128]{1,0:T(8,128)S(1)}, f32[256,128]{1,0:T(8,128)S(1)}, u32[]{:S(2)}, u32[]{:S(2)}) %collective-permute-start.24) | collective-permute-done | bytes 131104 | tf_op jit(solution)/shard_map/ppermute | solution.py:236
  188.2 3.3 %collective-permute-start.25 = (f32[128,128]{1,0:T(8,128)S(1)}, f32[128,128]{1,0:T(8,128)S(1)}, u32[]{:S(2)}, u32[]{:S(2)}) collective-permute-start(f32[128,128]{1,0:T(8,128)S(1)} %get-tuple-element.92), channel_id=1, source_target_pairs={{0,96},{48,720},{96,192},{144,48},{192,288},{240,144},{288,384},{3... | collective-permute-start | bytes 196616 | tf_op jit(solution)/shard_map/ppermute | solution.py:241
  191.6 2.3 %collective-permute-start.22 = (f32[64,128]{1,0:T(8,128)S(1)}, f32[64,128]{1,0:T(8,128)S(1)}, u32[]{:S(2)}, u32[]{:S(2)}) collective-permute-start(f32[64,128]{1,0:T(8,128)S(1)} %get-tuple-element.77), channel_id=1, source_target_pairs={{0,12},{12,24},{24,36},{1,13},{13,25},{25,37},{2,14},{14,26},{26,3... | collective-permute-start | bytes 98312 | tf_op jit(solution)/shard_map/ppermute | solution.py:238
  193.9 1.3 collective-permute-start.23
  195.2 0.3 collective-permute-done.22.refs_5_
  195.4 4.2 %collective-permute-done.23.refs_6_ = f32[64,128]{1,0:T(8,128)S(1)} collective-permute-done((f32[64,128]{1,0:T(8,128)S(1)}, f32[64,128]{1,0:T(8,128)S(1)}, u32[]{:S(2)}, u32[]{:S(2)}) %collective-permute-start.23) | collective-permute-done | bytes 32800 | tf_op jit(solution)/shard_map/ppermute | solution.py:239
  199.7 1.5 shard_map.88
  201.2 0.8 shard_map.89
  (25 shorter events, 0.4 us)
Async XLA Ops:
  0.6 10.8 %copy-start.1 = (f32[16,32,128]{2,1,0:T(8,128)S(1)}, f32[16,32,128]{2,1,0:T(8,128)}, u32[]{:S(2)}) copy-start(f32[16,32,128]{2,1,0:T(8,128)} %before.1) | copy-start | bytes 786436
  0.6 10.8 %copy-start = (f32[16,32,128]{2,1,0:T(8,128)S(1)}, f32[16,32,128]{2,1,0:T(8,128)}, u32[]{:S(2)}) copy-start(f32[16,32,128]{2,1,0:T(8,128)} %now.1) | copy-start | bytes 786436
  2.7 7.0 %collective-permute-start = (f32[72,512]{1,0:T(8,128)S(1)}, f32[72,512]{1,0:T(8,128)S(1)}, u32[]{:S(2)}, u32[]{:S(2)}) collective-permute-start(f32[72,512]{1,0:T(8,128)S(1)} %get-tuple-element.43), channel_id=1, source_target_pairs={{0,1},{1,2},{2,3},{3,4},{4,5},{5,6},{6,7},{7,8},{8,9},{9,10},{10,1... | collective-permute-start | bytes 442376 | tf_op jit(solution)/shard_map/ppermute | solution.py:280
  4.7 6.3 %collective-permute-start.1 = (f32[72,512]{1,0:T(8,128)S(1)}, f32[72,512]{1,0:T(8,128)S(1)}, u32[]{:S(2)}, u32[]{:S(2)}) collective-permute-start(f32[72,512]{1,0:T(8,128)S(1)} %get-tuple-element.44), channel_id=1, source_target_pairs={{1,0},{2,1},{3,2},{4,3},{5,4},{6,5},{7,6},{8,7},{9,8},{10,9},{11,1... | collective-permute-start | bytes 442376 | tf_op jit(solution)/shard_map/ppermute | solution.py:281
  8.3 0.7 copy-start.2
  9.0 0.7 copy-start.3
  12.8 25.7 %collective-permute-start.4 = (f32[336,128]{1,0:T(8,128)S(1)}, f32[336,128]{1,0:T(8,128)S(1)}, u32[]{:S(2)}, u32[]{:S(2)}) collective-permute-start(f32[336,128]{1,0:T(8,128)S(1)} %get-tuple-element.54), channel_id=1, source_target_pairs={{0,48},{48,0},{96,144},{144,96},{192,240},{240,192},{288,336},{336... | collective-permute-start | bytes 516104 | tf_op jit(solution)/shard_map/ppermute | solution.py:236
  38.5 14.1 %collective-permute-start.5 = (f32[168,128]{1,0:T(8,128)S(1)}, f32[168,128]{1,0:T(8,128)S(1)}, u32[]{:S(2)}, u32[]{:S(2)}) collective-permute-start(f32[168,128]{1,0:T(8,128)S(1)} %get-tuple-element.82), channel_id=1, source_target_pairs={{0,96},{48,720},{96,192},{144,48},{192,288},{240,144},{288,384},{3... | collective-permute-start | bytes 258056 | tf_op jit(solution)/shard_map/ppermute | solution.py:241
  42.0 5.3 %collective-permute-start.2 = (f32[104,128]{1,0:T(8,128)S(1)}, f32[104,128]{1,0:T(8,128)S(1)}, u32[]{:S(2)}, u32[]{:S(2)}) collective-permute-start(f32[104,128]{1,0:T(8,128)S(1)} %get-tuple-element.52), channel_id=1, source_target_pairs={{0,12},{12,24},{24,36},{1,13},{13,25},{25,37},{2,14},{14,26},{26,3... | collective-permute-start | bytes 159752 | tf_op jit(solution)/shard_map/ppermute | solution.py:238
  45.4 6.0 %collective-permute-start.3 = (f32[104,128]{1,0:T(8,128)S(1)}, f32[104,128]{1,0:T(8,128)S(1)}, u32[]{:S(2)}, u32[]{:S(2)}) collective-permute-start(f32[104,128]{1,0:T(8,128)S(1)} %get-tuple-element.53), channel_id=1, source_target_pairs={{12,0},{24,12},{36,24},{13,1},{25,13},{37,25},{14,2},{26,14},{38,2... | collective-permute-start | bytes 159752 | tf_op jit(solution)/shard_map/ppermute | solution.py:239
  53.5 19.2 %collective-permute-start.8 = (f32[320,128]{1,0:T(8,128)S(1)}, f32[320,128]{1,0:T(8,128)S(1)}, u32[]{:S(2)}, u32[]{:S(2)}) collective-permute-start(f32[320,128]{1,0:T(8,128)S(1)} %get-tuple-element.59), channel_id=1, source_target_pairs={{0,48},{48,0},{96,144},{144,96},{192,240},{240,192},{288,336},{336... | collective-permute-start | bytes 491528 | tf_op jit(solution)/shard_map/ppermute | solution.py:236
  72.8 12.5 %collective-permute-start.9 = (f32[160,128]{1,0:T(8,128)S(1)}, f32[160,128]{1,0:T(8,128)S(1)}, u32[]{:S(2)}, u32[]{:S(2)}) collective-permute-start(f32[160,128]{1,0:T(8,128)S(1)} %get-tuple-element.84), channel_id=1, source_target_pairs={{0,96},{48,720},{96,192},{144,48},{192,288},{240,144},{288,384},{3... | collective-permute-start | bytes 245768 | tf_op jit(solution)/shard_map/ppermute | solution.py:241
  74.7 5.1 %collective-permute-start.6 = (f32[96,128]{1,0:T(8,128)S(1)}, f32[96,128]{1,0:T(8,128)S(1)}, u32[]{:S(2)}, u32[]{:S(2)}) collective-permute-start(f32[96,128]{1,0:T(8,128)S(1)} %get-tuple-element.57), channel_id=1, source_target_pairs={{0,12},{12,24},{24,36},{1,13},{13,25},{25,37},{2,14},{14,26},{26,3... | collective-permute-start | bytes 147464 | tf_op jit(solution)/shard_map/ppermute | solution.py:238
  78.1 6.0 %collective-permute-start.7 = (f32[96,128]{1,0:T(8,128)S(1)}, f32[96,128]{1,0:T(8,128)S(1)}, u32[]{:S(2)}, u32[]{:S(2)}) collective-permute-start(f32[96,128]{1,0:T(8,128)S(1)} %get-tuple-element.58), channel_id=1, source_target_pairs={{12,0},{24,12},{36,24},{13,1},{25,13},{37,25},{14,2},{26,14},{38,2... | collective-permute-start | bytes 147464 | tf_op jit(solution)/shard_map/ppermute | solution.py:239
  86.1 17.1 %collective-permute-start.12 = (f32[304,128]{1,0:T(8,128)S(1)}, f32[304,128]{1,0:T(8,128)S(1)}, u32[]{:S(2)}, u32[]{:S(2)}) collective-permute-start(f32[304,128]{1,0:T(8,128)S(1)} %get-tuple-element.64), channel_id=1, source_target_pairs={{0,48},{48,0},{96,144},{144,96},{192,240},{240,192},{288,336},{336... | collective-permute-start | bytes 466952 | tf_op jit(solution)/shard_map/ppermute | solution.py:236
  103.2 13.5 %collective-permute-start.13 = (f32[152,128]{1,0:T(8,128)S(1)}, f32[152,128]{1,0:T(8,128)S(1)}, u32[]{:S(2)}, u32[]{:S(2)}) collective-permute-start(f32[152,128]{1,0:T(8,128)S(1)} %get-tuple-element.86), channel_id=1, source_target_pairs={{0,96},{48,720},{96,192},{144,48},{192,288},{240,144},{288,384},{3... | collective-permute-start | bytes 233480 | tf_op jit(solution)/shard_map/ppermute | solution.py:241
  105.9 5.5 %collective-permute-start.10 = (f32[88,128]{1,0:T(8,128)S(1)}, f32[88,128]{1,0:T(8,128)S(1)}, u32[]{:S(2)}, u32[]{:S(2)}) collective-permute-start(f32[88,128]{1,0:T(8,128)S(1)} %get-tuple-element.62), channel_id=1, source_target_pairs={{0,12},{12,24},{24,36},{1,13},{13,25},{25,37},{2,14},{14,26},{26,3... | collective-permute-start | bytes 135176 | tf_op jit(solution)/shard_map/ppermute | solution.py:238
  109.7 5.9 %collective-permute-start.11 = (f32[88,128]{1,0:T(8,128)S(1)}, f32[88,128]{1,0:T(8,128)S(1)}, u32[]{:S(2)}, u32[]{:S(2)}) collective-permute-start(f32[88,128]{1,0:T(8,128)S(1)} %get-tuple-element.63), channel_id=1, source_target_pairs={{12,0},{24,12},{36,24},{13,1},{25,13},{37,25},{14,2},{26,14},{38,2... | collective-permute-start | bytes 135176 | tf_op jit(solution)/shard_map/ppermute | solution.py:239
  117.6 13.6 %collective-permute-start.16 = (f32[288,128]{1,0:T(8,128)S(1)}, f32[288,128]{1,0:T(8,128)S(1)}, u32[]{:S(2)}, u32[]{:S(2)}) collective-permute-start(f32[288,128]{1,0:T(8,128)S(1)} %get-tuple-element.69), channel_id=1, source_target_pairs={{0,48},{48,0},{96,144},{144,96},{192,240},{240,192},{288,336},{336... | collective-permute-start | bytes 442376 | tf_op jit(solution)/shard_map/ppermute | solution.py:236
  131.3 13.0 %collective-permute-start.17 = (f32[144,128]{1,0:T(8,128)S(1)}, f32[144,128]{1,0:T(8,128)S(1)}, u32[]{:S(2)}, u32[]{:S(2)}) collective-permute-start(f32[144,128]{1,0:T(8,128)S(1)} %get-tuple-element.88), channel_id=1, source_target_pairs={{0,96},{48,720},{96,192},{144,48},{192,288},{240,144},{288,384},{3... | collective-permute-start | bytes 221192 | tf_op jit(solution)/shard_map/ppermute | solution.py:241
  135.0 3.9 %collective-permute-start.14 = (f32[80,128]{1,0:T(8,128)S(1)}, f32[80,128]{1,0:T(8,128)S(1)}, u32[]{:S(2)}, u32[]{:S(2)}) collective-permute-start(f32[80,128]{1,0:T(8,128)S(1)} %get-tuple-element.67), channel_id=1, source_target_pairs={{0,12},{12,24},{24,36},{1,13},{13,25},{25,37},{2,14},{14,26},{26,3... | collective-permute-start | bytes 122888 | tf_op jit(solution)/shard_map/ppermute | solution.py:238
  137.3 5.9 %collective-permute-start.15 = (f32[80,128]{1,0:T(8,128)S(1)}, f32[80,128]{1,0:T(8,128)S(1)}, u32[]{:S(2)}, u32[]{:S(2)}) collective-permute-start(f32[80,128]{1,0:T(8,128)S(1)} %get-tuple-element.68), channel_id=1, source_target_pairs={{12,0},{24,12},{36,24},{13,1},{25,13},{37,25},{14,2},{26,14},{38,2... | collective-permute-start | bytes 122888 | tf_op jit(solution)/shard_map/ppermute | solution.py:239
  145.2 17.1 %collective-permute-start.20 = (f32[272,128]{1,0:T(8,128)S(1)}, f32[272,128]{1,0:T(8,128)S(1)}, u32[]{:S(2)}, u32[]{:S(2)}) collective-permute-start(f32[272,128]{1,0:T(8,128)S(1)} %get-tuple-element.74), channel_id=1, source_target_pairs={{0,48},{48,0},{96,144},{144,96},{192,240},{240,192},{288,336},{336... | collective-permute-start | bytes 417800 | tf_op jit(solution)/shard_map/ppermute | solution.py:236
  162.3 12.2 %collective-permute-start.21 = (f32[136,128]{1,0:T(8,128)S(1)}, f32[136,128]{1,0:T(8,128)S(1)}, u32[]{:S(2)}, u32[]{:S(2)}) collective-permute-start(f32[136,128]{1,0:T(8,128)S(1)} %get-tuple-element.90), channel_id=1, source_target_pairs={{0,96},{48,720},{96,192},{144,48},{192,288},{240,144},{288,384},{3... | collective-permute-start | bytes 208904 | tf_op jit(solution)/shard_map/ppermute | solution.py:241
  165.3 3.8 %collective-permute-start.18 = (f32[72,128]{1,0:T(8,128)S(1)}, f32[72,128]{1,0:T(8,128)S(1)}, u32[]{:S(2)}, u32[]{:S(2)}) collective-permute-start(f32[72,128]{1,0:T(8,128)S(1)} %get-tuple-element.72), channel_id=1, source_target_pairs={{0,12},{12,24},{24,36},{1,13},{13,25},{25,37},{2,14},{14,26},{26,3... | collective-permute-start | bytes 110600 | tf_op jit(solution)/shard_map/ppermute | solution.py:238
  167.5 5.9 %collective-permute-start.19 = (f32[72,128]{1,0:T(8,128)S(1)}, f32[72,128]{1,0:T(8,128)S(1)}, u32[]{:S(2)}, u32[]{:S(2)}) collective-permute-start(f32[72,128]{1,0:T(8,128)S(1)} %get-tuple-element.73), channel_id=1, source_target_pairs={{12,0},{24,12},{36,24},{13,1},{25,13},{37,25},{14,2},{26,14},{38,2... | collective-permute-start | bytes 110600 | tf_op jit(solution)/shard_map/ppermute | solution.py:239
  175.0 13.2 %collective-permute-start.24 = (f32[256,128]{1,0:T(8,128)S(1)}, f32[256,128]{1,0:T(8,128)S(1)}, u32[]{:S(2)}, u32[]{:S(2)}) collective-permute-start(f32[256,128]{1,0:T(8,128)S(1)} %get-tuple-element.80), channel_id=1, source_target_pairs={{0,48},{48,0},{96,144},{144,96},{192,240},{240,192},{288,336},{336... | collective-permute-start | bytes 393224 | tf_op jit(solution)/shard_map/ppermute | solution.py:236
  188.2 13.0 %collective-permute-start.25 = (f32[128,128]{1,0:T(8,128)S(1)}, f32[128,128]{1,0:T(8,128)S(1)}, u32[]{:S(2)}, u32[]{:S(2)}) collective-permute-start(f32[128,128]{1,0:T(8,128)S(1)} %get-tuple-element.92), channel_id=1, source_target_pairs={{0,96},{48,720},{96,192},{144,48},{192,288},{240,144},{288,384},{3... | collective-permute-start | bytes 196616 | tf_op jit(solution)/shard_map/ppermute | solution.py:241
  191.6 3.9 %collective-permute-start.22 = (f32[64,128]{1,0:T(8,128)S(1)}, f32[64,128]{1,0:T(8,128)S(1)}, u32[]{:S(2)}, u32[]{:S(2)}) collective-permute-start(f32[64,128]{1,0:T(8,128)S(1)} %get-tuple-element.77), channel_id=1, source_target_pairs={{0,12},{12,24},{24,36},{1,13},{13,25},{25,37},{2,14},{14,26},{26,3... | collective-permute-start | bytes 98312 | tf_op jit(solution)/shard_map/ppermute | solution.py:238
  193.9 5.8 %collective-permute-start.23 = (f32[64,128]{1,0:T(8,128)S(1)}, f32[64,128]{1,0:T(8,128)S(1)}, u32[]{:S(2)}, u32[]{:S(2)}) collective-permute-start(f32[64,128]{1,0:T(8,128)S(1)} %get-tuple-element.78), channel_id=1, source_target_pairs={{12,0},{24,12},{36,24},{13,1},{25,13},{37,25},{14,2},{26,14},{38,2... | collective-permute-start | bytes 98312 | tf_op jit(solution)/shard_map/ppermute | solution.py:239
where the time goes:
time: 203 us; the launch traced here: 202 us
  starting transfers between devices  113 us (56%)
  waiting for transfers between devices  70.5 us (35%)
  Pallas kernels  15.3 us (8%)
    ppermute x6, starting transfers between devices, exchange(): swapped = lax.ppermute(pair, 'gx', [(i, i ^ 1) for i in range(count)])  64.2 us
    ppermute x6, waiting for transfers between devices, exchange(): swapped = lax.ppermute(pair, 'gx', [(i, i ^ 1) for i in range(count)])  41.7 us
    ppermute x6, waiting for transfers between devices, exchange(): from_y_high = lax.ppermute(y_low, 'gy', back(up))  25.3 us
    ppermute x6, starting transfers between devices, exchange(): outer = lax.ppermute(swapped[half:], 'gx', onward)  18.1 us
    ppermute x6, starting transfers between devices, exchange(): from_y_low = lax.ppermute(y_high, 'gy', up)  17.4 us
    pallas_call x13, Pallas kernels, call(): pl.pallas_call(kernel, out_shape=out, in_specs=inputs, out_specs=(VMEM,)...  13.2 us
    ppermute x6, starting transfers between devices, exchange(): from_y_high = lax.ppermute(y_low, 'gy', back(up))  7.93 us
  transfers between devices with their start and end apart: 26, of which 19 were waited for; matrix products, arithmetic and copies ran while one was open for 0% of the time, Pallas kernels for 4%

commit v1 on v0

--- a/solution.py
+++ b/solution.py
@@ -39,7 +39,7 @@
     return matmul(block, chosen(columns, nz), ((0,), (0,)))
 
 
-def pack_faces(field, columns, pair, y_low, y_high, rows):
+def pack_pair(field, columns, pair):
     _, nx, ny, nz = field.shape
     odd = lax.axis_index("gx") % 2
     inner = (1 - odd) * (nx - HALO)
@@ -51,6 +51,10 @@
             pair[place + face : place + face + 2 * columns, :] = packed(
                 field[1, pl.ds(first, HALO)].reshape(face, nz), columns
             )
+
+
+def pack_y(columns, field, y_low, y_high, rows):
+    _, nx, ny, _ = field.shape
     for y_face, y in ((y_low, 0), (y_high, ny - HALO)):
         for x in range(nx):
             y_face[HALO * x : HALO * (x + 1), :] = field[0, x, y : y + HALO, :]
@@ -88,14 +92,22 @@
         z_high[place * DEEP : (place + 1) * DEEP, :] = both[DEEP : 2 * DEEP]
 
 
-def widen_kernel(now, before, rate, from_low, from_high, wide_now, wide_before, wide_rate, pair, y_low, y_high, rows):
-    nx, ny, nz = now.shape
-    for place, (field, wide) in enumerate(((now, wide_now), (before, wide_before), (rate, wide_rate))):
-        wide[0] = field[...]
-        part = slice(place * DEEP, (place + 1) * DEEP)
-        block = jnp.concatenate([from_high[part, :], from_low[part, :]], axis=0)
-        wide[1] = unpacked(block, DEEP, nz).reshape(nx, ny, nz)
-    pack_faces(wide_now, extra(0), pair, y_low, y_high, rows)
+def widen(place, field, from_low, from_high, wide):
+    nx, ny, nz = field.shape
+    wide[0] = field[...]
+    part = slice(place * DEEP, (place + 1) * DEEP)
+    block = jnp.concatenate([from_high[part, :], from_low[part, :]], axis=0)
+    wide[1] = unpacked(block, DEEP, nz).reshape(nx, ny, nz)
+
+
+def widen_now(now, from_low, from_high, wide_now, pair):
+    widen(0, now, from_low, from_high, wide_now)
+    pack_pair(wide_now, extra(0), pair)
+
+
+def widen_rest(before, rate, from_low, from_high, wide_before, wide_rate):
+    widen(1, before, from_low, from_high, wide_before)
+    widen(2, rate, from_low, from_high, wide_rate)
 
 
 def part_one(step, now, before, rate, cells, amounts, y_low, y_high, *rest):
@@ -165,10 +177,7 @@
     columns = extra(step)
     tiles = 2 if columns else 1
     _, nx, ny, nz = rate.shape
-    if tiles == 2:
-        pair, y_low, y_high, halo, rows = rest
-    else:
-        (halo,) = rest
+    halo = rest[-1]
     odd = lax.axis_index("gx") % 2
     face = HALO * ny
     for block, first in ((inner, (1 - odd) * HALO), (outer, odd * HALO)):
@@ -193,20 +202,22 @@
                 following[x] = value
 
     if tiles == 2:
-        pack_faces(following, extra(step + 1), pair, y_low, y_high, rows)
+        pack_pair(following, extra(step + 1), rest[0])
 
 
 def arrays(*shapes):
     return tuple(jax.ShapeDtypeStruct(s, jnp.float32) for s in shapes)
 
 
-def face_shapes(shape, columns):
-    nx, ny, nz = shape
-    return (
-        (2 * (HALO * ny + 2 * columns), nz),
-        (HALO * nx + 2 * columns, nz),
-        (HALO * nx + 2 * columns, nz),
-    )
+def pair_shape(shape, columns):
+    _, ny, nz = shape
+    return (2 * (HALO * ny + 2 * columns), nz)
+
+
+def y_faces(field, columns):
+    _, nx, _, nz = field.shape
+    face = (HALO * nx + 2 * columns, nz)
+    return call(lambda *refs: pack_y(columns, *refs), arrays(face, face), [VMEM], (field,), scratch=[(HALO * nx, nz)])
 
 
 def call(kernel, out, inputs, operands, scratch=()):
@@ -229,11 +240,12 @@
     return [(b, a) for a, b in pairs]
 
 
-def exchange(faces, ny, columns):
-    pair, y_low, y_high = faces
+def exchange(field, pair, columns):
+    ny = field.shape[2]
     half = HALO * ny + 2 * columns
     count = lax.axis_size("gx")
     swapped = lax.ppermute(pair, "gx", [(i, i ^ 1) for i in range(count)])
+    y_low, y_high = y_faces(field, columns)
     up = line(lax.axis_size("gy"))
     from_y_low = lax.ppermute(y_high, "gy", up)
     from_y_high = lax.ppermute(y_low, "gy", back(up))
@@ -246,7 +258,6 @@
     shape = pressure_now.shape
     nx, ny, nz = shape
     field = (2,) + shape
-    rows = (HALO * nx, nz)
     grid_y = ny * lax.axis_size("gy")
     grid_z = nz * lax.axis_size("gz")
     x = source_cell // (grid_y * grid_z) - lax.axis_index("gx") * nx
@@ -280,16 +291,13 @@
     from_low = lax.ppermute(z_high, "gz", up)
     from_high = lax.ppermute(z_low, "gz", back(up))
     from_low, from_high, cells, *amounts = lax.optimization_barrier((from_low, from_high, cells, *amounts))
-    current, before, rate, *faces = call(
-        widen_kernel,
-        arrays(field, field, field, *face_shapes(shape, extra(0))),
-        [VMEM] * 5,
-        (pressure_now, pressure_before, rate, from_low, from_high),
-        scratch=[rows],
+    current, pair = call(
+        widen_now, arrays(field, pair_shape(shape, extra(0))), [VMEM] * 3, (pressure_now, from_low, from_high)
     )
+    before, rate = call(widen_rest, arrays(field, field), [VMEM] * 4, (pressure_before, rate, from_low, from_high))
     for step in range(STEPS):
         last = step == STEPS - 1
-        inner, outer, y_low, y_high = exchange(faces, ny, extra(step))
+        inner, outer, y_low, y_high = exchange(current, pair, extra(step))
         out = call(
             lambda *refs, step=step: part_one(step, *refs),
             arrays(shape, shape) if last else arrays(field),
@@ -298,13 +306,14 @@
             scratch=[(2, nx, ny + 16, nz)],
         )
         partial = out[0]
-        following, *faces = call(
+        following, *pairs = call(
             lambda *refs, step=step: part_two(step, *refs),
-            arrays(shape) if last else arrays(field, *face_shapes(shape, extra(step + 1))),
+            arrays(shape) if last else arrays(field, pair_shape(shape, extra(step + 1))),
             [VMEM] * 4,
             (partial, rate, inner, outer),
-            scratch=[(2, 2 * HALO, ny, nz)] if last else [(2, 2 * HALO, ny, nz), rows],
+            scratch=[(2, 2 * HALO, ny, nz)],
         )
+        pair = pairs[0] if pairs else None
         before, current = (out[1], following) if last else (current, following)
     return current, before
 

time: 203 us -> 204 us (level)
    pallas_call x13 -> x20, Pallas kernels: 13.2 us -> 15.3 us  [call(): pl.pallas_call(kernel, out_shape=out, in_specs=inputs, out_specs=(VMEM,)...]
  transfers between devices with their start and end apart: 26 -> 26, of which waited for: 19 -> 18; matrix products, arithmetic and copies ran while one was open for 0% -> 0% of each run, Pallas kernels for 4% -> 5%
where the time goes in v1:
time: 204 us; the launch traced here: 203 us
  starting transfers between devices  113 us (55%)
  waiting for transfers between devices  70 us (34%)
  Pallas kernels  17.3 us (8%)
    ppermute x6, starting transfers between devices, exchange(): swapped = lax.ppermute(pair, 'gx', [(i, i ^ 1) for i in range(count)])  64.3 us
    ppermute x6, waiting for transfers between devices, exchange(): swapped = lax.ppermute(pair, 'gx', [(i, i ^ 1) for i in range(count)])  41.8 us
    ppermute x6, waiting for transfers between devices, exchange(): from_y_high = lax.ppermute(y_low, 'gy', back(up))  25.2 us
    ppermute x6, starting transfers between devices, exchange(): outer = lax.ppermute(swapped[half:], 'gx', onward)  18.3 us
    ppermute x6, starting transfers between devices, exchange(): from_y_low = lax.ppermute(y_high, 'gy', up)  17.1 us
    pallas_call x20, Pallas kernels, call(): pl.pallas_call(kernel, out_shape=out, in_specs=inputs, out_specs=(VMEM,)...  15.3 us
    ppermute x6, starting transfers between devices, exchange(): from_y_high = lax.ppermute(y_low, 'gy', back(up))  7.75 us
  transfers between devices with their start and end apart: 26, of which 18 were waited for; matrix products, arithmetic and copies ran while one was open for 0% of the time, Pallas kernels for 5%

profile of v1, /device:TPU:64, one launch (start us, length us, event | category | flops | bytes accessed | tf_op | source)
XLA Modules:
  0.0 203.4 jit_solution(11669212276185275824)
XLA Ops:
  0.6 2.1 %first.1 = (f32[16,32,128]{2,1,0:T(8,128)S(1)}, f32[72,512]{1,0:T(8,128)S(1)}, f32[72,512]{1,0:T(8,128)S(1)}) custom-call(f32[8]{0:T(128)} %velocity_in.1, f32[16,32,128]{2,1,0:T(8,128)} %now.1, f32[16,32,128]{2,1,0:T(8,128)} %before.1, s32[16,32,128]{2,1,0:T(8,128)} %codes_in.1), custom_call_target="tpu_custom_call" | custom-call | flops 5000000 | bytes 1500000 | tf_op jit(solution)/shard_map/first/pallas_call | solution.py:274
  2.7 1.9 collective-permute-start
  4.7 3.6 %collective-permute-start.1 = (f32[72,512]{1,0:T(8,128)S(1)}, f32[72,512]{1,0:T(8,128)S(1)}, u32[]{:S(2)}, u32[]{:S(2)}) collective-permute-start(f32[72,512]{1,0:T(8,128)S(1)} %get-tuple-element.43), channel_id=1, source_target_pairs={{1,0},{2,1},{3,2},{4,3},{5,4},{6,5},{7,6},{8,7},{9,8},{10,9},{11,1... | collective-permute-start | bytes 442376 | tf_op jit(solution)/shard_map/ppermute | solution.py:292
  8.3 0.7 copy-done.2
  9.0 0.7 copy-done.3
  9.7 1.2 collective-permute-done.1.from_high
  11.4 1.1 shard_map.77
  12.6 14.3 %collective-permute-start.4 = (f32[336,128]{1,0:T(8,128)S(1)}, f32[336,128]{1,0:T(8,128)S(1)}, u32[]{:S(2)}, u32[]{:S(2)}) collective-permute-start(f32[336,128]{1,0:T(8,128)S(1)} %get-tuple-element.54), channel_id=1, source_target_pairs={{0,48},{48,0},{96,144},{144,96},{192,240},{240,192},{288,336},{336... | collective-permute-start | bytes 516104 | tf_op jit(solution)/shard_map/ppermute | solution.py:247
  26.9 11.5 %collective-permute-done.4 = f32[336,128]{1,0:T(8,128)S(1)} collective-permute-done((f32[336,128]{1,0:T(8,128)S(1)}, f32[336,128]{1,0:T(8,128)S(1)}, u32[]{:S(2)}, u32[]{:S(2)}) %collective-permute-start.4) | collective-permute-done | bytes 172064 | tf_op jit(solution)/shard_map/ppermute | solution.py:247
  38.4 3.5 %collective-permute-start.5 = (f32[168,128]{1,0:T(8,128)S(1)}, f32[168,128]{1,0:T(8,128)S(1)}, u32[]{:S(2)}, u32[]{:S(2)}) collective-permute-start(f32[168,128]{1,0:T(8,128)S(1)} %get-tuple-element.82), channel_id=1, source_target_pairs={{0,96},{48,720},{96,192},{144,48},{192,288},{240,144},{288,384},{3... | collective-permute-start | bytes 258056 | tf_op jit(solution)/shard_map/ppermute | solution.py:253
  41.9 0.2 shard_map.79
  42.1 3.4 %collective-permute-start.2 = (f32[104,128]{1,0:T(8,128)S(1)}, f32[104,128]{1,0:T(8,128)S(1)}, u32[]{:S(2)}, u32[]{:S(2)}) collective-permute-start(f32[104,128]{1,0:T(8,128)S(1)} %get-tuple-element.52), channel_id=1, source_target_pairs={{0,12},{12,24},{24,36},{1,13},{13,25},{25,37},{2,14},{14,26},{26,3... | collective-permute-start | bytes 159752 | tf_op jit(solution)/shard_map/ppermute | solution.py:250
  45.5 1.3 collective-permute-start.3
  46.8 0.7 shard_map.78
  47.5 4.0 %collective-permute-done.3.refs_6_ = f32[104,128]{1,0:T(8,128)S(1)} collective-permute-done((f32[104,128]{1,0:T(8,128)S(1)}, f32[104,128]{1,0:T(8,128)S(1)}, u32[]{:S(2)}, u32[]{:S(2)}) %collective-permute-start.3) | collective-permute-done | bytes 53280 | tf_op jit(solution)/shard_map/ppermute | solution.py:251
  51.5 1.3 shard_map.80.refs_0_
  52.9 0.8 shard_map.81
  53.6 12.5 %collective-permute-start.8 = (f32[320,128]{1,0:T(8,128)S(1)}, f32[320,128]{1,0:T(8,128)S(1)}, u32[]{:S(2)}, u32[]{:S(2)}) collective-permute-start(f32[320,128]{1,0:T(8,128)S(1)} %get-tuple-element.59), channel_id=1, source_target_pairs={{0,48},{48,0},{96,144},{144,96},{192,240},{240,192},{288,336},{336... | collective-permute-start | bytes 491528 | tf_op jit(solution)/shard_map/ppermute | solution.py:247
  66.2 6.7 %collective-permute-done.8 = f32[320,128]{1,0:T(8,128)S(1)} collective-permute-done((f32[320,128]{1,0:T(8,128)S(1)}, f32[320,128]{1,0:T(8,128)S(1)}, u32[]{:S(2)}, u32[]{:S(2)}) %collective-permute-start.8) | collective-permute-done | bytes 163872 | tf_op jit(solution)/shard_map/ppermute | solution.py:247
  72.9 1.9 collective-permute-start.9
  74.8 0.2 shard_map.82
  75.1 3.4 %collective-permute-start.6 = (f32[96,128]{1,0:T(8,128)S(1)}, f32[96,128]{1,0:T(8,128)S(1)}, u32[]{:S(2)}, u32[]{:S(2)}) collective-permute-start(f32[96,128]{1,0:T(8,128)S(1)} %get-tuple-element.57), channel_id=1, source_target_pairs={{0,12},{12,24},{24,36},{1,13},{13,25},{25,37},{2,14},{14,26},{26,3... | collective-permute-start | bytes 147464 | tf_op jit(solution)/shard_map/ppermute | solution.py:250
  78.5 1.3 collective-permute-start.7
  79.8 0.4 collective-permute-done.6.refs_5_
  80.2 4.3 %collective-permute-done.7.refs_6_ = f32[96,128]{1,0:T(8,128)S(1)} collective-permute-done((f32[96,128]{1,0:T(8,128)S(1)}, f32[96,128]{1,0:T(8,128)S(1)}, u32[]{:S(2)}, u32[]{:S(2)}) %collective-permute-start.7) | collective-permute-done | bytes 49184 | tf_op jit(solution)/shard_map/ppermute | solution.py:251
  84.4 1.4 shard_map.83.refs_0_
  85.8 0.8 shard_map.84
  86.6 11.1 %collective-permute-start.12 = (f32[304,128]{1,0:T(8,128)S(1)}, f32[304,128]{1,0:T(8,128)S(1)}, u32[]{:S(2)}, u32[]{:S(2)}) collective-permute-start(f32[304,128]{1,0:T(8,128)S(1)} %get-tuple-element.64), channel_id=1, source_target_pairs={{0,48},{48,0},{96,144},{144,96},{192,240},{240,192},{288,336},{336... | collective-permute-start | bytes 466952 | tf_op jit(solution)/shard_map/ppermute | solution.py:247
  97.6 6.0 %collective-permute-done.12 = f32[304,128]{1,0:T(8,128)S(1)} collective-permute-done((f32[304,128]{1,0:T(8,128)S(1)}, f32[304,128]{1,0:T(8,128)S(1)}, u32[]{:S(2)}, u32[]{:S(2)}) %collective-permute-start.12) | collective-permute-done | bytes 155680 | tf_op jit(solution)/shard_map/ppermute | solution.py:247
  103.7 2.6 %collective-permute-start.13 = (f32[152,128]{1,0:T(8,128)S(1)}, f32[152,128]{1,0:T(8,128)S(1)}, u32[]{:S(2)}, u32[]{:S(2)}) collective-permute-start(f32[152,128]{1,0:T(8,128)S(1)} %get-tuple-element.86), channel_id=1, source_target_pairs={{0,96},{48,720},{96,192},{144,48},{192,288},{240,144},{288,384},{3... | collective-permute-start | bytes 233480 | tf_op jit(solution)/shard_map/ppermute | solution.py:253
  106.3 0.2 shard_map.85
  106.5 3.8 %collective-permute-start.10 = (f32[88,128]{1,0:T(8,128)S(1)}, f32[88,128]{1,0:T(8,128)S(1)}, u32[]{:S(2)}, u32[]{:S(2)}) collective-permute-start(f32[88,128]{1,0:T(8,128)S(1)} %get-tuple-element.62), channel_id=1, source_target_pairs={{0,12},{12,24},{24,36},{1,13},{13,25},{25,37},{2,14},{14,26},{26,3... | collective-permute-start | bytes 135176 | tf_op jit(solution)/shard_map/ppermute | solution.py:250
  110.4 1.3 collective-permute-start.11
  111.7 0.4 collective-permute-done.10.refs_5_
  112.1 4.2 %collective-permute-done.11.refs_6_ = f32[88,128]{1,0:T(8,128)S(1)} collective-permute-done((f32[88,128]{1,0:T(8,128)S(1)}, f32[88,128]{1,0:T(8,128)S(1)}, u32[]{:S(2)}, u32[]{:S(2)}) %collective-permute-start.11) | collective-permute-done | bytes 45088 | tf_op jit(solution)/shard_map/ppermute | solution.py:251
  116.3 1.4 shard_map.86.refs_0_
  117.7 0.7 shard_map.87
  118.4 9.1 %collective-permute-start.16 = (f32[288,128]{1,0:T(8,128)S(1)}, f32[288,128]{1,0:T(8,128)S(1)}, u32[]{:S(2)}, u32[]{:S(2)}) collective-permute-start(f32[288,128]{1,0:T(8,128)S(1)} %get-tuple-element.69), channel_id=1, source_target_pairs={{0,48},{48,0},{96,144},{144,96},{192,240},{240,192},{288,336},{336... | collective-permute-start | bytes 442376 | tf_op jit(solution)/shard_map/ppermute | solution.py:247
  127.5 4.6 %collective-permute-done.16 = f32[288,128]{1,0:T(8,128)S(1)} collective-permute-done((f32[288,128]{1,0:T(8,128)S(1)}, f32[288,128]{1,0:T(8,128)S(1)}, u32[]{:S(2)}, u32[]{:S(2)}) %collective-permute-start.16) | collective-permute-done | bytes 147488 | tf_op jit(solution)/shard_map/ppermute | solution.py:247
  132.1 3.7 %collective-permute-start.17 = (f32[144,128]{1,0:T(8,128)S(1)}, f32[144,128]{1,0:T(8,128)S(1)}, u32[]{:S(2)}, u32[]{:S(2)}) collective-permute-start(f32[144,128]{1,0:T(8,128)S(1)} %get-tuple-element.88), channel_id=1, source_target_pairs={{0,96},{48,720},{96,192},{144,48},{192,288},{240,144},{288,384},{3... | collective-permute-start | bytes 221192 | tf_op jit(solution)/shard_map/ppermute | solution.py:253
  136.0 2.2 %collective-permute-start.14 = (f32[80,128]{1,0:T(8,128)S(1)}, f32[80,128]{1,0:T(8,128)S(1)}, u32[]{:S(2)}, u32[]{:S(2)}) collective-permute-start(f32[80,128]{1,0:T(8,128)S(1)} %get-tuple-element.67), channel_id=1, source_target_pairs={{0,12},{12,24},{24,36},{1,13},{13,25},{25,37},{2,14},{14,26},{26,3... | collective-permute-start | bytes 122888 | tf_op jit(solution)/shard_map/ppermute | solution.py:250
  138.3 1.3 collective-permute-start.15
  139.6 0.4 collective-permute-done.14.refs_5_
  139.9 4.2 %collective-permute-done.15.refs_6_ = f32[80,128]{1,0:T(8,128)S(1)} collective-permute-done((f32[80,128]{1,0:T(8,128)S(1)}, f32[80,128]{1,0:T(8,128)S(1)}, u32[]{:S(2)}, u32[]{:S(2)}) %collective-permute-start.15) | collective-permute-done | bytes 40992 | tf_op jit(solution)/shard_map/ppermute | solution.py:251
  144.2 1.2 shard_map.89.refs_0_
  145.4 0.7 shard_map.90
  146.1 9.4 %collective-permute-start.20 = (f32[272,128]{1,0:T(8,128)S(1)}, f32[272,128]{1,0:T(8,128)S(1)}, u32[]{:S(2)}, u32[]{:S(2)}) collective-permute-start(f32[272,128]{1,0:T(8,128)S(1)} %get-tuple-element.74), channel_id=1, source_target_pairs={{0,48},{48,0},{96,144},{144,96},{192,240},{240,192},{288,336},{336... | collective-permute-start | bytes 417800 | tf_op jit(solution)/shard_map/ppermute | solution.py:247
  155.5 7.7 %collective-permute-done.20 = f32[272,128]{1,0:T(8,128)S(1)} collective-permute-done((f32[272,128]{1,0:T(8,128)S(1)}, f32[272,128]{1,0:T(8,128)S(1)}, u32[]{:S(2)}, u32[]{:S(2)}) %collective-permute-start.20) | collective-permute-done | bytes 139296 | tf_op jit(solution)/shard_map/ppermute | solution.py:247
  163.3 3.1 %collective-permute-start.21 = (f32[136,128]{1,0:T(8,128)S(1)}, f32[136,128]{1,0:T(8,128)S(1)}, u32[]{:S(2)}, u32[]{:S(2)}) collective-permute-start(f32[136,128]{1,0:T(8,128)S(1)} %get-tuple-element.90), channel_id=1, source_target_pairs={{0,96},{48,720},{96,192},{144,48},{192,288},{240,144},{288,384},{3... | collective-permute-start | bytes 208904 | tf_op jit(solution)/shard_map/ppermute | solution.py:253
  166.6 2.2 %collective-permute-start.18 = (f32[72,128]{1,0:T(8,128)S(1)}, f32[72,128]{1,0:T(8,128)S(1)}, u32[]{:S(2)}, u32[]{:S(2)}) collective-permute-start(f32[72,128]{1,0:T(8,128)S(1)} %get-tuple-element.72), channel_id=1, source_target_pairs={{0,12},{12,24},{24,36},{1,13},{13,25},{25,37},{2,14},{14,26},{26,3... | collective-permute-start | bytes 110600 | tf_op jit(solution)/shard_map/ppermute | solution.py:250
  168.8 1.3 collective-permute-start.19
  170.1 0.3 collective-permute-done.18.refs_5_
  170.4 4.2 %collective-permute-done.19.refs_6_ = f32[72,128]{1,0:T(8,128)S(1)} collective-permute-done((f32[72,128]{1,0:T(8,128)S(1)}, f32[72,128]{1,0:T(8,128)S(1)}, u32[]{:S(2)}, u32[]{:S(2)}) %collective-permute-start.19) | collective-permute-done | bytes 36896 | tf_op jit(solution)/shard_map/ppermute | solution.py:251
  174.7 1.3 shard_map.92.refs_0_
  176.0 0.4 shard_map.93
  176.4 8.0 %collective-permute-start.24 = (f32[256,128]{1,0:T(8,128)S(1)}, f32[256,128]{1,0:T(8,128)S(1)}, u32[]{:S(2)}, u32[]{:S(2)}) collective-permute-start(f32[256,128]{1,0:T(8,128)S(1)} %get-tuple-element.80), channel_id=1, source_target_pairs={{0,48},{48,0},{96,144},{144,96},{192,240},{240,192},{288,336},{336... | collective-permute-start | bytes 393224 | tf_op jit(solution)/shard_map/ppermute | solution.py:247
  184.4 5.2 %collective-permute-done.24 = f32[256,128]{1,0:T(8,128)S(1)} collective-permute-done((f32[256,128]{1,0:T(8,128)S(1)}, f32[256,128]{1,0:T(8,128)S(1)}, u32[]{:S(2)}, u32[]{:S(2)}) %collective-permute-start.24) | collective-permute-done | bytes 131104 | tf_op jit(solution)/shard_map/ppermute | solution.py:247
  189.6 3.6 %collective-permute-start.25 = (f32[128,128]{1,0:T(8,128)S(1)}, f32[128,128]{1,0:T(8,128)S(1)}, u32[]{:S(2)}, u32[]{:S(2)}) collective-permute-start(f32[128,128]{1,0:T(8,128)S(1)} %get-tuple-element.92), channel_id=1, source_target_pairs={{0,96},{48,720},{96,192},{144,48},{192,288},{240,144},{288,384},{3... | collective-permute-start | bytes 196616 | tf_op jit(solution)/shard_map/ppermute | solution.py:253
  193.3 2.0 %collective-permute-start.22 = (f32[64,128]{1,0:T(8,128)S(1)}, f32[64,128]{1,0:T(8,128)S(1)}, u32[]{:S(2)}, u32[]{:S(2)}) collective-permute-start(f32[64,128]{1,0:T(8,128)S(1)} %get-tuple-element.77), channel_id=1, source_target_pairs={{0,12},{12,24},{24,36},{1,13},{13,25},{25,37},{2,14},{14,26},{26,3... | collective-permute-start | bytes 98312 | tf_op jit(solution)/shard_map/ppermute | solution.py:250
  195.3 1.3 collective-permute-start.23
  196.6 0.3 collective-permute-done.22.refs_5_
  196.9 4.2 %collective-permute-done.23.refs_6_ = f32[64,128]{1,0:T(8,128)S(1)} collective-permute-done((f32[64,128]{1,0:T(8,128)S(1)}, f32[64,128]{1,0:T(8,128)S(1)}, u32[]{:S(2)}, u32[]{:S(2)}) %collective-permute-start.23) | collective-permute-done | bytes 32800 | tf_op jit(solution)/shard_map/ppermute | solution.py:251
  201.1 1.5 shard_map.95
  202.6 0.8 shard_map.96
  (32 shorter events, 1.1 us)
Async XLA Ops:
  0.6 10.8 %copy-start.1 = (f32[16,32,128]{2,1,0:T(8,128)S(1)}, f32[16,32,128]{2,1,0:T(8,128)}, u32[]{:S(2)}) copy-start(f32[16,32,128]{2,1,0:T(8,128)} %now.1) | copy-start | bytes 786436
  2.7 7.0 %collective-permute-start = (f32[72,512]{1,0:T(8,128)S(1)}, f32[72,512]{1,0:T(8,128)S(1)}, u32[]{:S(2)}, u32[]{:S(2)}) collective-permute-start(f32[72,512]{1,0:T(8,128)S(1)} %get-tuple-element.42), channel_id=1, source_target_pairs={{0,1},{1,2},{2,3},{3,4},{4,5},{5,6},{6,7},{7,8},{8,9},{9,10},{10,1... | collective-permute-start | bytes 442376 | tf_op jit(solution)/shard_map/ppermute | solution.py:291
  4.7 6.3 %collective-permute-start.1 = (f32[72,512]{1,0:T(8,128)S(1)}, f32[72,512]{1,0:T(8,128)S(1)}, u32[]{:S(2)}, u32[]{:S(2)}) collective-permute-start(f32[72,512]{1,0:T(8,128)S(1)} %get-tuple-element.43), channel_id=1, source_target_pairs={{1,0},{2,1},{3,2},{4,3},{5,4},{6,5},{7,6},{8,7},{9,8},{10,9},{11,1... | collective-permute-start | bytes 442376 | tf_op jit(solution)/shard_map/ppermute | solution.py:292
  8.3 0.7 copy-start.2
  9.0 0.7 copy-start.3
  12.6 25.7 %collective-permute-start.4 = (f32[336,128]{1,0:T(8,128)S(1)}, f32[336,128]{1,0:T(8,128)S(1)}, u32[]{:S(2)}, u32[]{:S(2)}) collective-permute-start(f32[336,128]{1,0:T(8,128)S(1)} %get-tuple-element.54), channel_id=1, source_target_pairs={{0,48},{48,0},{96,144},{144,96},{192,240},{240,192},{288,336},{336... | collective-permute-start | bytes 516104 | tf_op jit(solution)/shard_map/ppermute | solution.py:247
  38.4 14.5 %collective-permute-start.5 = (f32[168,128]{1,0:T(8,128)S(1)}, f32[168,128]{1,0:T(8,128)S(1)}, u32[]{:S(2)}, u32[]{:S(2)}) collective-permute-start(f32[168,128]{1,0:T(8,128)S(1)} %get-tuple-element.82), channel_id=1, source_target_pairs={{0,96},{48,720},{96,192},{144,48},{192,288},{240,144},{288,384},{3... | collective-permute-start | bytes 258056 | tf_op jit(solution)/shard_map/ppermute | solution.py:253
  41.8 5.0 %copy-start = (f32[16,32,128]{2,1,0:T(8,128)S(1)}, f32[16,32,128]{2,1,0:T(8,128)}, u32[]{:S(2)}) copy-start(f32[16,32,128]{2,1,0:T(8,128)} %before.1) | copy-start | bytes 786436
  42.1 5.4 %collective-permute-start.2 = (f32[104,128]{1,0:T(8,128)S(1)}, f32[104,128]{1,0:T(8,128)S(1)}, u32[]{:S(2)}, u32[]{:S(2)}) collective-permute-start(f32[104,128]{1,0:T(8,128)S(1)} %get-tuple-element.52), channel_id=1, source_target_pairs={{0,12},{12,24},{24,36},{1,13},{13,25},{25,37},{2,14},{14,26},{26,3... | collective-permute-start | bytes 159752 | tf_op jit(solution)/shard_map/ppermute | solution.py:250
  45.5 6.0 %collective-permute-start.3 = (f32[104,128]{1,0:T(8,128)S(1)}, f32[104,128]{1,0:T(8,128)S(1)}, u32[]{:S(2)}, u32[]{:S(2)}) collective-permute-start(f32[104,128]{1,0:T(8,128)S(1)} %get-tuple-element.53), channel_id=1, source_target_pairs={{12,0},{24,12},{36,24},{13,1},{25,13},{37,25},{14,2},{26,14},{38,2... | collective-permute-start | bytes 159752 | tf_op jit(solution)/shard_map/ppermute | solution.py:251
  53.6 19.2 %collective-permute-start.8 = (f32[320,128]{1,0:T(8,128)S(1)}, f32[320,128]{1,0:T(8,128)S(1)}, u32[]{:S(2)}, u32[]{:S(2)}) collective-permute-start(f32[320,128]{1,0:T(8,128)S(1)} %get-tuple-element.59), channel_id=1, source_target_pairs={{0,48},{48,0},{96,144},{144,96},{192,240},{240,192},{288,336},{336... | collective-permute-start | bytes 491528 | tf_op jit(solution)/shard_map/ppermute | solution.py:247
  72.9 12.9 %collective-permute-start.9 = (f32[160,128]{1,0:T(8,128)S(1)}, f32[160,128]{1,0:T(8,128)S(1)}, u32[]{:S(2)}, u32[]{:S(2)}) collective-permute-start(f32[160,128]{1,0:T(8,128)S(1)} %get-tuple-element.84), channel_id=1, source_target_pairs={{0,96},{48,720},{96,192},{144,48},{192,288},{240,144},{288,384},{3... | collective-permute-start | bytes 245768 | tf_op jit(solution)/shard_map/ppermute | solution.py:253
  75.1 5.1 %collective-permute-start.6 = (f32[96,128]{1,0:T(8,128)S(1)}, f32[96,128]{1,0:T(8,128)S(1)}, u32[]{:S(2)}, u32[]{:S(2)}) collective-permute-start(f32[96,128]{1,0:T(8,128)S(1)} %get-tuple-element.57), channel_id=1, source_target_pairs={{0,12},{12,24},{24,36},{1,13},{13,25},{25,37},{2,14},{14,26},{26,3... | collective-permute-start | bytes 147464 | tf_op jit(solution)/shard_map/ppermute | solution.py:250
  78.5 6.0 %collective-permute-start.7 = (f32[96,128]{1,0:T(8,128)S(1)}, f32[96,128]{1,0:T(8,128)S(1)}, u32[]{:S(2)}, u32[]{:S(2)}) collective-permute-start(f32[96,128]{1,0:T(8,128)S(1)} %get-tuple-element.58), channel_id=1, source_target_pairs={{12,0},{24,12},{36,24},{13,1},{25,13},{37,25},{14,2},{26,14},{38,2... | collective-permute-start | bytes 147464 | tf_op jit(solution)/shard_map/ppermute | solution.py:251
  86.6 17.1 %collective-permute-start.12 = (f32[304,128]{1,0:T(8,128)S(1)}, f32[304,128]{1,0:T(8,128)S(1)}, u32[]{:S(2)}, u32[]{:S(2)}) collective-permute-start(f32[304,128]{1,0:T(8,128)S(1)} %get-tuple-element.64), channel_id=1, source_target_pairs={{0,48},{48,0},{96,144},{144,96},{192,240},{240,192},{288,336},{336... | collective-permute-start | bytes 466952 | tf_op jit(solution)/shard_map/ppermute | solution.py:247
  103.7 14.0 %collective-permute-start.13 = (f32[152,128]{1,0:T(8,128)S(1)}, f32[152,128]{1,0:T(8,128)S(1)}, u32[]{:S(2)}, u32[]{:S(2)}) collective-permute-start(f32[152,128]{1,0:T(8,128)S(1)} %get-tuple-element.86), channel_id=1, source_target_pairs={{0,96},{48,720},{96,192},{144,48},{192,288},{240,144},{288,384},{3... | collective-permute-start | bytes 233480 | tf_op jit(solution)/shard_map/ppermute | solution.py:253
  106.5 5.5 %collective-permute-start.10 = (f32[88,128]{1,0:T(8,128)S(1)}, f32[88,128]{1,0:T(8,128)S(1)}, u32[]{:S(2)}, u32[]{:S(2)}) collective-permute-start(f32[88,128]{1,0:T(8,128)S(1)} %get-tuple-element.62), channel_id=1, source_target_pairs={{0,12},{12,24},{24,36},{1,13},{13,25},{25,37},{2,14},{14,26},{26,3... | collective-permute-start | bytes 135176 | tf_op jit(solution)/shard_map/ppermute | solution.py:250
  110.4 5.9 %collective-permute-start.11 = (f32[88,128]{1,0:T(8,128)S(1)}, f32[88,128]{1,0:T(8,128)S(1)}, u32[]{:S(2)}, u32[]{:S(2)}) collective-permute-start(f32[88,128]{1,0:T(8,128)S(1)} %get-tuple-element.63), channel_id=1, source_target_pairs={{12,0},{24,12},{36,24},{13,1},{25,13},{37,25},{14,2},{26,14},{38,2... | collective-permute-start | bytes 135176 | tf_op jit(solution)/shard_map/ppermute | solution.py:251
  118.4 13.7 %collective-permute-start.16 = (f32[288,128]{1,0:T(8,128)S(1)}, f32[288,128]{1,0:T(8,128)S(1)}, u32[]{:S(2)}, u32[]{:S(2)}) collective-permute-start(f32[288,128]{1,0:T(8,128)S(1)} %get-tuple-element.69), channel_id=1, source_target_pairs={{0,48},{48,0},{96,144},{144,96},{192,240},{240,192},{288,336},{336... | collective-permute-start | bytes 442376 | tf_op jit(solution)/shard_map/ppermute | solution.py:247
  132.1 13.2 %collective-permute-start.17 = (f32[144,128]{1,0:T(8,128)S(1)}, f32[144,128]{1,0:T(8,128)S(1)}, u32[]{:S(2)}, u32[]{:S(2)}) collective-permute-start(f32[144,128]{1,0:T(8,128)S(1)} %get-tuple-element.88), channel_id=1, source_target_pairs={{0,96},{48,720},{96,192},{144,48},{192,288},{240,144},{288,384},{3... | collective-permute-start | bytes 221192 | tf_op jit(solution)/shard_map/ppermute | solution.py:253
  136.0 3.9 %collective-permute-start.14 = (f32[80,128]{1,0:T(8,128)S(1)}, f32[80,128]{1,0:T(8,128)S(1)}, u32[]{:S(2)}, u32[]{:S(2)}) collective-permute-start(f32[80,128]{1,0:T(8,128)S(1)} %get-tuple-element.67), channel_id=1, source_target_pairs={{0,12},{12,24},{24,36},{1,13},{13,25},{25,37},{2,14},{14,26},{26,3... | collective-permute-start | bytes 122888 | tf_op jit(solution)/shard_map/ppermute | solution.py:250
  138.3 5.9 %collective-permute-start.15 = (f32[80,128]{1,0:T(8,128)S(1)}, f32[80,128]{1,0:T(8,128)S(1)}, u32[]{:S(2)}, u32[]{:S(2)}) collective-permute-start(f32[80,128]{1,0:T(8,128)S(1)} %get-tuple-element.68), channel_id=1, source_target_pairs={{12,0},{24,12},{36,24},{13,1},{25,13},{37,25},{14,2},{26,14},{38,2... | collective-permute-start | bytes 122888 | tf_op jit(solution)/shard_map/ppermute | solution.py:251
  146.1 17.1 %collective-permute-start.20 = (f32[272,128]{1,0:T(8,128)S(1)}, f32[272,128]{1,0:T(8,128)S(1)}, u32[]{:S(2)}, u32[]{:S(2)}) collective-permute-start(f32[272,128]{1,0:T(8,128)S(1)} %get-tuple-element.74), channel_id=1, source_target_pairs={{0,48},{48,0},{96,144},{144,96},{192,240},{240,192},{288,336},{336... | collective-permute-start | bytes 417800 | tf_op jit(solution)/shard_map/ppermute | solution.py:247
  163.3 12.7 %collective-permute-start.21 = (f32[136,128]{1,0:T(8,128)S(1)}, f32[136,128]{1,0:T(8,128)S(1)}, u32[]{:S(2)}, u32[]{:S(2)}) collective-permute-start(f32[136,128]{1,0:T(8,128)S(1)} %get-tuple-element.90), channel_id=1, source_target_pairs={{0,96},{48,720},{96,192},{144,48},{192,288},{240,144},{288,384},{3... | collective-permute-start | bytes 208904 | tf_op jit(solution)/shard_map/ppermute | solution.py:253
  166.6 3.8 %collective-permute-start.18 = (f32[72,128]{1,0:T(8,128)S(1)}, f32[72,128]{1,0:T(8,128)S(1)}, u32[]{:S(2)}, u32[]{:S(2)}) collective-permute-start(f32[72,128]{1,0:T(8,128)S(1)} %get-tuple-element.72), channel_id=1, source_target_pairs={{0,12},{12,24},{24,36},{1,13},{13,25},{25,37},{2,14},{14,26},{26,3... | collective-permute-start | bytes 110600 | tf_op jit(solution)/shard_map/ppermute | solution.py:250
  168.8 5.9 %collective-permute-start.19 = (f32[72,128]{1,0:T(8,128)S(1)}, f32[72,128]{1,0:T(8,128)S(1)}, u32[]{:S(2)}, u32[]{:S(2)}) collective-permute-start(f32[72,128]{1,0:T(8,128)S(1)} %get-tuple-element.73), channel_id=1, source_target_pairs={{12,0},{24,12},{36,24},{13,1},{25,13},{37,25},{14,2},{26,14},{38,2... | collective-permute-start | bytes 110600 | tf_op jit(solution)/shard_map/ppermute | solution.py:251
  176.4 13.2 %collective-permute-start.24 = (f32[256,128]{1,0:T(8,128)S(1)}, f32[256,128]{1,0:T(8,128)S(1)}, u32[]{:S(2)}, u32[]{:S(2)}) collective-permute-start(f32[256,128]{1,0:T(8,128)S(1)} %get-tuple-element.80), channel_id=1, source_target_pairs={{0,48},{48,0},{96,144},{144,96},{192,240},{240,192},{288,336},{336... | collective-permute-start | bytes 393224 | tf_op jit(solution)/shard_map/ppermute | solution.py:247
  189.6 13.0 %collective-permute-start.25 = (f32[128,128]{1,0:T(8,128)S(1)}, f32[128,128]{1,0:T(8,128)S(1)}, u32[]{:S(2)}, u32[]{:S(2)}) collective-permute-start(f32[128,128]{1,0:T(8,128)S(1)} %get-tuple-element.92), channel_id=1, source_target_pairs={{0,96},{48,720},{96,192},{144,48},{192,288},{240,144},{288,384},{3... | collective-permute-start | bytes 196616 | tf_op jit(solution)/shard_map/ppermute | solution.py:253
  193.3 3.6 %collective-permute-start.22 = (f32[64,128]{1,0:T(8,128)S(1)}, f32[64,128]{1,0:T(8,128)S(1)}, u32[]{:S(2)}, u32[]{:S(2)}) collective-permute-start(f32[64,128]{1,0:T(8,128)S(1)} %get-tuple-element.77), channel_id=1, source_target_pairs={{0,12},{12,24},{24,36},{1,13},{13,25},{25,37},{2,14},{14,26},{26,3... | collective-permute-start | bytes 98312 | tf_op jit(solution)/shard_map/ppermute | solution.py:250
  195.3 5.8 %collective-permute-start.23 = (f32[64,128]{1,0:T(8,128)S(1)}, f32[64,128]{1,0:T(8,128)S(1)}, u32[]{:S(2)}, u32[]{:S(2)}) collective-permute-start(f32[64,128]{1,0:T(8,128)S(1)} %get-tuple-element.78), channel_id=1, source_target_pairs={{12,0},{24,12},{36,24},{13,1},{25,13},{37,25},{14,2},{26,14},{38,2... | collective-permute-start | bytes 98312 | tf_op jit(solution)/shard_map/ppermute | solution.py:251

commit v2 on v1

--- a/solution.py
+++ b/solution.py
@@ -39,18 +39,42 @@
     return matmul(block, chosen(columns, nz), ((0,), (0,)))
 
 
-def pack_pair(field, columns, pair):
+def side(place):
+    odd = lax.axis_index("gx") % 2
+    return 1 - odd if place == "inner" else odd
+
+
+def pack_x(field, columns, place, face_ref, first=0):
     _, nx, ny, nz = field.shape
-    odd = lax.axis_index("gx") % 2
-    inner = (1 - odd) * (nx - HALO)
-    outer = odd * (nx - HALO)
+    start = side(place) * (nx - HALO)
     face = HALO * ny
-    for place, first in ((0, inner), (face + 2 * columns, outer)):
-        pair[place : place + face, :] = field[0, pl.ds(first, HALO)].reshape(face, nz)
-        if columns:
-            pair[place + face : place + face + 2 * columns, :] = packed(
-                field[1, pl.ds(first, HALO)].reshape(face, nz), columns
-            )
+    face_ref[first : first + face, :] = field[0, pl.ds(start, HALO)].reshape(face, nz)
+    if columns:
+        face_ref[first + face : first + face + 2 * columns, :] = packed(
+            field[1, pl.ds(start, HALO)].reshape(face, nz), columns
+        )
+
+
+def add_x(field, rate, columns, place, block, halo):
+    _, nx, ny, nz = rate.shape
+    face = HALO * ny
+    high = side(place)
+    tiles = 2 if columns else 1
+    halo[0] = block[0:face, :].reshape(HALO, ny, nz)
+    if columns:
+        halo[1] = unpacked(block[face : face + 2 * columns, :], columns, nz).reshape(HALO, ny, nz)
+    for t in range(tiles):
+        beyond = [halo[t, high * (m - 1) + (1 - high) * (HALO - m)] for m in range(1, HALO + 1)]
+        for j in range(HALO):
+            x = high * (nx - 1 - j) + (1 - high) * j
+            total = None
+            for m in range(1, HALO + 1 - j):
+                term = jnp.float32(WEIGHTS[j + m - 1]) * beyond[m - 1]
+                total = term if total is None else total + term
+            if len(field.shape) == 4:
+                field[t, x] = field[t, x] + rate[t, x] * total
+            else:
+                field[x] = field[x] + rate[t, x] * total
 
 
 def pack_y(columns, field, y_low, y_high, rows):
@@ -102,7 +126,8 @@
 
 def widen_now(now, from_low, from_high, wide_now, pair):
     widen(0, now, from_low, from_high, wide_now)
-    pack_pair(wide_now, extra(0), pair)
+    pack_x(wide_now, extra(0), "inner", pair)
+    pack_x(wide_now, extra(0), "outer", pair, pair.shape[0] // 2)
 
 
 def widen_rest(before, rate, from_low, from_high, wide_before, wide_rate):
@@ -110,8 +135,8 @@
     widen(2, rate, from_low, from_high, wide_rate)
 
 
-def part_one(step, now, before, rate, cells, amounts, y_low, y_high, *rest):
-    following, wide = rest[0], rest[-1]
+def part_one(step, now, before, rate, cells, amounts, inner, y_low, y_high, *rest):
+    following, wide, halo = rest[0], rest[-2], rest[-1]
     columns = extra(step)
     tiles = 2 if columns else 1
     _, nx, ny, nz = now.shape
@@ -153,6 +178,7 @@
                 following[x] = value
     if tiles == 1:
         rest[1][...] = now[0]
+    add_x(following, rate, columns, "inner", inner, halo)
 
     @pl.when(jnp.max(cells[...]) >= 0)
     def _():
@@ -171,47 +197,35 @@
                     here = following.at[x]
                 row = here[pl.ds(y, 1), :]
                 here[pl.ds(y, 1), :] = row + jnp.where(lanes == number % nz, amounts[s : s + 1, :], jnp.float32(0))
-
-
-def part_two(step, partial, rate, inner, outer, following, *rest):
+    if tiles == 2:
+        pack_x(following, extra(step + 1), "inner", rest[1])
+
+
+def part_two(step, partial, rate, outer, *rest):
     columns = extra(step)
-    tiles = 2 if columns else 1
-    _, nx, ny, nz = rate.shape
     halo = rest[-1]
-    odd = lax.axis_index("gx") % 2
-    face = HALO * ny
-    for block, first in ((inner, (1 - odd) * HALO), (outer, odd * HALO)):
-        halo[0, pl.ds(first, HALO)] = block[0:face, :].reshape(HALO, ny, nz)
-        if columns:
-            halo[1, pl.ds(first, HALO)] = unpacked(block[face : face + 2 * columns, :], columns, nz).reshape(HALO, ny, nz)
-    for t in range(tiles):
-        for x in range(nx):
-            total = None
-            for k, weight in enumerate(WEIGHTS, 1):
-                for at in (x - k, x + k):
-                    if 0 <= at < nx:
-                        continue
-                    term = jnp.float32(weight) * halo[t, at + HALO if at < 0 else at - nx + HALO]
-                    total = term if total is None else total + term
-            value = partial[t, x] if tiles == 2 else partial[x]
-            if total is not None:
-                value = value + rate[t, x] * total
-            if tiles == 2:
-                following[t, x] = value
-            else:
-                following[x] = value
-
-    if tiles == 2:
-        pack_pair(following, extra(step + 1), rest[0])
+    following = rest[1] if columns else rest[0]
+    following[...] = partial[...]
+    add_x(following, rate, columns, "outer", outer, halo)
+    if columns:
+        inner_face, pair = rest[0], rest[2]
+        half = pair.shape[0] // 2
+        pair[0:half, :] = inner_face[...]
+        pack_x(following, extra(step + 1), "outer", pair, half)
 
 
 def arrays(*shapes):
     return tuple(jax.ShapeDtypeStruct(s, jnp.float32) for s in shapes)
 
 
+def face_shape(shape, columns):
+    _, ny, nz = shape
+    return (HALO * ny + 2 * columns, nz)
+
+
 def pair_shape(shape, columns):
-    _, ny, nz = shape
-    return (2 * (HALO * ny + 2 * columns), nz)
+    rows, nz = face_shape(shape, columns)
+    return (2 * rows, nz)
 
 
 def y_faces(field, columns):
@@ -290,7 +304,6 @@
     up = line(lax.axis_size("gz"))
     from_low = lax.ppermute(z_high, "gz", up)
     from_high = lax.ppermute(z_low, "gz", back(up))
-    from_low, from_high, cells, *amounts = lax.optimization_barrier((from_low, from_high, cells, *amounts))
     current, pair = call(
         widen_now, arrays(field, pair_shape(shape, extra(0))), [VMEM] * 3, (pressure_now, from_low, from_high)
     )
@@ -300,18 +313,18 @@
         inner, outer, y_low, y_high = exchange(current, pair, extra(step))
         out = call(
             lambda *refs, step=step: part_one(step, *refs),
-            arrays(shape, shape) if last else arrays(field),
-            [VMEM] * 7,
-            (current, before, rate, cells, amounts[step], y_low, y_high),
-            scratch=[(2, nx, ny + 16, nz)],
+            arrays(shape, shape) if last else arrays(field, face_shape(shape, extra(step + 1))),
+            [VMEM] * 8,
+            (current, before, rate, cells, amounts[step], inner, y_low, y_high),
+            scratch=[(2, nx, ny + 16, nz), (2, HALO, ny, nz)],
         )
         partial = out[0]
         following, *pairs = call(
             lambda *refs, step=step: part_two(step, *refs),
             arrays(shape) if last else arrays(field, pair_shape(shape, extra(step + 1))),
-            [VMEM] * 4,
-            (partial, rate, inner, outer),
-            scratch=[(2, 2 * HALO, ny, nz)],
+            [VMEM] * (3 if last else 4),
+            (partial, rate, outer) if last else (partial, rate, outer, out[1]),
+            scratch=[(2, HALO, ny, nz)],
         )
         pair = pairs[0] if pairs else None
         before, current = (out[1], following) if last else (current, following)

time: 204 us -> 199 us (0.975)
  waiting for transfers between devices: 70 us -> 66.7 us
    ppermute x6, waiting for transfers between devices: 25.2 us -> 21.2 us  [exchange(): from_y_high = lax.ppermute(y_low, 'gy', back(up))]
    ppermute x6, waiting for transfers between devices: 41.8 us -> 38.7 us  [exchange(): swapped = lax.ppermute(pair, 'gx', [(i, i ^ 1) for i in range(count)])]
    ppermute x6, starting transfers between devices: 64.3 us -> 61.6 us  [exchange(): swapped = lax.ppermute(pair, 'gx', [(i, i ^ 1) for i in range(count)])]
    ppermute x6, waiting for transfers between devices: 0.02 us -> 2.31 us  [exchange(): outer = lax.ppermute(swapped[half:], 'gx', onward)]
  transfers between devices with their start and end apart: 26 -> 26, of which waited for: 18 -> 19; matrix products, arithmetic and copies ran while one was open for 0% -> 0% of each run, Pallas kernels for 5% -> 6%
where the time goes in v2:
time: 199 us; the launch traced here: 198 us
  starting transfers between devices  111 us (56%)
  waiting for transfers between devices  66.7 us (34%)
  Pallas kernels  18.7 us (9%)
    ppermute x6, starting transfers between devices, exchange(): swapped = lax.ppermute(pair, 'gx', [(i, i ^ 1) for i in range(count)])  61.6 us
    ppermute x6, waiting for transfers between devices, exchange(): swapped = lax.ppermute(pair, 'gx', [(i, i ^ 1) for i in range(count)])  38.7 us
    ppermute x6, waiting for transfers between devices, exchange(): from_y_high = lax.ppermute(y_low, 'gy', back(up))  21.2 us
    ppermute x6, starting transfers between devices, exchange(): from_y_low = lax.ppermute(y_high, 'gy', up)  18.1 us
    ppermute x6, starting transfers between devices, exchange(): outer = lax.ppermute(swapped[half:], 'gx', onward)  17.7 us
    pallas_call x20, Pallas kernels, call(): pl.pallas_call(kernel, out_shape=out, in_specs=inputs, out_specs=(VMEM,)...  16.6 us
    ppermute x6, starting transfers between devices, exchange(): from_y_high = lax.ppermute(y_low, 'gy', back(up))  7.75 us
  transfers between devices with their start and end apart: 26, of which 19 were waited for; matrix products, arithmetic and copies ran while one was open for 0% of the time, Pallas kernels for 6%

profile of v2, /device:TPU:64, one launch (start us, length us, event | category | flops | bytes accessed | tf_op | source)
XLA Modules:
  0.0 197.7 jit_solution(13752302731440383833)
XLA Ops:
  0.6 2.1 %first.1 = (f32[16,32,128]{2,1,0:T(8,128)S(1)}, f32[72,512]{1,0:T(8,128)S(1)}, f32[72,512]{1,0:T(8,128)S(1)}) custom-call(f32[8]{0:T(128)} %velocity_in.1, f32[16,32,128]{2,1,0:T(8,128)} %now.1, f32[16,32,128]{2,1,0:T(8,128)} %before.1, s32[16,32,128]{2,1,0:T(8,128)} %codes_in.1), custom_call_target="tpu_custom_call" | custom-call | flops 5000000 | bytes 1500000 | tf_op jit(solution)/shard_map/first/pallas_call | solution.py:288
  2.7 1.9 collective-permute-start
  4.7 3.6 %collective-permute-start.1 = (f32[72,512]{1,0:T(8,128)S(1)}, f32[72,512]{1,0:T(8,128)S(1)}, u32[]{:S(2)}, u32[]{:S(2)}) collective-permute-start(f32[72,512]{1,0:T(8,128)S(1)} %get-tuple-element.44), channel_id=1, source_target_pairs={{1,0},{2,1},{3,2},{4,3},{5,4},{6,5},{7,6},{8,7},{9,8},{10,9},{11,1... | collective-permute-start | bytes 442376 | tf_op jit(solution)/shard_map/ppermute | solution.py:306
  8.3 0.9 collective-permute-done.from_low
  9.2 1.8 collective-permute-done.1.from_high
  11.0 1.1 shard_map.77
  12.1 14.3 %collective-permute-start.2 = (f32[336,128]{1,0:T(8,128)S(1)}, f32[336,128]{1,0:T(8,128)S(1)}, u32[]{:S(2)}, u32[]{:S(2)}) collective-permute-start(f32[336,128]{1,0:T(8,128)S(1)} %get-tuple-element.49), channel_id=1, source_target_pairs={{0,48},{48,0},{96,144},{144,96},{192,240},{240,192},{288,336},{336... | collective-permute-start | bytes 516104 | tf_op jit(solution)/shard_map/ppermute | solution.py:261
  26.4 0.2 shard_map.79
  26.6 3.5 %collective-permute-start.3 = (f32[104,128]{1,0:T(8,128)S(1)}, f32[104,128]{1,0:T(8,128)S(1)}, u32[]{:S(2)}, u32[]{:S(2)}) collective-permute-start(f32[104,128]{1,0:T(8,128)S(1)} %get-tuple-element.50), channel_id=1, source_target_pairs={{0,12},{12,24},{24,36},{1,13},{13,25},{25,37},{2,14},{14,26},{26,3... | collective-permute-start | bytes 159752 | tf_op jit(solution)/shard_map/ppermute | solution.py:264
  30.2 1.3 collective-permute-start.4
  31.5 6.8 %collective-permute-done.2 = f32[336,128]{1,0:T(8,128)S(1)} collective-permute-done((f32[336,128]{1,0:T(8,128)S(1)}, f32[336,128]{1,0:T(8,128)S(1)}, u32[]{:S(2)}, u32[]{:S(2)}) %collective-permute-start.2) | collective-permute-done | bytes 172064 | tf_op jit(solution)/shard_map/ppermute | solution.py:261
  38.3 3.5 %collective-permute-start.5 = (f32[168,128]{1,0:T(8,128)S(1)}, f32[168,128]{1,0:T(8,128)S(1)}, u32[]{:S(2)}, u32[]{:S(2)}) collective-permute-start(f32[168,128]{1,0:T(8,128)S(1)} %get-tuple-element.84), channel_id=1, source_target_pairs={{0,96},{48,720},{96,192},{144,48},{192,288},{240,144},{288,384},{3... | collective-permute-start | bytes 258056 | tf_op jit(solution)/shard_map/ppermute | solution.py:267
  41.9 0.7 shard_map.78
  42.7 1.9 shard_map.80
  44.6 2.3 %collective-permute-done.5.refs_2_ = f32[168,128]{1,0:T(8,128)S(1)} collective-permute-done((f32[168,128]{1,0:T(8,128)S(1)}, f32[168,128]{1,0:T(8,128)S(1)}, u32[]{:S(2)}, u32[]{:S(2)}) %collective-permute-start.5) | collective-permute-done | bytes 86048 | tf_op jit(solution)/shard_map/ppermute | solution.py:267
  46.9 0.5 shard_map.81
  47.4 10.3 %collective-permute-start.6 = (f32[320,128]{1,0:T(8,128)S(1)}, f32[320,128]{1,0:T(8,128)S(1)}, u32[]{:S(2)}, u32[]{:S(2)}) collective-permute-start(f32[320,128]{1,0:T(8,128)S(1)} %get-tuple-element.55), channel_id=1, source_target_pairs={{0,48},{48,0},{96,144},{144,96},{192,240},{240,192},{288,336},{336... | collective-permute-start | bytes 491528 | tf_op jit(solution)/shard_map/ppermute | solution.py:261
  57.7 6.4 %collective-permute-done.6 = f32[320,128]{1,0:T(8,128)S(1)} collective-permute-done((f32[320,128]{1,0:T(8,128)S(1)}, f32[320,128]{1,0:T(8,128)S(1)}, u32[]{:S(2)}, u32[]{:S(2)}) %collective-permute-start.6) | collective-permute-done | bytes 163872 | tf_op jit(solution)/shard_map/ppermute | solution.py:261
  64.1 2.1 %collective-permute-start.9 = (f32[160,128]{1,0:T(8,128)S(1)}, f32[160,128]{1,0:T(8,128)S(1)}, u32[]{:S(2)}, u32[]{:S(2)}) collective-permute-start(f32[160,128]{1,0:T(8,128)S(1)} %get-tuple-element.86), channel_id=1, source_target_pairs={{0,96},{48,720},{96,192},{144,48},{192,288},{240,144},{288,384},{3... | collective-permute-start | bytes 245768 | tf_op jit(solution)/shard_map/ppermute | solution.py:267
  66.3 0.2 shard_map.82
  66.5 3.4 %collective-permute-start.7 = (f32[96,128]{1,0:T(8,128)S(1)}, f32[96,128]{1,0:T(8,128)S(1)}, u32[]{:S(2)}, u32[]{:S(2)}) collective-permute-start(f32[96,128]{1,0:T(8,128)S(1)} %get-tuple-element.56), channel_id=1, source_target_pairs={{0,12},{12,24},{24,36},{1,13},{13,25},{25,37},{2,14},{14,26},{26,3... | collective-permute-start | bytes 147464 | tf_op jit(solution)/shard_map/ppermute | solution.py:264
  70.0 1.3 collective-permute-start.8
  71.3 0.4 collective-permute-done.7.refs_6_
  71.7 4.3 %collective-permute-done.8.refs_7_ = f32[96,128]{1,0:T(8,128)S(1)} collective-permute-done((f32[96,128]{1,0:T(8,128)S(1)}, f32[96,128]{1,0:T(8,128)S(1)}, u32[]{:S(2)}, u32[]{:S(2)}) %collective-permute-start.8) | collective-permute-done | bytes 49184 | tf_op jit(solution)/shard_map/ppermute | solution.py:265
  76.0 1.9 shard_map.83
  77.9 0.6 shard_map.84
  78.4 12.4 %collective-permute-start.10 = (f32[304,128]{1,0:T(8,128)S(1)}, f32[304,128]{1,0:T(8,128)S(1)}, u32[]{:S(2)}, u32[]{:S(2)}) collective-permute-start(f32[304,128]{1,0:T(8,128)S(1)} %get-tuple-element.61), channel_id=1, source_target_pairs={{0,48},{48,0},{96,144},{144,96},{192,240},{240,192},{288,336},{336... | collective-permute-start | bytes 466952 | tf_op jit(solution)/shard_map/ppermute | solution.py:261
  90.8 3.9 %collective-permute-done.10 = f32[304,128]{1,0:T(8,128)S(1)} collective-permute-done((f32[304,128]{1,0:T(8,128)S(1)}, f32[304,128]{1,0:T(8,128)S(1)}, u32[]{:S(2)}, u32[]{:S(2)}) %collective-permute-start.10) | collective-permute-done | bytes 155680 | tf_op jit(solution)/shard_map/ppermute | solution.py:261
  94.7 1.9 collective-permute-start.13
  96.6 0.2 shard_map.85
  96.8 3.9 %collective-permute-start.11 = (f32[88,128]{1,0:T(8,128)S(1)}, f32[88,128]{1,0:T(8,128)S(1)}, u32[]{:S(2)}, u32[]{:S(2)}) collective-permute-start(f32[88,128]{1,0:T(8,128)S(1)} %get-tuple-element.62), channel_id=1, source_target_pairs={{0,12},{12,24},{24,36},{1,13},{13,25},{25,37},{2,14},{14,26},{26,3... | collective-permute-start | bytes 135176 | tf_op jit(solution)/shard_map/ppermute | solution.py:264
  100.7 1.3 collective-permute-start.12
  102.0 0.4 collective-permute-done.11.refs_6_
  102.4 4.2 %collective-permute-done.12.refs_7_ = f32[88,128]{1,0:T(8,128)S(1)} collective-permute-done((f32[88,128]{1,0:T(8,128)S(1)}, f32[88,128]{1,0:T(8,128)S(1)}, u32[]{:S(2)}, u32[]{:S(2)}) %collective-permute-start.12) | collective-permute-done | bytes 45088 | tf_op jit(solution)/shard_map/ppermute | solution.py:265
  106.8 1.9 shard_map.86
  108.6 0.5 shard_map.87
  109.2 9.8 %collective-permute-start.14 = (f32[288,128]{1,0:T(8,128)S(1)}, f32[288,128]{1,0:T(8,128)S(1)}, u32[]{:S(2)}, u32[]{:S(2)}) collective-permute-start(f32[288,128]{1,0:T(8,128)S(1)} %get-tuple-element.67), channel_id=1, source_target_pairs={{0,48},{48,0},{96,144},{144,96},{192,240},{240,192},{288,336},{336... | collective-permute-start | bytes 442376 | tf_op jit(solution)/shard_map/ppermute | solution.py:261
  119.0 6.8 %collective-permute-done.14 = f32[288,128]{1,0:T(8,128)S(1)} collective-permute-done((f32[288,128]{1,0:T(8,128)S(1)}, f32[288,128]{1,0:T(8,128)S(1)}, u32[]{:S(2)}, u32[]{:S(2)}) %collective-permute-start.14) | collective-permute-done | bytes 147488 | tf_op jit(solution)/shard_map/ppermute | solution.py:261
  125.8 2.6 %collective-permute-start.17 = (f32[144,128]{1,0:T(8,128)S(1)}, f32[144,128]{1,0:T(8,128)S(1)}, u32[]{:S(2)}, u32[]{:S(2)}) collective-permute-start(f32[144,128]{1,0:T(8,128)S(1)} %get-tuple-element.90), channel_id=1, source_target_pairs={{0,96},{48,720},{96,192},{144,48},{192,288},{240,144},{288,384},{3... | collective-permute-start | bytes 221192 | tf_op jit(solution)/shard_map/ppermute | solution.py:267
  128.4 0.2 shard_map.88
  128.6 3.4 %collective-permute-start.15 = (f32[80,128]{1,0:T(8,128)S(1)}, f32[80,128]{1,0:T(8,128)S(1)}, u32[]{:S(2)}, u32[]{:S(2)}) collective-permute-start(f32[80,128]{1,0:T(8,128)S(1)} %get-tuple-element.68), channel_id=1, source_target_pairs={{0,12},{12,24},{24,36},{1,13},{13,25},{25,37},{2,14},{14,26},{26,3... | collective-permute-start | bytes 122888 | tf_op jit(solution)/shard_map/ppermute | solution.py:264
  132.0 1.3 collective-permute-start.16
  133.3 0.4 collective-permute-done.15.refs_6_
  133.7 4.2 %collective-permute-done.16.refs_7_ = f32[80,128]{1,0:T(8,128)S(1)} collective-permute-done((f32[80,128]{1,0:T(8,128)S(1)}, f32[80,128]{1,0:T(8,128)S(1)}, u32[]{:S(2)}, u32[]{:S(2)}) %collective-permute-start.16) | collective-permute-done | bytes 40992 | tf_op jit(solution)/shard_map/ppermute | solution.py:265
  138.0 1.9 shard_map.89
  139.9 0.5 shard_map.90
  140.4 7.6 %collective-permute-start.18 = (f32[272,128]{1,0:T(8,128)S(1)}, f32[272,128]{1,0:T(8,128)S(1)}, u32[]{:S(2)}, u32[]{:S(2)}) collective-permute-start(f32[272,128]{1,0:T(8,128)S(1)} %get-tuple-element.73), channel_id=1, source_target_pairs={{0,48},{48,0},{96,144},{144,96},{192,240},{240,192},{288,336},{336... | collective-permute-start | bytes 417800 | tf_op jit(solution)/shard_map/ppermute | solution.py:261
  148.1 6.2 %collective-permute-done.18 = f32[272,128]{1,0:T(8,128)S(1)} collective-permute-done((f32[272,128]{1,0:T(8,128)S(1)}, f32[272,128]{1,0:T(8,128)S(1)}, u32[]{:S(2)}, u32[]{:S(2)}) %collective-permute-start.18) | collective-permute-done | bytes 139296 | tf_op jit(solution)/shard_map/ppermute | solution.py:261
  154.3 4.4 %collective-permute-start.21 = (f32[136,128]{1,0:T(8,128)S(1)}, f32[136,128]{1,0:T(8,128)S(1)}, u32[]{:S(2)}, u32[]{:S(2)}) collective-permute-start(f32[136,128]{1,0:T(8,128)S(1)} %get-tuple-element.92), channel_id=1, source_target_pairs={{0,96},{48,720},{96,192},{144,48},{192,288},{240,144},{288,384},{3... | collective-permute-start | bytes 208904 | tf_op jit(solution)/shard_map/ppermute | solution.py:267
  158.9 2.0 collective-permute-start.19
  160.9 1.3 collective-permute-start.20
  162.2 0.3 collective-permute-done.19.refs_6_
  162.5 4.2 %collective-permute-done.20.refs_7_ = f32[72,128]{1,0:T(8,128)S(1)} collective-permute-done((f32[72,128]{1,0:T(8,128)S(1)}, f32[72,128]{1,0:T(8,128)S(1)}, u32[]{:S(2)}, u32[]{:S(2)}) %collective-permute-start.20) | collective-permute-done | bytes 36896 | tf_op jit(solution)/shard_map/ppermute | solution.py:265
  166.8 1.4 shard_map.92
  168.2 0.3 shard_map.93
  168.5 7.2 %collective-permute-start.22 = (f32[256,128]{1,0:T(8,128)S(1)}, f32[256,128]{1,0:T(8,128)S(1)}, u32[]{:S(2)}, u32[]{:S(2)}) collective-permute-start(f32[256,128]{1,0:T(8,128)S(1)} %get-tuple-element.79), channel_id=1, source_target_pairs={{0,48},{48,0},{96,144},{144,96},{192,240},{240,192},{288,336},{336... | collective-permute-start | bytes 393224 | tf_op jit(solution)/shard_map/ppermute | solution.py:261
  175.7 8.7 %collective-permute-done.22 = f32[256,128]{1,0:T(8,128)S(1)} collective-permute-done((f32[256,128]{1,0:T(8,128)S(1)}, f32[256,128]{1,0:T(8,128)S(1)}, u32[]{:S(2)}, u32[]{:S(2)}) %collective-permute-start.22) | collective-permute-done | bytes 131104 | tf_op jit(solution)/shard_map/ppermute | solution.py:261
  184.5 3.1 %collective-permute-start.25 = (f32[128,128]{1,0:T(8,128)S(1)}, f32[128,128]{1,0:T(8,128)S(1)}, u32[]{:S(2)}, u32[]{:S(2)}) collective-permute-start(f32[128,128]{1,0:T(8,128)S(1)} %get-tuple-element.94), channel_id=1, source_target_pairs={{0,96},{48,720},{96,192},{144,48},{192,288},{240,144},{288,384},{3... | collective-permute-start | bytes 196616 | tf_op jit(solution)/shard_map/ppermute | solution.py:267
  187.6 1.9 collective-permute-start.23
  189.5 1.3 collective-permute-start.24
  190.8 0.3 collective-permute-done.23.refs_6_
  191.1 4.2 %collective-permute-done.24.refs_7_ = f32[64,128]{1,0:T(8,128)S(1)} collective-permute-done((f32[64,128]{1,0:T(8,128)S(1)}, f32[64,128]{1,0:T(8,128)S(1)}, u32[]{:S(2)}, u32[]{:S(2)}) %collective-permute-start.24) | collective-permute-done | bytes 32800 | tf_op jit(solution)/shard_map/ppermute | solution.py:265
  195.4 1.5 shard_map.95
  197.0 0.8 shard_map.96
  (32 shorter events, 0.9 us)
Async XLA Ops:
  0.6 10.3 %copy-start.1 = (f32[16,32,128]{2,1,0:T(8,128)S(1)}, f32[16,32,128]{2,1,0:T(8,128)}, u32[]{:S(2)}) copy-start(f32[16,32,128]{2,1,0:T(8,128)} %now.1) | copy-start | bytes 786436
  2.7 6.5 %collective-permute-start = (f32[72,512]{1,0:T(8,128)S(1)}, f32[72,512]{1,0:T(8,128)S(1)}, u32[]{:S(2)}, u32[]{:S(2)}) collective-permute-start(f32[72,512]{1,0:T(8,128)S(1)} %get-tuple-element.43), channel_id=1, source_target_pairs={{0,1},{1,2},{2,3},{3,4},{4,5},{5,6},{6,7},{7,8},{8,9},{9,10},{10,1... | collective-permute-start | bytes 442376 | tf_op jit(solution)/shard_map/ppermute | solution.py:305
  4.7 6.3 %collective-permute-start.1 = (f32[72,512]{1,0:T(8,128)S(1)}, f32[72,512]{1,0:T(8,128)S(1)}, u32[]{:S(2)}, u32[]{:S(2)}) collective-permute-start(f32[72,512]{1,0:T(8,128)S(1)} %get-tuple-element.44), channel_id=1, source_target_pairs={{1,0},{2,1},{3,2},{4,3},{5,4},{6,5},{7,6},{8,7},{9,8},{10,9},{11,1... | collective-permute-start | bytes 442376 | tf_op jit(solution)/shard_map/ppermute | solution.py:306
  8.3 18.0 %copy-start.2 = (f32[6,16]{1,0:T(8,128)S(1)}, f32[6,16]{1,0:T(8,128)}, u32[]{:S(2)}) copy-start(f32[6,16]{1,0:T(8,128)} %param.10) | copy-start | bytes 1156
  12.1 26.2 %collective-permute-start.2 = (f32[336,128]{1,0:T(8,128)S(1)}, f32[336,128]{1,0:T(8,128)S(1)}, u32[]{:S(2)}, u32[]{:S(2)}) collective-permute-start(f32[336,128]{1,0:T(8,128)S(1)} %get-tuple-element.49), channel_id=1, source_target_pairs={{0,48},{48,0},{96,144},{144,96},{192,240},{240,192},{288,336},{336... | collective-permute-start | bytes 516104 | tf_op jit(solution)/shard_map/ppermute | solution.py:261
  26.6 15.2 %copy-start = (f32[16,32,128]{2,1,0:T(8,128)S(1)}, f32[16,32,128]{2,1,0:T(8,128)}, u32[]{:S(2)}) copy-start(f32[16,32,128]{2,1,0:T(8,128)} %before.1) | copy-start | bytes 786436
  26.6 15.9 %collective-permute-start.3 = (f32[104,128]{1,0:T(8,128)S(1)}, f32[104,128]{1,0:T(8,128)S(1)}, u32[]{:S(2)}, u32[]{:S(2)}) collective-permute-start(f32[104,128]{1,0:T(8,128)S(1)} %get-tuple-element.50), channel_id=1, source_target_pairs={{0,12},{12,24},{24,36},{1,13},{13,25},{25,37},{2,14},{14,26},{26,3... | collective-permute-start | bytes 159752 | tf_op jit(solution)/shard_map/ppermute | solution.py:264
  30.2 12.4 %collective-permute-start.4 = (f32[104,128]{1,0:T(8,128)S(1)}, f32[104,128]{1,0:T(8,128)S(1)}, u32[]{:S(2)}, u32[]{:S(2)}) collective-permute-start(f32[104,128]{1,0:T(8,128)S(1)} %get-tuple-element.51), channel_id=1, source_target_pairs={{12,0},{24,12},{36,24},{13,1},{25,13},{37,25},{14,2},{26,14},{38,2... | collective-permute-start | bytes 159752 | tf_op jit(solution)/shard_map/ppermute | solution.py:265
  38.3 3.5 %copy-start.3 = (s32[16]{0:T(128)S(1)}, s32[16]{0:T(128)}, u32[]{:S(2)}) copy-start(s32[16]{0:T(128)} %param.11) | copy-start | bytes 196
  38.3 8.6 %collective-permute-start.5 = (f32[168,128]{1,0:T(8,128)S(1)}, f32[168,128]{1,0:T(8,128)S(1)}, u32[]{:S(2)}, u32[]{:S(2)}) collective-permute-start(f32[168,128]{1,0:T(8,128)S(1)} %get-tuple-element.84), channel_id=1, source_target_pairs={{0,96},{48,720},{96,192},{144,48},{192,288},{240,144},{288,384},{3... | collective-permute-start | bytes 258056 | tf_op jit(solution)/shard_map/ppermute | solution.py:267
  47.4 16.7 %collective-permute-start.6 = (f32[320,128]{1,0:T(8,128)S(1)}, f32[320,128]{1,0:T(8,128)S(1)}, u32[]{:S(2)}, u32[]{:S(2)}) collective-permute-start(f32[320,128]{1,0:T(8,128)S(1)} %get-tuple-element.55), channel_id=1, source_target_pairs={{0,48},{48,0},{96,144},{144,96},{192,240},{240,192},{288,336},{336... | collective-permute-start | bytes 491528 | tf_op jit(solution)/shard_map/ppermute | solution.py:261
  64.1 13.8 %collective-permute-start.9 = (f32[160,128]{1,0:T(8,128)S(1)}, f32[160,128]{1,0:T(8,128)S(1)}, u32[]{:S(2)}, u32[]{:S(2)}) collective-permute-start(f32[160,128]{1,0:T(8,128)S(1)} %get-tuple-element.86), channel_id=1, source_target_pairs={{0,96},{48,720},{96,192},{144,48},{192,288},{240,144},{288,384},{3... | collective-permute-start | bytes 245768 | tf_op jit(solution)/shard_map/ppermute | solution.py:267
  66.5 5.2 %collective-permute-start.7 = (f32[96,128]{1,0:T(8,128)S(1)}, f32[96,128]{1,0:T(8,128)S(1)}, u32[]{:S(2)}, u32[]{:S(2)}) collective-permute-start(f32[96,128]{1,0:T(8,128)S(1)} %get-tuple-element.56), channel_id=1, source_target_pairs={{0,12},{12,24},{24,36},{1,13},{13,25},{25,37},{2,14},{14,26},{26,3... | collective-permute-start | bytes 147464 | tf_op jit(solution)/shard_map/ppermute | solution.py:264
  70.0 6.0 %collective-permute-start.8 = (f32[96,128]{1,0:T(8,128)S(1)}, f32[96,128]{1,0:T(8,128)S(1)}, u32[]{:S(2)}, u32[]{:S(2)}) collective-permute-start(f32[96,128]{1,0:T(8,128)S(1)} %get-tuple-element.57), channel_id=1, source_target_pairs={{12,0},{24,12},{36,24},{13,1},{25,13},{37,25},{14,2},{26,14},{38,2... | collective-permute-start | bytes 147464 | tf_op jit(solution)/shard_map/ppermute | solution.py:265
  78.4 16.2 %collective-permute-start.10 = (f32[304,128]{1,0:T(8,128)S(1)}, f32[304,128]{1,0:T(8,128)S(1)}, u32[]{:S(2)}, u32[]{:S(2)}) collective-permute-start(f32[304,128]{1,0:T(8,128)S(1)} %get-tuple-element.61), channel_id=1, source_target_pairs={{0,48},{48,0},{96,144},{144,96},{192,240},{240,192},{288,336},{336... | collective-permute-start | bytes 466952 | tf_op jit(solution)/shard_map/ppermute | solution.py:261
  94.7 13.9 %collective-permute-start.13 = (f32[152,128]{1,0:T(8,128)S(1)}, f32[152,128]{1,0:T(8,128)S(1)}, u32[]{:S(2)}, u32[]{:S(2)}) collective-permute-start(f32[152,128]{1,0:T(8,128)S(1)} %get-tuple-element.88), channel_id=1, source_target_pairs={{0,96},{48,720},{96,192},{144,48},{192,288},{240,144},{288,384},{3... | collective-permute-start | bytes 233480 | tf_op jit(solution)/shard_map/ppermute | solution.py:267
  96.8 5.6 %collective-permute-start.11 = (f32[88,128]{1,0:T(8,128)S(1)}, f32[88,128]{1,0:T(8,128)S(1)}, u32[]{:S(2)}, u32[]{:S(2)}) collective-permute-start(f32[88,128]{1,0:T(8,128)S(1)} %get-tuple-element.62), channel_id=1, source_target_pairs={{0,12},{12,24},{24,36},{1,13},{13,25},{25,37},{2,14},{14,26},{26,3... | collective-permute-start | bytes 135176 | tf_op jit(solution)/shard_map/ppermute | solution.py:264
  100.7 5.9 %collective-permute-start.12 = (f32[88,128]{1,0:T(8,128)S(1)}, f32[88,128]{1,0:T(8,128)S(1)}, u32[]{:S(2)}, u32[]{:S(2)}) collective-permute-start(f32[88,128]{1,0:T(8,128)S(1)} %get-tuple-element.63), channel_id=1, source_target_pairs={{12,0},{24,12},{36,24},{13,1},{25,13},{37,25},{14,2},{26,14},{38,2... | collective-permute-start | bytes 135176 | tf_op jit(solution)/shard_map/ppermute | solution.py:265
  109.2 16.6 %collective-permute-start.14 = (f32[288,128]{1,0:T(8,128)S(1)}, f32[288,128]{1,0:T(8,128)S(1)}, u32[]{:S(2)}, u32[]{:S(2)}) collective-permute-start(f32[288,128]{1,0:T(8,128)S(1)} %get-tuple-element.67), channel_id=1, source_target_pairs={{0,48},{48,0},{96,144},{144,96},{192,240},{240,192},{288,336},{336... | collective-permute-start | bytes 442376 | tf_op jit(solution)/shard_map/ppermute | solution.py:261
  125.8 14.1 %collective-permute-start.17 = (f32[144,128]{1,0:T(8,128)S(1)}, f32[144,128]{1,0:T(8,128)S(1)}, u32[]{:S(2)}, u32[]{:S(2)}) collective-permute-start(f32[144,128]{1,0:T(8,128)S(1)} %get-tuple-element.90), channel_id=1, source_target_pairs={{0,96},{48,720},{96,192},{144,48},{192,288},{240,144},{288,384},{3... | collective-permute-start | bytes 221192 | tf_op jit(solution)/shard_map/ppermute | solution.py:267
  128.6 5.0 %collective-permute-start.15 = (f32[80,128]{1,0:T(8,128)S(1)}, f32[80,128]{1,0:T(8,128)S(1)}, u32[]{:S(2)}, u32[]{:S(2)}) collective-permute-start(f32[80,128]{1,0:T(8,128)S(1)} %get-tuple-element.68), channel_id=1, source_target_pairs={{0,12},{12,24},{24,36},{1,13},{13,25},{25,37},{2,14},{14,26},{26,3... | collective-permute-start | bytes 122888 | tf_op jit(solution)/shard_map/ppermute | solution.py:264
  132.0 5.9 %collective-permute-start.16 = (f32[80,128]{1,0:T(8,128)S(1)}, f32[80,128]{1,0:T(8,128)S(1)}, u32[]{:S(2)}, u32[]{:S(2)}) collective-permute-start(f32[80,128]{1,0:T(8,128)S(1)} %get-tuple-element.69), channel_id=1, source_target_pairs={{12,0},{24,12},{36,24},{13,1},{25,13},{37,25},{14,2},{26,14},{38,2... | collective-permute-start | bytes 122888 | tf_op jit(solution)/shard_map/ppermute | solution.py:265
  140.4 13.8 %collective-permute-start.18 = (f32[272,128]{1,0:T(8,128)S(1)}, f32[272,128]{1,0:T(8,128)S(1)}, u32[]{:S(2)}, u32[]{:S(2)}) collective-permute-start(f32[272,128]{1,0:T(8,128)S(1)} %get-tuple-element.73), channel_id=1, source_target_pairs={{0,48},{48,0},{96,144},{144,96},{192,240},{240,192},{288,336},{336... | collective-permute-start | bytes 417800 | tf_op jit(solution)/shard_map/ppermute | solution.py:261
  154.3 13.9 %collective-permute-start.21 = (f32[136,128]{1,0:T(8,128)S(1)}, f32[136,128]{1,0:T(8,128)S(1)}, u32[]{:S(2)}, u32[]{:S(2)}) collective-permute-start(f32[136,128]{1,0:T(8,128)S(1)} %get-tuple-element.92), channel_id=1, source_target_pairs={{0,96},{48,720},{96,192},{144,48},{192,288},{240,144},{288,384},{3... | collective-permute-start | bytes 208904 | tf_op jit(solution)/shard_map/ppermute | solution.py:267
  158.9 3.6 %collective-permute-start.19 = (f32[72,128]{1,0:T(8,128)S(1)}, f32[72,128]{1,0:T(8,128)S(1)}, u32[]{:S(2)}, u32[]{:S(2)}) collective-permute-start(f32[72,128]{1,0:T(8,128)S(1)} %get-tuple-element.74), channel_id=1, source_target_pairs={{0,12},{12,24},{24,36},{1,13},{13,25},{25,37},{2,14},{14,26},{26,3... | collective-permute-start | bytes 110600 | tf_op jit(solution)/shard_map/ppermute | solution.py:264
  160.9 5.9 %collective-permute-start.20 = (f32[72,128]{1,0:T(8,128)S(1)}, f32[72,128]{1,0:T(8,128)S(1)}, u32[]{:S(2)}, u32[]{:S(2)}) collective-permute-start(f32[72,128]{1,0:T(8,128)S(1)} %get-tuple-element.75), channel_id=1, source_target_pairs={{12,0},{24,12},{36,24},{13,1},{25,13},{37,25},{14,2},{26,14},{38,2... | collective-permute-start | bytes 110600 | tf_op jit(solution)/shard_map/ppermute | solution.py:265
  168.5 15.9 %collective-permute-start.22 = (f32[256,128]{1,0:T(8,128)S(1)}, f32[256,128]{1,0:T(8,128)S(1)}, u32[]{:S(2)}, u32[]{:S(2)}) collective-permute-start(f32[256,128]{1,0:T(8,128)S(1)} %get-tuple-element.79), channel_id=1, source_target_pairs={{0,48},{48,0},{96,144},{144,96},{192,240},{240,192},{288,336},{336... | collective-permute-start | bytes 393224 | tf_op jit(solution)/shard_map/ppermute | solution.py:261
  184.5 12.5 %collective-permute-start.25 = (f32[128,128]{1,0:T(8,128)S(1)}, f32[128,128]{1,0:T(8,128)S(1)}, u32[]{:S(2)}, u32[]{:S(2)}) collective-permute-start(f32[128,128]{1,0:T(8,128)S(1)} %get-tuple-element.94), channel_id=1, source_target_pairs={{0,96},{48,720},{96,192},{144,48},{192,288},{240,144},{288,384},{3... | collective-permute-start | bytes 196616 | tf_op jit(solution)/shard_map/ppermute | solution.py:267
  187.6 3.5 %collective-permute-start.23 = (f32[64,128]{1,0:T(8,128)S(1)}, f32[64,128]{1,0:T(8,128)S(1)}, u32[]{:S(2)}, u32[]{:S(2)}) collective-permute-start(f32[64,128]{1,0:T(8,128)S(1)} %get-tuple-element.80), channel_id=1, source_target_pairs={{0,12},{12,24},{24,36},{1,13},{13,25},{25,37},{2,14},{14,26},{26,3... | collective-permute-start | bytes 98312 | tf_op jit(solution)/shard_map/ppermute | solution.py:264
  189.5 5.8 %collective-permute-start.24 = (f32[64,128]{1,0:T(8,128)S(1)}, f32[64,128]{1,0:T(8,128)S(1)}, u32[]{:S(2)}, u32[]{:S(2)}) collective-permute-start(f32[64,128]{1,0:T(8,128)S(1)} %get-tuple-element.81), channel_id=1, source_target_pairs={{12,0},{24,12},{36,24},{13,1},{25,13},{37,25},{14,2},{26,14},{38,2... | collective-permute-start | bytes 98312 | tf_op jit(solution)/shard_map/ppermute | solution.py:265

commit v3 on v2

--- a/solution.py
+++ b/solution.py
@@ -135,21 +135,17 @@
     widen(2, rate, from_low, from_high, wide_rate)
 
 
-def part_one(step, now, before, rate, cells, amounts, inner, y_low, y_high, *rest):
-    following, wide, halo = rest[0], rest[-2], rest[-1]
+def part_zero(step, now, before, rate, *rest):
+    following, wide = rest[0], rest[-1]
     columns = extra(step)
     tiles = 2 if columns else 1
     _, nx, ny, nz = now.shape
+    edge = jnp.zeros((HALO, nz), jnp.float32)
     for t in range(tiles):
-        for place, y_face in ((8 - HALO, y_low), (8 + ny, y_high)):
-            if t == 0:
-                face = y_face[0 : HALO * nx, :]
-            else:
-                face = unpacked(y_face[HALO * nx : HALO * nx + 2 * columns, 0 : HALO * nx], columns, nz)
-            for x in range(nx):
-                wide[t, x, place : place + HALO, :] = face[HALO * x : HALO * (x + 1), :]
-        for x in range(nx):
+        for x in range(nx):
+            wide[t, x, 8 - HALO : 8, :] = edge
             wide[t, x, 8 : 8 + ny, :] = now[t, x]
+            wide[t, x, 8 + ny : 8 + ny + HALO, :] = edge
     both = jnp.concatenate([now[0].reshape(nx * ny, nz), now[1].reshape(nx * ny, nz)], axis=1)
     i = lax.broadcasted_iota(jnp.int32, (2 * nz, tiles * nz), 0)
     j = lax.broadcasted_iota(jnp.int32, (2 * nz, tiles * nz), 1)
@@ -178,6 +174,37 @@
                 following[x] = value
     if tiles == 1:
         rest[1][...] = now[0]
+
+
+def part_one(step, partial, rate, cells, amounts, inner, y_low, y_high, *rest):
+    following, halo, beside = rest[0], rest[-2], rest[-1]
+    columns = extra(step)
+    tiles = 2 if columns else 1
+    _, nx, ny, nz = rate.shape
+    zeros = jnp.zeros((8, nz), jnp.float32)
+    for t in range(tiles):
+        for x in range(nx):
+            beside[0, t, x, 8:16, :] = zeros
+            beside[1, t, x, 0:8, :] = zeros
+        for n, (y_face, first) in enumerate(((y_low, 4), (y_high, 8))):
+            if t == 0:
+                face = y_face[0 : HALO * nx, :]
+            else:
+                face = unpacked(y_face[HALO * nx : HALO * nx + 2 * columns, 0 : HALO * nx], columns, nz)
+            for x in range(nx):
+                beside[n, t, x, first : first + HALO, :] = face[HALO * x : HALO * (x + 1), :]
+        for x in range(nx):
+            low = high = None
+            for k, weight in enumerate(WEIGHTS, 1):
+                term = jnp.float32(weight) * beside[0, t, x, 8 - k : 16 - k, :]
+                low = term if low is None else low + term
+                term = jnp.float32(weight) * beside[1, t, x, k : 8 + k, :]
+                high = term if high is None else high + term
+            old = partial.at[t, x] if tiles == 2 else partial.at[x]
+            new = following.at[t, x] if tiles == 2 else following.at[x]
+            new[0:8, :] = old[0:8, :] + rate[t, x, 0:8, :] * low
+            new[8 : ny - 8, :] = old[8 : ny - 8, :]
+            new[ny - 8 : ny, :] = old[ny - 8 : ny, :] + rate[t, x, ny - 8 : ny, :] * high
     add_x(following, rate, columns, "inner", inner, halo)
 
     @pl.when(jnp.max(cells[...]) >= 0)
@@ -311,12 +338,19 @@
     for step in range(STEPS):
         last = step == STEPS - 1
         inner, outer, y_low, y_high = exchange(current, pair, extra(step))
+        early = call(
+            lambda *refs, step=step: part_zero(step, *refs),
+            arrays(shape, shape) if last else arrays(field),
+            [VMEM] * 3,
+            (current, before, rate),
+            scratch=[(2, nx, ny + 16, nz)],
+        )
         out = call(
             lambda *refs, step=step: part_one(step, *refs),
-            arrays(shape, shape) if last else arrays(field, face_shape(shape, extra(step + 1))),
-            [VMEM] * 8,
-            (current, before, rate, cells, amounts[step], inner, y_low, y_high),
-            scratch=[(2, nx, ny + 16, nz), (2, HALO, ny, nz)],
+            arrays(shape) if last else arrays(field, face_shape(shape, extra(step + 1))),
+            [VMEM] * 7,
+            (early[0], rate, cells, amounts[step], inner, y_low, y_high),
+            scratch=[(2, HALO, ny, nz), (2, 2, nx, 16, nz)],
         )
         partial = out[0]
         following, *pairs = call(
@@ -327,7 +361,7 @@
             scratch=[(2, HALO, ny, nz)],
         )
         pair = pairs[0] if pairs else None
-        before, current = (out[1], following) if last else (current, following)
+        before, current = (early[1], following) if last else (current, following)
     return current, before
 
 

time: 199 us -> 194 us (0.975)
  waiting for transfers between devices: 66.7 us -> 61.5 us
    ppermute x6, waiting for transfers between devices: 21.2 us -> 16.9 us  [exchange(): from_y_high = lax.ppermute(y_low, 'gy', back(up))]
    ppermute x6, starting transfers between devices: 17.7 us -> 20.4 us  [exchange(): outer = lax.ppermute(swapped[half:], 'gx', onward)]
    pallas_call x20 -> x26, Pallas kernels: 16.6 us -> 16.6 us  [call(): pl.pallas_call(kernel, out_shape=out, in_specs=inputs, out_specs=(VMEM,)...]
  transfers between devices with their start and end apart: 26 -> 26, of which waited for: 19 -> 14; matrix products, arithmetic and copies ran while one was open for 0% -> 0% of each run, Pallas kernels for 6% -> 6%
where the time goes in v3:
time: 194 us; the launch traced here: 193 us
  starting transfers between devices  111 us (57%)
  waiting for transfers between devices  61.5 us (32%)
  Pallas kernels  18.7 us (10%)
    ppermute x6, starting transfers between devices, exchange(): swapped = lax.ppermute(pair, 'gx', [(i, i ^ 1) for i in range(count)])  60 us
    ppermute x6, waiting for transfers between devices, exchange(): swapped = lax.ppermute(pair, 'gx', [(i, i ^ 1) for i in range(count)])  39.7 us
    ppermute x6, starting transfers between devices, exchange(): outer = lax.ppermute(swapped[half:], 'gx', onward)  20.4 us
    ppermute x6, starting transfers between devices, exchange(): from_y_low = lax.ppermute(y_high, 'gy', up)  17.3 us
    ppermute x6, waiting for transfers between devices, exchange(): from_y_high = lax.ppermute(y_low, 'gy', back(up))  16.9 us
    pallas_call x26, Pallas kernels, call(): pl.pallas_call(kernel, out_shape=out, in_specs=inputs, out_specs=(VMEM,)...  16.6 us
    ppermute x6, starting transfers between devices, exchange(): from_y_high = lax.ppermute(y_low, 'gy', back(up))  7.93 us
  transfers between devices with their start and end apart: 26, of which 14 were waited for; matrix products, arithmetic and copies ran while one was open for 0% of the time, Pallas kernels for 6%

profile of v3, /device:TPU:64, one launch (start us, length us, event | category | flops | bytes accessed | tf_op | source)
XLA Modules:
  0.0 193.1 jit_solution(16329577058330257551)
XLA Ops:
  0.6 2.1 %first.1 = (f32[16,32,128]{2,1,0:T(8,128)S(1)}, f32[72,512]{1,0:T(8,128)S(1)}, f32[72,512]{1,0:T(8,128)S(1)}) custom-call(f32[8]{0:T(128)} %velocity_in.1, f32[16,32,128]{2,1,0:T(8,128)} %now.1, f32[16,32,128]{2,1,0:T(8,128)} %before.1, s32[16,32,128]{2,1,0:T(8,128)} %codes_in.1), custom_call_target="tpu_custom_call" | custom-call | flops 5000000 | bytes 1500000 | tf_op jit(solution)/shard_map/first/pallas_call | solution.py:315
  2.7 1.9 collective-permute-start
  4.7 3.6 %collective-permute-start.1 = (f32[72,512]{1,0:T(8,128)S(1)}, f32[72,512]{1,0:T(8,128)S(1)}, u32[]{:S(2)}, u32[]{:S(2)}) collective-permute-start(f32[72,512]{1,0:T(8,128)S(1)} %get-tuple-element.44), channel_id=1, source_target_pairs={{1,0},{2,1},{3,2},{4,3},{5,4},{6,5},{7,6},{8,7},{9,8},{10,9},{11,1... | collective-permute-start | bytes 442376 | tf_op jit(solution)/shard_map/ppermute | solution.py:333
  8.3 0.9 collective-permute-done.from_low
  9.2 1.8 collective-permute-done.1.from_high
  11.0 1.1 shard_map.77
  12.1 14.3 %collective-permute-start.2 = (f32[336,128]{1,0:T(8,128)S(1)}, f32[336,128]{1,0:T(8,128)S(1)}, u32[]{:S(2)}, u32[]{:S(2)}) collective-permute-start(f32[336,128]{1,0:T(8,128)S(1)} %get-tuple-element.49), channel_id=1, source_target_pairs={{0,48},{48,0},{96,144},{144,96},{192,240},{240,192},{288,336},{336... | collective-permute-start | bytes 516104 | tf_op jit(solution)/shard_map/ppermute | solution.py:288
  26.4 0.2 shard_map.80
  26.6 3.5 %collective-permute-start.3 = (f32[104,128]{1,0:T(8,128)S(1)}, f32[104,128]{1,0:T(8,128)S(1)}, u32[]{:S(2)}, u32[]{:S(2)}) collective-permute-start(f32[104,128]{1,0:T(8,128)S(1)} %get-tuple-element.50), channel_id=1, source_target_pairs={{0,12},{12,24},{24,36},{1,13},{13,25},{25,37},{2,14},{14,26},{26,3... | collective-permute-start | bytes 159752 | tf_op jit(solution)/shard_map/ppermute | solution.py:291
  30.2 1.3 collective-permute-start.4
  31.5 6.8 %collective-permute-done.2 = f32[336,128]{1,0:T(8,128)S(1)} collective-permute-done((f32[336,128]{1,0:T(8,128)S(1)}, f32[336,128]{1,0:T(8,128)S(1)}, u32[]{:S(2)}, u32[]{:S(2)}) %collective-permute-start.2) | collective-permute-done | bytes 172064 | tf_op jit(solution)/shard_map/ppermute | solution.py:288
  38.3 3.5 %collective-permute-start.5 = (f32[168,128]{1,0:T(8,128)S(1)}, f32[168,128]{1,0:T(8,128)S(1)}, u32[]{:S(2)}, u32[]{:S(2)}) collective-permute-start(f32[168,128]{1,0:T(8,128)S(1)} %get-tuple-element.84), channel_id=1, source_target_pairs={{0,96},{48,720},{96,192},{144,48},{192,288},{240,144},{288,384},{3... | collective-permute-start | bytes 258056 | tf_op jit(solution)/shard_map/ppermute | solution.py:294
  41.9 0.7 shard_map.78
  42.5 1.1 shard_map.79.refs_0_
  43.8 0.7 shard_map.81
  44.6 2.3 %collective-permute-done.5.refs_2_ = f32[168,128]{1,0:T(8,128)S(1)} collective-permute-done((f32[168,128]{1,0:T(8,128)S(1)}, f32[168,128]{1,0:T(8,128)S(1)}, u32[]{:S(2)}, u32[]{:S(2)}) %collective-permute-start.5) | collective-permute-done | bytes 86048 | tf_op jit(solution)/shard_map/ppermute | solution.py:294
  46.9 0.5 shard_map.82
  47.4 10.3 %collective-permute-start.6 = (f32[320,128]{1,0:T(8,128)S(1)}, f32[320,128]{1,0:T(8,128)S(1)}, u32[]{:S(2)}, u32[]{:S(2)}) collective-permute-start(f32[320,128]{1,0:T(8,128)S(1)} %get-tuple-element.55), channel_id=1, source_target_pairs={{0,48},{48,0},{96,144},{144,96},{192,240},{240,192},{288,336},{336... | collective-permute-start | bytes 491528 | tf_op jit(solution)/shard_map/ppermute | solution.py:288
  57.7 6.4 %collective-permute-done.6 = f32[320,128]{1,0:T(8,128)S(1)} collective-permute-done((f32[320,128]{1,0:T(8,128)S(1)}, f32[320,128]{1,0:T(8,128)S(1)}, u32[]{:S(2)}, u32[]{:S(2)}) %collective-permute-start.6) | collective-permute-done | bytes 163872 | tf_op jit(solution)/shard_map/ppermute | solution.py:288
  64.1 2.0 %collective-permute-start.9 = (f32[160,128]{1,0:T(8,128)S(1)}, f32[160,128]{1,0:T(8,128)S(1)}, u32[]{:S(2)}, u32[]{:S(2)}) collective-permute-start(f32[160,128]{1,0:T(8,128)S(1)} %get-tuple-element.86), channel_id=1, source_target_pairs={{0,96},{48,720},{96,192},{144,48},{192,288},{240,144},{288,384},{3... | collective-permute-start | bytes 245768 | tf_op jit(solution)/shard_map/ppermute | solution.py:294
  66.2 0.2 shard_map.84
  66.4 3.6 %collective-permute-start.7 = (f32[96,128]{1,0:T(8,128)S(1)}, f32[96,128]{1,0:T(8,128)S(1)}, u32[]{:S(2)}, u32[]{:S(2)}) collective-permute-start(f32[96,128]{1,0:T(8,128)S(1)} %get-tuple-element.56), channel_id=1, source_target_pairs={{0,12},{12,24},{24,36},{1,13},{13,25},{25,37},{2,14},{14,26},{26,3... | collective-permute-start | bytes 147464 | tf_op jit(solution)/shard_map/ppermute | solution.py:291
  70.0 1.3 collective-permute-start.8
  71.3 1.1 shard_map.83.refs_0_
  72.4 3.6 %collective-permute-done.8.refs_6_ = f32[96,128]{1,0:T(8,128)S(1)} collective-permute-done((f32[96,128]{1,0:T(8,128)S(1)}, f32[96,128]{1,0:T(8,128)S(1)}, u32[]{:S(2)}, u32[]{:S(2)}) %collective-permute-start.8) | collective-permute-done | bytes 49184 | tf_op jit(solution)/shard_map/ppermute | solution.py:292
  76.0 0.7 shard_map.85
  76.7 0.6 shard_map.86
  77.3 12.4 %collective-permute-start.10 = (f32[304,128]{1,0:T(8,128)S(1)}, f32[304,128]{1,0:T(8,128)S(1)}, u32[]{:S(2)}, u32[]{:S(2)}) collective-permute-start(f32[304,128]{1,0:T(8,128)S(1)} %get-tuple-element.61), channel_id=1, source_target_pairs={{0,48},{48,0},{96,144},{144,96},{192,240},{240,192},{288,336},{336... | collective-permute-start | bytes 466952 | tf_op jit(solution)/shard_map/ppermute | solution.py:288
  89.6 5.5 %collective-permute-done.10 = f32[304,128]{1,0:T(8,128)S(1)} collective-permute-done((f32[304,128]{1,0:T(8,128)S(1)}, f32[304,128]{1,0:T(8,128)S(1)}, u32[]{:S(2)}, u32[]{:S(2)}) %collective-permute-start.10) | collective-permute-done | bytes 155680 | tf_op jit(solution)/shard_map/ppermute | solution.py:288
  95.1 1.9 collective-permute-start.13
  97.1 0.2 shard_map.88
  97.3 3.7 %collective-permute-start.11 = (f32[88,128]{1,0:T(8,128)S(1)}, f32[88,128]{1,0:T(8,128)S(1)}, u32[]{:S(2)}, u32[]{:S(2)}) collective-permute-start(f32[88,128]{1,0:T(8,128)S(1)} %get-tuple-element.62), channel_id=1, source_target_pairs={{0,12},{12,24},{24,36},{1,13},{13,25},{25,37},{2,14},{14,26},{26,3... | collective-permute-start | bytes 135176 | tf_op jit(solution)/shard_map/ppermute | solution.py:291
  101.1 1.3 collective-permute-start.12
  102.4 1.1 shard_map.87.refs_0_
  103.5 3.5 %collective-permute-done.12.refs_6_ = f32[88,128]{1,0:T(8,128)S(1)} collective-permute-done((f32[88,128]{1,0:T(8,128)S(1)}, f32[88,128]{1,0:T(8,128)S(1)}, u32[]{:S(2)}, u32[]{:S(2)}) %collective-permute-start.12) | collective-permute-done | bytes 45088 | tf_op jit(solution)/shard_map/ppermute | solution.py:292
  107.1 0.7 shard_map.89
  107.8 0.6 shard_map.90
  108.3 9.8 %collective-permute-start.14 = (f32[288,128]{1,0:T(8,128)S(1)}, f32[288,128]{1,0:T(8,128)S(1)}, u32[]{:S(2)}, u32[]{:S(2)}) collective-permute-start(f32[288,128]{1,0:T(8,128)S(1)} %get-tuple-element.67), channel_id=1, source_target_pairs={{0,48},{48,0},{96,144},{144,96},{192,240},{240,192},{288,336},{336... | collective-permute-start | bytes 442376 | tf_op jit(solution)/shard_map/ppermute | solution.py:288
  118.1 5.2 %collective-permute-done.14 = f32[288,128]{1,0:T(8,128)S(1)} collective-permute-done((f32[288,128]{1,0:T(8,128)S(1)}, f32[288,128]{1,0:T(8,128)S(1)}, u32[]{:S(2)}, u32[]{:S(2)}) %collective-permute-start.14) | collective-permute-done | bytes 147488 | tf_op jit(solution)/shard_map/ppermute | solution.py:288
  123.4 4.7 %collective-permute-start.17 = (f32[144,128]{1,0:T(8,128)S(1)}, f32[144,128]{1,0:T(8,128)S(1)}, u32[]{:S(2)}, u32[]{:S(2)}) collective-permute-start(f32[144,128]{1,0:T(8,128)S(1)} %get-tuple-element.90), channel_id=1, source_target_pairs={{0,96},{48,720},{96,192},{144,48},{192,288},{240,144},{288,384},{3... | collective-permute-start | bytes 221192 | tf_op jit(solution)/shard_map/ppermute | solution.py:294
  128.1 0.2 shard_map.92
  128.3 1.3 collective-permute-start.15
  129.6 1.5 collective-permute-start.16
  131.1 1.1 shard_map.91.refs_0_
  132.2 3.3 %collective-permute-done.16.refs_6_ = f32[80,128]{1,0:T(8,128)S(1)} collective-permute-done((f32[80,128]{1,0:T(8,128)S(1)}, f32[80,128]{1,0:T(8,128)S(1)}, u32[]{:S(2)}, u32[]{:S(2)}) %collective-permute-start.16) | collective-permute-done | bytes 40992 | tf_op jit(solution)/shard_map/ppermute | solution.py:292
  135.6 0.7 shard_map.93
  136.3 0.5 shard_map.94
  136.9 7.4 %collective-permute-start.18 = (f32[272,128]{1,0:T(8,128)S(1)}, f32[272,128]{1,0:T(8,128)S(1)}, u32[]{:S(2)}, u32[]{:S(2)}) collective-permute-start(f32[272,128]{1,0:T(8,128)S(1)} %get-tuple-element.73), channel_id=1, source_target_pairs={{0,48},{48,0},{96,144},{144,96},{192,240},{240,192},{288,336},{336... | collective-permute-start | bytes 417800 | tf_op jit(solution)/shard_map/ppermute | solution.py:288
  144.3 6.1 %collective-permute-done.18 = f32[272,128]{1,0:T(8,128)S(1)} collective-permute-done((f32[272,128]{1,0:T(8,128)S(1)}, f32[272,128]{1,0:T(8,128)S(1)}, u32[]{:S(2)}, u32[]{:S(2)}) %collective-permute-start.18) | collective-permute-done | bytes 139296 | tf_op jit(solution)/shard_map/ppermute | solution.py:288
  150.4 3.9 %collective-permute-start.21 = (f32[136,128]{1,0:T(8,128)S(1)}, f32[136,128]{1,0:T(8,128)S(1)}, u32[]{:S(2)}, u32[]{:S(2)}) collective-permute-start(f32[136,128]{1,0:T(8,128)S(1)} %get-tuple-element.92), channel_id=1, source_target_pairs={{0,96},{48,720},{96,192},{144,48},{192,288},{240,144},{288,384},{3... | collective-permute-start | bytes 208904 | tf_op jit(solution)/shard_map/ppermute | solution.py:294
  154.5 3.2 %collective-permute-start.19 = (f32[72,128]{1,0:T(8,128)S(1)}, f32[72,128]{1,0:T(8,128)S(1)}, u32[]{:S(2)}, u32[]{:S(2)}) collective-permute-start(f32[72,128]{1,0:T(8,128)S(1)} %get-tuple-element.74), channel_id=1, source_target_pairs={{0,12},{12,24},{24,36},{1,13},{13,25},{25,37},{2,14},{14,26},{26,3... | collective-permute-start | bytes 110600 | tf_op jit(solution)/shard_map/ppermute | solution.py:291
  157.7 1.3 collective-permute-start.20
  159.0 1.1 shard_map.95.refs_0_
  160.1 3.4 %collective-permute-done.20.refs_6_ = f32[72,128]{1,0:T(8,128)S(1)} collective-permute-done((f32[72,128]{1,0:T(8,128)S(1)}, f32[72,128]{1,0:T(8,128)S(1)}, u32[]{:S(2)}, u32[]{:S(2)}) %collective-permute-start.20) | collective-permute-done | bytes 36896 | tf_op jit(solution)/shard_map/ppermute | solution.py:292
  163.6 0.4 shard_map.97
  164.0 0.3 shard_map.98
  164.4 5.9 %collective-permute-start.22 = (f32[256,128]{1,0:T(8,128)S(1)}, f32[256,128]{1,0:T(8,128)S(1)}, u32[]{:S(2)}, u32[]{:S(2)}) collective-permute-start(f32[256,128]{1,0:T(8,128)S(1)} %get-tuple-element.80), channel_id=1, source_target_pairs={{0,48},{48,0},{96,144},{144,96},{192,240},{240,192},{288,336},{336... | collective-permute-start | bytes 393224 | tf_op jit(solution)/shard_map/ppermute | solution.py:288
  170.2 9.7 %collective-permute-done.22 = f32[256,128]{1,0:T(8,128)S(1)} collective-permute-done((f32[256,128]{1,0:T(8,128)S(1)}, f32[256,128]{1,0:T(8,128)S(1)}, u32[]{:S(2)}, u32[]{:S(2)}) %collective-permute-start.22) | collective-permute-done | bytes 131104 | tf_op jit(solution)/shard_map/ppermute | solution.py:288
  179.9 4.3 %collective-permute-start.25 = (f32[128,128]{1,0:T(8,128)S(1)}, f32[128,128]{1,0:T(8,128)S(1)}, u32[]{:S(2)}, u32[]{:S(2)}) collective-permute-start(f32[128,128]{1,0:T(8,128)S(1)} %get-tuple-element.94), channel_id=1, source_target_pairs={{0,96},{48,720},{96,192},{144,48},{192,288},{240,144},{288,384},{3... | collective-permute-start | bytes 196616 | tf_op jit(solution)/shard_map/ppermute | solution.py:294
  184.2 2.0 %collective-permute-start.23 = (f32[64,128]{1,0:T(8,128)S(1)}, f32[64,128]{1,0:T(8,128)S(1)}, u32[]{:S(2)}, u32[]{:S(2)}) collective-permute-start(f32[64,128]{1,0:T(8,128)S(1)} %get-tuple-element.81), channel_id=1, source_target_pairs={{0,12},{12,24},{24,36},{1,13},{13,25},{25,37},{2,14},{14,26},{26,3... | collective-permute-start | bytes 98312 | tf_op jit(solution)/shard_map/ppermute | solution.py:291
  186.2 1.3 collective-permute-start.24
  187.5 1.4 shard_map.99
  188.9 3.1 %collective-permute-done.24.refs_6_ = f32[64,128]{1,0:T(8,128)S(1)} collective-permute-done((f32[64,128]{1,0:T(8,128)S(1)}, f32[64,128]{1,0:T(8,128)S(1)}, u32[]{:S(2)}, u32[]{:S(2)}) %collective-permute-start.24) | collective-permute-done | bytes 32800 | tf_op jit(solution)/shard_map/ppermute | solution.py:292
  192.3 0.8 shard_map.102
  (38 shorter events, 1.1 us)
Async XLA Ops:
  0.6 10.3 %copy-start.1 = (f32[16,32,128]{2,1,0:T(8,128)S(1)}, f32[16,32,128]{2,1,0:T(8,128)}, u32[]{:S(2)}) copy-start(f32[16,32,128]{2,1,0:T(8,128)} %now.1) | copy-start | bytes 786436
  2.7 6.5 %collective-permute-start = (f32[72,512]{1,0:T(8,128)S(1)}, f32[72,512]{1,0:T(8,128)S(1)}, u32[]{:S(2)}, u32[]{:S(2)}) collective-permute-start(f32[72,512]{1,0:T(8,128)S(1)} %get-tuple-element.43), channel_id=1, source_target_pairs={{0,1},{1,2},{2,3},{3,4},{4,5},{5,6},{6,7},{7,8},{8,9},{9,10},{10,1... | collective-permute-start | bytes 442376 | tf_op jit(solution)/shard_map/ppermute | solution.py:332
  4.7 6.3 %collective-permute-start.1 = (f32[72,512]{1,0:T(8,128)S(1)}, f32[72,512]{1,0:T(8,128)S(1)}, u32[]{:S(2)}, u32[]{:S(2)}) collective-permute-start(f32[72,512]{1,0:T(8,128)S(1)} %get-tuple-element.44), channel_id=1, source_target_pairs={{1,0},{2,1},{3,2},{4,3},{5,4},{6,5},{7,6},{8,7},{9,8},{10,9},{11,1... | collective-permute-start | bytes 442376 | tf_op jit(solution)/shard_map/ppermute | solution.py:333
  8.3 18.0 %copy-start.2 = (f32[6,16]{1,0:T(8,128)S(1)}, f32[6,16]{1,0:T(8,128)}, u32[]{:S(2)}) copy-start(f32[6,16]{1,0:T(8,128)} %param.10) | copy-start | bytes 1156
  12.1 26.2 %collective-permute-start.2 = (f32[336,128]{1,0:T(8,128)S(1)}, f32[336,128]{1,0:T(8,128)S(1)}, u32[]{:S(2)}, u32[]{:S(2)}) collective-permute-start(f32[336,128]{1,0:T(8,128)S(1)} %get-tuple-element.49), channel_id=1, source_target_pairs={{0,48},{48,0},{96,144},{144,96},{192,240},{240,192},{288,336},{336... | collective-permute-start | bytes 516104 | tf_op jit(solution)/shard_map/ppermute | solution.py:288
  26.6 15.2 %copy-start = (f32[16,32,128]{2,1,0:T(8,128)S(1)}, f32[16,32,128]{2,1,0:T(8,128)}, u32[]{:S(2)}) copy-start(f32[16,32,128]{2,1,0:T(8,128)} %before.1) | copy-start | bytes 786436
  26.6 17.0 %collective-permute-start.3 = (f32[104,128]{1,0:T(8,128)S(1)}, f32[104,128]{1,0:T(8,128)S(1)}, u32[]{:S(2)}, u32[]{:S(2)}) collective-permute-start(f32[104,128]{1,0:T(8,128)S(1)} %get-tuple-element.50), channel_id=1, source_target_pairs={{0,12},{12,24},{24,36},{1,13},{13,25},{25,37},{2,14},{14,26},{26,3... | collective-permute-start | bytes 159752 | tf_op jit(solution)/shard_map/ppermute | solution.py:291
  30.2 13.5 %collective-permute-start.4 = (f32[104,128]{1,0:T(8,128)S(1)}, f32[104,128]{1,0:T(8,128)S(1)}, u32[]{:S(2)}, u32[]{:S(2)}) collective-permute-start(f32[104,128]{1,0:T(8,128)S(1)} %get-tuple-element.51), channel_id=1, source_target_pairs={{12,0},{24,12},{36,24},{13,1},{25,13},{37,25},{14,2},{26,14},{38,2... | collective-permute-start | bytes 159752 | tf_op jit(solution)/shard_map/ppermute | solution.py:292
  38.3 3.5 %copy-start.3 = (s32[16]{0:T(128)S(1)}, s32[16]{0:T(128)}, u32[]{:S(2)}) copy-start(s32[16]{0:T(128)} %param.11) | copy-start | bytes 196
  38.3 8.6 %collective-permute-start.5 = (f32[168,128]{1,0:T(8,128)S(1)}, f32[168,128]{1,0:T(8,128)S(1)}, u32[]{:S(2)}, u32[]{:S(2)}) collective-permute-start(f32[168,128]{1,0:T(8,128)S(1)} %get-tuple-element.84), channel_id=1, source_target_pairs={{0,96},{48,720},{96,192},{144,48},{192,288},{240,144},{288,384},{3... | collective-permute-start | bytes 258056 | tf_op jit(solution)/shard_map/ppermute | solution.py:294
  47.4 16.7 %collective-permute-start.6 = (f32[320,128]{1,0:T(8,128)S(1)}, f32[320,128]{1,0:T(8,128)S(1)}, u32[]{:S(2)}, u32[]{:S(2)}) collective-permute-start(f32[320,128]{1,0:T(8,128)S(1)} %get-tuple-element.55), channel_id=1, source_target_pairs={{0,48},{48,0},{96,144},{144,96},{192,240},{240,192},{288,336},{336... | collective-permute-start | bytes 491528 | tf_op jit(solution)/shard_map/ppermute | solution.py:288
  64.1 12.6 %collective-permute-start.9 = (f32[160,128]{1,0:T(8,128)S(1)}, f32[160,128]{1,0:T(8,128)S(1)}, u32[]{:S(2)}, u32[]{:S(2)}) collective-permute-start(f32[160,128]{1,0:T(8,128)S(1)} %get-tuple-element.86), channel_id=1, source_target_pairs={{0,96},{48,720},{96,192},{144,48},{192,288},{240,144},{288,384},{3... | collective-permute-start | bytes 245768 | tf_op jit(solution)/shard_map/ppermute | solution.py:294
  66.4 6.0 %collective-permute-start.7 = (f32[96,128]{1,0:T(8,128)S(1)}, f32[96,128]{1,0:T(8,128)S(1)}, u32[]{:S(2)}, u32[]{:S(2)}) collective-permute-start(f32[96,128]{1,0:T(8,128)S(1)} %get-tuple-element.56), channel_id=1, source_target_pairs={{0,12},{12,24},{24,36},{1,13},{13,25},{25,37},{2,14},{14,26},{26,3... | collective-permute-start | bytes 147464 | tf_op jit(solution)/shard_map/ppermute | solution.py:291
  70.0 6.0 %collective-permute-start.8 = (f32[96,128]{1,0:T(8,128)S(1)}, f32[96,128]{1,0:T(8,128)S(1)}, u32[]{:S(2)}, u32[]{:S(2)}) collective-permute-start(f32[96,128]{1,0:T(8,128)S(1)} %get-tuple-element.57), channel_id=1, source_target_pairs={{12,0},{24,12},{36,24},{13,1},{25,13},{37,25},{14,2},{26,14},{38,2... | collective-permute-start | bytes 147464 | tf_op jit(solution)/shard_map/ppermute | solution.py:292
  77.3 17.8 %collective-permute-start.10 = (f32[304,128]{1,0:T(8,128)S(1)}, f32[304,128]{1,0:T(8,128)S(1)}, u32[]{:S(2)}, u32[]{:S(2)}) collective-permute-start(f32[304,128]{1,0:T(8,128)S(1)} %get-tuple-element.61), channel_id=1, source_target_pairs={{0,48},{48,0},{96,144},{144,96},{192,240},{240,192},{288,336},{336... | collective-permute-start | bytes 466952 | tf_op jit(solution)/shard_map/ppermute | solution.py:288
  95.1 12.6 %collective-permute-start.13 = (f32[152,128]{1,0:T(8,128)S(1)}, f32[152,128]{1,0:T(8,128)S(1)}, u32[]{:S(2)}, u32[]{:S(2)}) collective-permute-start(f32[152,128]{1,0:T(8,128)S(1)} %get-tuple-element.88), channel_id=1, source_target_pairs={{0,96},{48,720},{96,192},{144,48},{192,288},{240,144},{288,384},{3... | collective-permute-start | bytes 233480 | tf_op jit(solution)/shard_map/ppermute | solution.py:294
  97.3 6.2 %collective-permute-start.11 = (f32[88,128]{1,0:T(8,128)S(1)}, f32[88,128]{1,0:T(8,128)S(1)}, u32[]{:S(2)}, u32[]{:S(2)}) collective-permute-start(f32[88,128]{1,0:T(8,128)S(1)} %get-tuple-element.62), channel_id=1, source_target_pairs={{0,12},{12,24},{24,36},{1,13},{13,25},{25,37},{2,14},{14,26},{26,3... | collective-permute-start | bytes 135176 | tf_op jit(solution)/shard_map/ppermute | solution.py:291
  101.1 5.9 %collective-permute-start.12 = (f32[88,128]{1,0:T(8,128)S(1)}, f32[88,128]{1,0:T(8,128)S(1)}, u32[]{:S(2)}, u32[]{:S(2)}) collective-permute-start(f32[88,128]{1,0:T(8,128)S(1)} %get-tuple-element.63), channel_id=1, source_target_pairs={{12,0},{24,12},{36,24},{13,1},{25,13},{37,25},{14,2},{26,14},{38,2... | collective-permute-start | bytes 135176 | tf_op jit(solution)/shard_map/ppermute | solution.py:292
  108.3 15.0 %collective-permute-start.14 = (f32[288,128]{1,0:T(8,128)S(1)}, f32[288,128]{1,0:T(8,128)S(1)}, u32[]{:S(2)}, u32[]{:S(2)}) collective-permute-start(f32[288,128]{1,0:T(8,128)S(1)} %get-tuple-element.67), channel_id=1, source_target_pairs={{0,48},{48,0},{96,144},{144,96},{192,240},{240,192},{288,336},{336... | collective-permute-start | bytes 442376 | tf_op jit(solution)/shard_map/ppermute | solution.py:288
  123.4 13.0 %collective-permute-start.17 = (f32[144,128]{1,0:T(8,128)S(1)}, f32[144,128]{1,0:T(8,128)S(1)}, u32[]{:S(2)}, u32[]{:S(2)}) collective-permute-start(f32[144,128]{1,0:T(8,128)S(1)} %get-tuple-element.90), channel_id=1, source_target_pairs={{0,96},{48,720},{96,192},{144,48},{192,288},{240,144},{288,384},{3... | collective-permute-start | bytes 221192 | tf_op jit(solution)/shard_map/ppermute | solution.py:294
  128.3 3.9 %collective-permute-start.15 = (f32[80,128]{1,0:T(8,128)S(1)}, f32[80,128]{1,0:T(8,128)S(1)}, u32[]{:S(2)}, u32[]{:S(2)}) collective-permute-start(f32[80,128]{1,0:T(8,128)S(1)} %get-tuple-element.68), channel_id=1, source_target_pairs={{0,12},{12,24},{24,36},{1,13},{13,25},{25,37},{2,14},{14,26},{26,3... | collective-permute-start | bytes 122888 | tf_op jit(solution)/shard_map/ppermute | solution.py:291
  129.6 5.9 %collective-permute-start.16 = (f32[80,128]{1,0:T(8,128)S(1)}, f32[80,128]{1,0:T(8,128)S(1)}, u32[]{:S(2)}, u32[]{:S(2)}) collective-permute-start(f32[80,128]{1,0:T(8,128)S(1)} %get-tuple-element.69), channel_id=1, source_target_pairs={{12,0},{24,12},{36,24},{13,1},{25,13},{37,25},{14,2},{26,14},{38,2... | collective-permute-start | bytes 122888 | tf_op jit(solution)/shard_map/ppermute | solution.py:292
  136.9 13.5 %collective-permute-start.18 = (f32[272,128]{1,0:T(8,128)S(1)}, f32[272,128]{1,0:T(8,128)S(1)}, u32[]{:S(2)}, u32[]{:S(2)}) collective-permute-start(f32[272,128]{1,0:T(8,128)S(1)} %get-tuple-element.73), channel_id=1, source_target_pairs={{0,48},{48,0},{96,144},{144,96},{192,240},{240,192},{288,336},{336... | collective-permute-start | bytes 417800 | tf_op jit(solution)/shard_map/ppermute | solution.py:288
  150.4 13.6 %collective-permute-start.21 = (f32[136,128]{1,0:T(8,128)S(1)}, f32[136,128]{1,0:T(8,128)S(1)}, u32[]{:S(2)}, u32[]{:S(2)}) collective-permute-start(f32[136,128]{1,0:T(8,128)S(1)} %get-tuple-element.92), channel_id=1, source_target_pairs={{0,96},{48,720},{96,192},{144,48},{192,288},{240,144},{288,384},{3... | collective-permute-start | bytes 208904 | tf_op jit(solution)/shard_map/ppermute | solution.py:294
  154.5 5.6 %collective-permute-start.19 = (f32[72,128]{1,0:T(8,128)S(1)}, f32[72,128]{1,0:T(8,128)S(1)}, u32[]{:S(2)}, u32[]{:S(2)}) collective-permute-start(f32[72,128]{1,0:T(8,128)S(1)} %get-tuple-element.74), channel_id=1, source_target_pairs={{0,12},{12,24},{24,36},{1,13},{13,25},{25,37},{2,14},{14,26},{26,3... | collective-permute-start | bytes 110600 | tf_op jit(solution)/shard_map/ppermute | solution.py:291
  157.7 5.9 %collective-permute-start.20 = (f32[72,128]{1,0:T(8,128)S(1)}, f32[72,128]{1,0:T(8,128)S(1)}, u32[]{:S(2)}, u32[]{:S(2)}) collective-permute-start(f32[72,128]{1,0:T(8,128)S(1)} %get-tuple-element.75), channel_id=1, source_target_pairs={{12,0},{24,12},{36,24},{13,1},{25,13},{37,25},{14,2},{26,14},{38,2... | collective-permute-start | bytes 110600 | tf_op jit(solution)/shard_map/ppermute | solution.py:292
  164.4 15.5 %collective-permute-start.22 = (f32[256,128]{1,0:T(8,128)S(1)}, f32[256,128]{1,0:T(8,128)S(1)}, u32[]{:S(2)}, u32[]{:S(2)}) collective-permute-start(f32[256,128]{1,0:T(8,128)S(1)} %get-tuple-element.80), channel_id=1, source_target_pairs={{0,48},{48,0},{96,144},{144,96},{192,240},{240,192},{288,336},{336... | collective-permute-start | bytes 393224 | tf_op jit(solution)/shard_map/ppermute | solution.py:288
  179.9 12.4 %collective-permute-start.25 = (f32[128,128]{1,0:T(8,128)S(1)}, f32[128,128]{1,0:T(8,128)S(1)}, u32[]{:S(2)}, u32[]{:S(2)}) collective-permute-start(f32[128,128]{1,0:T(8,128)S(1)} %get-tuple-element.94), channel_id=1, source_target_pairs={{0,96},{48,720},{96,192},{144,48},{192,288},{240,144},{288,384},{3... | collective-permute-start | bytes 196616 | tf_op jit(solution)/shard_map/ppermute | solution.py:294
  184.2 4.7 %collective-permute-start.23 = (f32[64,128]{1,0:T(8,128)S(1)}, f32[64,128]{1,0:T(8,128)S(1)}, u32[]{:S(2)}, u32[]{:S(2)}) collective-permute-start(f32[64,128]{1,0:T(8,128)S(1)} %get-tuple-element.81), channel_id=1, source_target_pairs={{0,12},{12,24},{24,36},{1,13},{13,25},{25,37},{2,14},{14,26},{26,3... | collective-permute-start | bytes 98312 | tf_op jit(solution)/shard_map/ppermute | solution.py:291
  186.2 5.8 %collective-permute-start.24 = (f32[64,128]{1,0:T(8,128)S(1)}, f32[64,128]{1,0:T(8,128)S(1)}, u32[]{:S(2)}, u32[]{:S(2)}) collective-permute-start(f32[64,128]{1,0:T(8,128)S(1)} %get-tuple-element.82), channel_id=1, source_target_pairs={{12,0},{24,12},{36,24},{13,1},{25,13},{37,25},{14,2},{26,14},{38,2... | collective-permute-start | bytes 98312 | tf_op jit(solution)/shard_map/ppermute | solution.py:292

commit v4 on v3

--- a/solution.py
+++ b/solution.py
@@ -94,13 +94,23 @@
     copies = [
         pltpu.make_async_copy(source, target, arrived.at[n])
         for n, (source, target) in enumerate(
-            ((velocity_in, velocity), (codes_in, codes), (now_in, now), (before_in, before))
+            ((now_in, now), (before_in, before), (velocity_in, velocity), (codes_in, codes))
         )
     ]
     for copy in copies:
         copy.start()
+
+    def pack(place, field):
+        both = packed(field[...].reshape(nx * ny, nz), DEEP)
+        z_low[place * DEEP : (place + 1) * DEEP, :] = both[0:DEEP]
+        z_high[place * DEEP : (place + 1) * DEEP, :] = both[DEEP : 2 * DEEP]
+
     copies[0].wait()
+    pack(0, now)
     copies[1].wait()
+    pack(1, before)
+    copies[2].wait()
+    copies[3].wait()
     squares = [velocity[r] * velocity[r] for r in range(regions)]
     for x in range(nx):
         code = codes[x]
@@ -108,12 +118,7 @@
         for r in range(1, regions):
             value = jnp.where(code == r, squares[r], value)
         rate[x] = value
-    copies[2].wait()
-    copies[3].wait()
-    for place, field in enumerate((now, before, rate)):
-        both = packed(field[...].reshape(nx * ny, nz), DEEP)
-        z_low[place * DEEP : (place + 1) * DEEP, :] = both[0:DEEP]
-        z_high[place * DEEP : (place + 1) * DEEP, :] = both[DEEP : 2 * DEEP]
+    pack(2, rate)
 
 
 def widen(place, field, from_low, from_high, wide):
@@ -224,6 +229,7 @@
                     here = following.at[x]
                 row = here[pl.ds(y, 1), :]
                 here[pl.ds(y, 1), :] = row + jnp.where(lanes == number % nz, amounts[s : s + 1, :], jnp.float32(0))
+
     if tiles == 2:
         pack_x(following, extra(step + 1), "inner", rest[1])
 

time: 194 us -> 194 us (level)
    ppermute x6, starting transfers between devices: 17.3 us -> 19.8 us  [exchange(): from_y_low = lax.ppermute(y_high, 'gy', up)]
    ppermute x6, starting transfers between devices: 20.4 us -> 18.1 us  [exchange(): outer = lax.ppermute(swapped[half:], 'gx', onward)]
where the time goes in v4:
time: 194 us; the launch traced here: 193 us
  starting transfers between devices  111 us (57%)
  waiting for transfers between devices  61.4 us (32%)
  Pallas kernels  18.9 us (10%)
    ppermute x6, starting transfers between devices, exchange(): swapped = lax.ppermute(pair, 'gx', [(i, i ^ 1) for i in range(count)])  59.9 us
    ppermute x6, waiting for transfers between devices, exchange(): swapped = lax.ppermute(pair, 'gx', [(i, i ^ 1) for i in range(count)])  39.5 us
    ppermute x6, starting transfers between devices, exchange(): from_y_low = lax.ppermute(y_high, 'gy', up)  19.8 us
    ppermute x6, starting transfers between devices, exchange(): outer = lax.ppermute(swapped[half:], 'gx', onward)  18.1 us
    ppermute x6, waiting for transfers between devices, exchange(): from_y_high = lax.ppermute(y_low, 'gy', back(up))  16.9 us
    pallas_call x26, Pallas kernels, call(): pl.pallas_call(kernel, out_shape=out, in_specs=inputs, out_specs=(VMEM,)...  16.6 us
    ppermute x6, starting transfers between devices, exchange(): from_y_high = lax.ppermute(y_low, 'gy', back(up))  7.93 us
  transfers between devices with their start and end apart: 26, of which 14 were waited for; matrix products, arithmetic and copies ran while one was open for 0% of the time, Pallas kernels for 6%

profile of v4, /device:TPU:64, one launch (start us, length us, event | category | flops | bytes accessed | tf_op | source)
XLA Modules:
  0.0 193.3 jit_solution(11005229554943433380)
XLA Ops:
  0.6 2.3 %first.1 = (f32[16,32,128]{2,1,0:T(8,128)S(1)}, f32[72,512]{1,0:T(8,128)S(1)}, f32[72,512]{1,0:T(8,128)S(1)}) custom-call(f32[8]{0:T(128)} %velocity_in.1, f32[16,32,128]{2,1,0:T(8,128)} %now.1, f32[16,32,128]{2,1,0:T(8,128)} %before.1, s32[16,32,128]{2,1,0:T(8,128)} %codes_in.1), custom_call_target="tpu_custom_call" | custom-call | flops 5000000 | bytes 1500000 | tf_op jit(solution)/shard_map/first/pallas_call | solution.py:321
  2.9 1.9 collective-permute-start
  4.9 3.6 %collective-permute-start.1 = (f32[72,512]{1,0:T(8,128)S(1)}, f32[72,512]{1,0:T(8,128)S(1)}, u32[]{:S(2)}, u32[]{:S(2)}) collective-permute-start(f32[72,512]{1,0:T(8,128)S(1)} %get-tuple-element.44), channel_id=1, source_target_pairs={{1,0},{2,1},{3,2},{4,3},{5,4},{6,5},{7,6},{8,7},{9,8},{10,9},{11,1... | collective-permute-start | bytes 442376 | tf_op jit(solution)/shard_map/ppermute | solution.py:339
  8.5 0.9 collective-permute-done.from_low
  9.4 1.8 collective-permute-done.1.from_high
  11.2 1.1 shard_map.77
  12.3 14.3 %collective-permute-start.2 = (f32[336,128]{1,0:T(8,128)S(1)}, f32[336,128]{1,0:T(8,128)S(1)}, u32[]{:S(2)}, u32[]{:S(2)}) collective-permute-start(f32[336,128]{1,0:T(8,128)S(1)} %get-tuple-element.49), channel_id=1, source_target_pairs={{0,48},{48,0},{96,144},{144,96},{192,240},{240,192},{288,336},{336... | collective-permute-start | bytes 516104 | tf_op jit(solution)/shard_map/ppermute | solution.py:294
  26.6 0.2 shard_map.80
  26.8 3.5 %collective-permute-start.3 = (f32[104,128]{1,0:T(8,128)S(1)}, f32[104,128]{1,0:T(8,128)S(1)}, u32[]{:S(2)}, u32[]{:S(2)}) collective-permute-start(f32[104,128]{1,0:T(8,128)S(1)} %get-tuple-element.50), channel_id=1, source_target_pairs={{0,12},{12,24},{24,36},{1,13},{13,25},{25,37},{2,14},{14,26},{26,3... | collective-permute-start | bytes 159752 | tf_op jit(solution)/shard_map/ppermute | solution.py:297
  30.4 1.3 collective-permute-start.4
  31.7 6.8 %collective-permute-done.2 = f32[336,128]{1,0:T(8,128)S(1)} collective-permute-done((f32[336,128]{1,0:T(8,128)S(1)}, f32[336,128]{1,0:T(8,128)S(1)}, u32[]{:S(2)}, u32[]{:S(2)}) %collective-permute-start.2) | collective-permute-done | bytes 172064 | tf_op jit(solution)/shard_map/ppermute | solution.py:294
  38.5 3.5 %collective-permute-start.5 = (f32[168,128]{1,0:T(8,128)S(1)}, f32[168,128]{1,0:T(8,128)S(1)}, u32[]{:S(2)}, u32[]{:S(2)}) collective-permute-start(f32[168,128]{1,0:T(8,128)S(1)} %get-tuple-element.84), channel_id=1, source_target_pairs={{0,96},{48,720},{96,192},{144,48},{192,288},{240,144},{288,384},{3... | collective-permute-start | bytes 258056 | tf_op jit(solution)/shard_map/ppermute | solution.py:300
  42.1 0.7 shard_map.78
  42.8 1.1 shard_map.79.refs_0_
  44.0 0.7 shard_map.81
  44.8 2.3 %collective-permute-done.5.refs_2_ = f32[168,128]{1,0:T(8,128)S(1)} collective-permute-done((f32[168,128]{1,0:T(8,128)S(1)}, f32[168,128]{1,0:T(8,128)S(1)}, u32[]{:S(2)}, u32[]{:S(2)}) %collective-permute-start.5) | collective-permute-done | bytes 86048 | tf_op jit(solution)/shard_map/ppermute | solution.py:300
  47.1 0.5 shard_map.82
  47.6 10.3 %collective-permute-start.6 = (f32[320,128]{1,0:T(8,128)S(1)}, f32[320,128]{1,0:T(8,128)S(1)}, u32[]{:S(2)}, u32[]{:S(2)}) collective-permute-start(f32[320,128]{1,0:T(8,128)S(1)} %get-tuple-element.55), channel_id=1, source_target_pairs={{0,48},{48,0},{96,144},{144,96},{192,240},{240,192},{288,336},{336... | collective-permute-start | bytes 491528 | tf_op jit(solution)/shard_map/ppermute | solution.py:294
  57.9 6.4 %collective-permute-done.6 = f32[320,128]{1,0:T(8,128)S(1)} collective-permute-done((f32[320,128]{1,0:T(8,128)S(1)}, f32[320,128]{1,0:T(8,128)S(1)}, u32[]{:S(2)}, u32[]{:S(2)}) %collective-permute-start.6) | collective-permute-done | bytes 163872 | tf_op jit(solution)/shard_map/ppermute | solution.py:294
  64.3 2.0 %collective-permute-start.9 = (f32[160,128]{1,0:T(8,128)S(1)}, f32[160,128]{1,0:T(8,128)S(1)}, u32[]{:S(2)}, u32[]{:S(2)}) collective-permute-start(f32[160,128]{1,0:T(8,128)S(1)} %get-tuple-element.86), channel_id=1, source_target_pairs={{0,96},{48,720},{96,192},{144,48},{192,288},{240,144},{288,384},{3... | collective-permute-start | bytes 245768 | tf_op jit(solution)/shard_map/ppermute | solution.py:300
  66.4 0.2 shard_map.84
  66.6 3.6 %collective-permute-start.7 = (f32[96,128]{1,0:T(8,128)S(1)}, f32[96,128]{1,0:T(8,128)S(1)}, u32[]{:S(2)}, u32[]{:S(2)}) collective-permute-start(f32[96,128]{1,0:T(8,128)S(1)} %get-tuple-element.56), channel_id=1, source_target_pairs={{0,12},{12,24},{24,36},{1,13},{13,25},{25,37},{2,14},{14,26},{26,3... | collective-permute-start | bytes 147464 | tf_op jit(solution)/shard_map/ppermute | solution.py:297
  70.2 1.3 collective-permute-start.8
  71.5 1.1 shard_map.83.refs_0_
  72.6 3.5 %collective-permute-done.8.refs_6_ = f32[96,128]{1,0:T(8,128)S(1)} collective-permute-done((f32[96,128]{1,0:T(8,128)S(1)}, f32[96,128]{1,0:T(8,128)S(1)}, u32[]{:S(2)}, u32[]{:S(2)}) %collective-permute-start.8) | collective-permute-done | bytes 49184 | tf_op jit(solution)/shard_map/ppermute | solution.py:298
  76.2 0.7 shard_map.85
  76.9 0.6 shard_map.86
  77.5 12.3 %collective-permute-start.10 = (f32[304,128]{1,0:T(8,128)S(1)}, f32[304,128]{1,0:T(8,128)S(1)}, u32[]{:S(2)}, u32[]{:S(2)}) collective-permute-start(f32[304,128]{1,0:T(8,128)S(1)} %get-tuple-element.61), channel_id=1, source_target_pairs={{0,48},{48,0},{96,144},{144,96},{192,240},{240,192},{288,336},{336... | collective-permute-start | bytes 466952 | tf_op jit(solution)/shard_map/ppermute | solution.py:294
  89.9 5.5 %collective-permute-done.10 = f32[304,128]{1,0:T(8,128)S(1)} collective-permute-done((f32[304,128]{1,0:T(8,128)S(1)}, f32[304,128]{1,0:T(8,128)S(1)}, u32[]{:S(2)}, u32[]{:S(2)}) %collective-permute-start.10) | collective-permute-done | bytes 155680 | tf_op jit(solution)/shard_map/ppermute | solution.py:294
  95.3 1.9 collective-permute-start.13
  97.3 0.2 shard_map.88
  97.5 3.8 %collective-permute-start.11 = (f32[88,128]{1,0:T(8,128)S(1)}, f32[88,128]{1,0:T(8,128)S(1)}, u32[]{:S(2)}, u32[]{:S(2)}) collective-permute-start(f32[88,128]{1,0:T(8,128)S(1)} %get-tuple-element.62), channel_id=1, source_target_pairs={{0,12},{12,24},{24,36},{1,13},{13,25},{25,37},{2,14},{14,26},{26,3... | collective-permute-start | bytes 135176 | tf_op jit(solution)/shard_map/ppermute | solution.py:297
  101.3 1.3 collective-permute-start.12
  102.6 1.1 shard_map.87.refs_0_
  103.7 3.5 %collective-permute-done.12.refs_6_ = f32[88,128]{1,0:T(8,128)S(1)} collective-permute-done((f32[88,128]{1,0:T(8,128)S(1)}, f32[88,128]{1,0:T(8,128)S(1)}, u32[]{:S(2)}, u32[]{:S(2)}) %collective-permute-start.12) | collective-permute-done | bytes 45088 | tf_op jit(solution)/shard_map/ppermute | solution.py:298
  107.3 0.7 shard_map.89
  108.0 0.6 shard_map.90
  108.5 9.7 %collective-permute-start.14 = (f32[288,128]{1,0:T(8,128)S(1)}, f32[288,128]{1,0:T(8,128)S(1)}, u32[]{:S(2)}, u32[]{:S(2)}) collective-permute-start(f32[288,128]{1,0:T(8,128)S(1)} %get-tuple-element.67), channel_id=1, source_target_pairs={{0,48},{48,0},{96,144},{144,96},{192,240},{240,192},{288,336},{336... | collective-permute-start | bytes 442376 | tf_op jit(solution)/shard_map/ppermute | solution.py:294
  118.3 5.2 %collective-permute-done.14 = f32[288,128]{1,0:T(8,128)S(1)} collective-permute-done((f32[288,128]{1,0:T(8,128)S(1)}, f32[288,128]{1,0:T(8,128)S(1)}, u32[]{:S(2)}, u32[]{:S(2)}) %collective-permute-start.14) | collective-permute-done | bytes 147488 | tf_op jit(solution)/shard_map/ppermute | solution.py:294
  123.5 4.8 %collective-permute-start.17 = (f32[144,128]{1,0:T(8,128)S(1)}, f32[144,128]{1,0:T(8,128)S(1)}, u32[]{:S(2)}, u32[]{:S(2)}) collective-permute-start(f32[144,128]{1,0:T(8,128)S(1)} %get-tuple-element.90), channel_id=1, source_target_pairs={{0,96},{48,720},{96,192},{144,48},{192,288},{240,144},{288,384},{3... | collective-permute-start | bytes 221192 | tf_op jit(solution)/shard_map/ppermute | solution.py:300
  128.3 0.2 shard_map.92
  128.5 1.3 collective-permute-start.15
  129.8 1.5 collective-permute-start.16
  131.3 1.1 shard_map.91.refs_0_
  132.5 3.3 %collective-permute-done.16.refs_6_ = f32[80,128]{1,0:T(8,128)S(1)} collective-permute-done((f32[80,128]{1,0:T(8,128)S(1)}, f32[80,128]{1,0:T(8,128)S(1)}, u32[]{:S(2)}, u32[]{:S(2)}) %collective-permute-start.16) | collective-permute-done | bytes 40992 | tf_op jit(solution)/shard_map/ppermute | solution.py:298
  135.8 0.7 shard_map.93
  136.5 0.5 shard_map.94
  137.1 7.4 %collective-permute-start.18 = (f32[272,128]{1,0:T(8,128)S(1)}, f32[272,128]{1,0:T(8,128)S(1)}, u32[]{:S(2)}, u32[]{:S(2)}) collective-permute-start(f32[272,128]{1,0:T(8,128)S(1)} %get-tuple-element.73), channel_id=1, source_target_pairs={{0,48},{48,0},{96,144},{144,96},{192,240},{240,192},{288,336},{336... | collective-permute-start | bytes 417800 | tf_op jit(solution)/shard_map/ppermute | solution.py:294
  144.5 6.1 %collective-permute-done.18 = f32[272,128]{1,0:T(8,128)S(1)} collective-permute-done((f32[272,128]{1,0:T(8,128)S(1)}, f32[272,128]{1,0:T(8,128)S(1)}, u32[]{:S(2)}, u32[]{:S(2)}) %collective-permute-start.18) | collective-permute-done | bytes 139296 | tf_op jit(solution)/shard_map/ppermute | solution.py:294
  150.6 3.9 %collective-permute-start.21 = (f32[136,128]{1,0:T(8,128)S(1)}, f32[136,128]{1,0:T(8,128)S(1)}, u32[]{:S(2)}, u32[]{:S(2)}) collective-permute-start(f32[136,128]{1,0:T(8,128)S(1)} %get-tuple-element.92), channel_id=1, source_target_pairs={{0,96},{48,720},{96,192},{144,48},{192,288},{240,144},{288,384},{3... | collective-permute-start | bytes 208904 | tf_op jit(solution)/shard_map/ppermute | solution.py:300
  154.7 3.1 %collective-permute-start.19 = (f32[72,128]{1,0:T(8,128)S(1)}, f32[72,128]{1,0:T(8,128)S(1)}, u32[]{:S(2)}, u32[]{:S(2)}) collective-permute-start(f32[72,128]{1,0:T(8,128)S(1)} %get-tuple-element.74), channel_id=1, source_target_pairs={{0,12},{12,24},{24,36},{1,13},{13,25},{25,37},{2,14},{14,26},{26,3... | collective-permute-start | bytes 110600 | tf_op jit(solution)/shard_map/ppermute | solution.py:297
  157.8 1.3 collective-permute-start.20
  159.1 1.1 shard_map.95.refs_0_
  160.2 3.4 %collective-permute-done.20.refs_6_ = f32[72,128]{1,0:T(8,128)S(1)} collective-permute-done((f32[72,128]{1,0:T(8,128)S(1)}, f32[72,128]{1,0:T(8,128)S(1)}, u32[]{:S(2)}, u32[]{:S(2)}) %collective-permute-start.20) | collective-permute-done | bytes 36896 | tf_op jit(solution)/shard_map/ppermute | solution.py:298
  163.7 0.4 shard_map.97
  164.2 0.3 shard_map.98
  164.5 5.8 %collective-permute-start.22 = (f32[256,128]{1,0:T(8,128)S(1)}, f32[256,128]{1,0:T(8,128)S(1)}, u32[]{:S(2)}, u32[]{:S(2)}) collective-permute-start(f32[256,128]{1,0:T(8,128)S(1)} %get-tuple-element.80), channel_id=1, source_target_pairs={{0,48},{48,0},{96,144},{144,96},{192,240},{240,192},{288,336},{336... | collective-permute-start | bytes 393224 | tf_op jit(solution)/shard_map/ppermute | solution.py:294
  170.3 9.6 %collective-permute-done.22 = f32[256,128]{1,0:T(8,128)S(1)} collective-permute-done((f32[256,128]{1,0:T(8,128)S(1)}, f32[256,128]{1,0:T(8,128)S(1)}, u32[]{:S(2)}, u32[]{:S(2)}) %collective-permute-start.22) | collective-permute-done | bytes 131104 | tf_op jit(solution)/shard_map/ppermute | solution.py:294
  179.9 1.9 collective-permute-start.25
  181.8 4.6 %collective-permute-start.23 = (f32[64,128]{1,0:T(8,128)S(1)}, f32[64,128]{1,0:T(8,128)S(1)}, u32[]{:S(2)}, u32[]{:S(2)}) collective-permute-start(f32[64,128]{1,0:T(8,128)S(1)} %get-tuple-element.81), channel_id=1, source_target_pairs={{0,12},{12,24},{24,36},{1,13},{13,25},{25,37},{2,14},{14,26},{26,3... | collective-permute-start | bytes 98312 | tf_op jit(solution)/shard_map/ppermute | solution.py:297
  186.5 1.3 collective-permute-start.24
  187.8 1.4 shard_map.99
  189.2 3.1 %collective-permute-done.24.refs_6_ = f32[64,128]{1,0:T(8,128)S(1)} collective-permute-done((f32[64,128]{1,0:T(8,128)S(1)}, f32[64,128]{1,0:T(8,128)S(1)}, u32[]{:S(2)}, u32[]{:S(2)}) %collective-permute-start.24) | collective-permute-done | bytes 32800 | tf_op jit(solution)/shard_map/ppermute | solution.py:298
  192.6 0.8 shard_map.102
  (38 shorter events, 1.1 us)
Async XLA Ops:
  0.6 10.5 %copy-start.1 = (f32[16,32,128]{2,1,0:T(8,128)S(1)}, f32[16,32,128]{2,1,0:T(8,128)}, u32[]{:S(2)}) copy-start(f32[16,32,128]{2,1,0:T(8,128)} %now.1) | copy-start | bytes 786436
  2.9 6.5 %collective-permute-start = (f32[72,512]{1,0:T(8,128)S(1)}, f32[72,512]{1,0:T(8,128)S(1)}, u32[]{:S(2)}, u32[]{:S(2)}) collective-permute-start(f32[72,512]{1,0:T(8,128)S(1)} %get-tuple-element.43), channel_id=1, source_target_pairs={{0,1},{1,2},{2,3},{3,4},{4,5},{5,6},{6,7},{7,8},{8,9},{9,10},{10,1... | collective-permute-start | bytes 442376 | tf_op jit(solution)/shard_map/ppermute | solution.py:338
  4.9 6.3 %collective-permute-start.1 = (f32[72,512]{1,0:T(8,128)S(1)}, f32[72,512]{1,0:T(8,128)S(1)}, u32[]{:S(2)}, u32[]{:S(2)}) collective-permute-start(f32[72,512]{1,0:T(8,128)S(1)} %get-tuple-element.44), channel_id=1, source_target_pairs={{1,0},{2,1},{3,2},{4,3},{5,4},{6,5},{7,6},{8,7},{9,8},{10,9},{11,1... | collective-permute-start | bytes 442376 | tf_op jit(solution)/shard_map/ppermute | solution.py:339
  8.5 18.0 %copy-start.2 = (f32[6,16]{1,0:T(8,128)S(1)}, f32[6,16]{1,0:T(8,128)}, u32[]{:S(2)}) copy-start(f32[6,16]{1,0:T(8,128)} %param.10) | copy-start | bytes 1156
  12.3 26.2 %collective-permute-start.2 = (f32[336,128]{1,0:T(8,128)S(1)}, f32[336,128]{1,0:T(8,128)S(1)}, u32[]{:S(2)}, u32[]{:S(2)}) collective-permute-start(f32[336,128]{1,0:T(8,128)S(1)} %get-tuple-element.49), channel_id=1, source_target_pairs={{0,48},{48,0},{96,144},{144,96},{192,240},{240,192},{288,336},{336... | collective-permute-start | bytes 516104 | tf_op jit(solution)/shard_map/ppermute | solution.py:294
  26.8 15.2 %copy-start = (f32[16,32,128]{2,1,0:T(8,128)S(1)}, f32[16,32,128]{2,1,0:T(8,128)}, u32[]{:S(2)}) copy-start(f32[16,32,128]{2,1,0:T(8,128)} %before.1) | copy-start | bytes 786436
  26.8 17.0 %collective-permute-start.3 = (f32[104,128]{1,0:T(8,128)S(1)}, f32[104,128]{1,0:T(8,128)S(1)}, u32[]{:S(2)}, u32[]{:S(2)}) collective-permute-start(f32[104,128]{1,0:T(8,128)S(1)} %get-tuple-element.50), channel_id=1, source_target_pairs={{0,12},{12,24},{24,36},{1,13},{13,25},{25,37},{2,14},{14,26},{26,3... | collective-permute-start | bytes 159752 | tf_op jit(solution)/shard_map/ppermute | solution.py:297
  30.4 13.5 %collective-permute-start.4 = (f32[104,128]{1,0:T(8,128)S(1)}, f32[104,128]{1,0:T(8,128)S(1)}, u32[]{:S(2)}, u32[]{:S(2)}) collective-permute-start(f32[104,128]{1,0:T(8,128)S(1)} %get-tuple-element.51), channel_id=1, source_target_pairs={{12,0},{24,12},{36,24},{13,1},{25,13},{37,25},{14,2},{26,14},{38,2... | collective-permute-start | bytes 159752 | tf_op jit(solution)/shard_map/ppermute | solution.py:298
  38.5 3.5 %copy-start.3 = (s32[16]{0:T(128)S(1)}, s32[16]{0:T(128)}, u32[]{:S(2)}) copy-start(s32[16]{0:T(128)} %param.11) | copy-start | bytes 196
  38.5 8.6 %collective-permute-start.5 = (f32[168,128]{1,0:T(8,128)S(1)}, f32[168,128]{1,0:T(8,128)S(1)}, u32[]{:S(2)}, u32[]{:S(2)}) collective-permute-start(f32[168,128]{1,0:T(8,128)S(1)} %get-tuple-element.84), channel_id=1, source_target_pairs={{0,96},{48,720},{96,192},{144,48},{192,288},{240,144},{288,384},{3... | collective-permute-start | bytes 258056 | tf_op jit(solution)/shard_map/ppermute | solution.py:300
  47.6 16.7 %collective-permute-start.6 = (f32[320,128]{1,0:T(8,128)S(1)}, f32[320,128]{1,0:T(8,128)S(1)}, u32[]{:S(2)}, u32[]{:S(2)}) collective-permute-start(f32[320,128]{1,0:T(8,128)S(1)} %get-tuple-element.55), channel_id=1, source_target_pairs={{0,48},{48,0},{96,144},{144,96},{192,240},{240,192},{288,336},{336... | collective-permute-start | bytes 491528 | tf_op jit(solution)/shard_map/ppermute | solution.py:294
  64.3 12.6 %collective-permute-start.9 = (f32[160,128]{1,0:T(8,128)S(1)}, f32[160,128]{1,0:T(8,128)S(1)}, u32[]{:S(2)}, u32[]{:S(2)}) collective-permute-start(f32[160,128]{1,0:T(8,128)S(1)} %get-tuple-element.86), channel_id=1, source_target_pairs={{0,96},{48,720},{96,192},{144,48},{192,288},{240,144},{288,384},{3... | collective-permute-start | bytes 245768 | tf_op jit(solution)/shard_map/ppermute | solution.py:300
  66.6 6.0 %collective-permute-start.7 = (f32[96,128]{1,0:T(8,128)S(1)}, f32[96,128]{1,0:T(8,128)S(1)}, u32[]{:S(2)}, u32[]{:S(2)}) collective-permute-start(f32[96,128]{1,0:T(8,128)S(1)} %get-tuple-element.56), channel_id=1, source_target_pairs={{0,12},{12,24},{24,36},{1,13},{13,25},{25,37},{2,14},{14,26},{26,3... | collective-permute-start | bytes 147464 | tf_op jit(solution)/shard_map/ppermute | solution.py:297
  70.2 6.0 %collective-permute-start.8 = (f32[96,128]{1,0:T(8,128)S(1)}, f32[96,128]{1,0:T(8,128)S(1)}, u32[]{:S(2)}, u32[]{:S(2)}) collective-permute-start(f32[96,128]{1,0:T(8,128)S(1)} %get-tuple-element.57), channel_id=1, source_target_pairs={{12,0},{24,12},{36,24},{13,1},{25,13},{37,25},{14,2},{26,14},{38,2... | collective-permute-start | bytes 147464 | tf_op jit(solution)/shard_map/ppermute | solution.py:298
  77.5 17.8 %collective-permute-start.10 = (f32[304,128]{1,0:T(8,128)S(1)}, f32[304,128]{1,0:T(8,128)S(1)}, u32[]{:S(2)}, u32[]{:S(2)}) collective-permute-start(f32[304,128]{1,0:T(8,128)S(1)} %get-tuple-element.61), channel_id=1, source_target_pairs={{0,48},{48,0},{96,144},{144,96},{192,240},{240,192},{288,336},{336... | collective-permute-start | bytes 466952 | tf_op jit(solution)/shard_map/ppermute | solution.py:294
  95.3 12.6 %collective-permute-start.13 = (f32[152,128]{1,0:T(8,128)S(1)}, f32[152,128]{1,0:T(8,128)S(1)}, u32[]{:S(2)}, u32[]{:S(2)}) collective-permute-start(f32[152,128]{1,0:T(8,128)S(1)} %get-tuple-element.88), channel_id=1, source_target_pairs={{0,96},{48,720},{96,192},{144,48},{192,288},{240,144},{288,384},{3... | collective-permute-start | bytes 233480 | tf_op jit(solution)/shard_map/ppermute | solution.py:300
  97.5 6.2 %collective-permute-start.11 = (f32[88,128]{1,0:T(8,128)S(1)}, f32[88,128]{1,0:T(8,128)S(1)}, u32[]{:S(2)}, u32[]{:S(2)}) collective-permute-start(f32[88,128]{1,0:T(8,128)S(1)} %get-tuple-element.62), channel_id=1, source_target_pairs={{0,12},{12,24},{24,36},{1,13},{13,25},{25,37},{2,14},{14,26},{26,3... | collective-permute-start | bytes 135176 | tf_op jit(solution)/shard_map/ppermute | solution.py:297
  101.3 5.9 %collective-permute-start.12 = (f32[88,128]{1,0:T(8,128)S(1)}, f32[88,128]{1,0:T(8,128)S(1)}, u32[]{:S(2)}, u32[]{:S(2)}) collective-permute-start(f32[88,128]{1,0:T(8,128)S(1)} %get-tuple-element.63), channel_id=1, source_target_pairs={{12,0},{24,12},{36,24},{13,1},{25,13},{37,25},{14,2},{26,14},{38,2... | collective-permute-start | bytes 135176 | tf_op jit(solution)/shard_map/ppermute | solution.py:298
  108.5 14.9 %collective-permute-start.14 = (f32[288,128]{1,0:T(8,128)S(1)}, f32[288,128]{1,0:T(8,128)S(1)}, u32[]{:S(2)}, u32[]{:S(2)}) collective-permute-start(f32[288,128]{1,0:T(8,128)S(1)} %get-tuple-element.67), channel_id=1, source_target_pairs={{0,48},{48,0},{96,144},{144,96},{192,240},{240,192},{288,336},{336... | collective-permute-start | bytes 442376 | tf_op jit(solution)/shard_map/ppermute | solution.py:294
  123.5 13.0 %collective-permute-start.17 = (f32[144,128]{1,0:T(8,128)S(1)}, f32[144,128]{1,0:T(8,128)S(1)}, u32[]{:S(2)}, u32[]{:S(2)}) collective-permute-start(f32[144,128]{1,0:T(8,128)S(1)} %get-tuple-element.90), channel_id=1, source_target_pairs={{0,96},{48,720},{96,192},{144,48},{192,288},{240,144},{288,384},{3... | collective-permute-start | bytes 221192 | tf_op jit(solution)/shard_map/ppermute | solution.py:300
  128.5 3.9 %collective-permute-start.15 = (f32[80,128]{1,0:T(8,128)S(1)}, f32[80,128]{1,0:T(8,128)S(1)}, u32[]{:S(2)}, u32[]{:S(2)}) collective-permute-start(f32[80,128]{1,0:T(8,128)S(1)} %get-tuple-element.68), channel_id=1, source_target_pairs={{0,12},{12,24},{24,36},{1,13},{13,25},{25,37},{2,14},{14,26},{26,3... | collective-permute-start | bytes 122888 | tf_op jit(solution)/shard_map/ppermute | solution.py:297
  129.8 5.9 %collective-permute-start.16 = (f32[80,128]{1,0:T(8,128)S(1)}, f32[80,128]{1,0:T(8,128)S(1)}, u32[]{:S(2)}, u32[]{:S(2)}) collective-permute-start(f32[80,128]{1,0:T(8,128)S(1)} %get-tuple-element.69), channel_id=1, source_target_pairs={{12,0},{24,12},{36,24},{13,1},{25,13},{37,25},{14,2},{26,14},{38,2... | collective-permute-start | bytes 122888 | tf_op jit(solution)/shard_map/ppermute | solution.py:298
  137.1 13.5 %collective-permute-start.18 = (f32[272,128]{1,0:T(8,128)S(1)}, f32[272,128]{1,0:T(8,128)S(1)}, u32[]{:S(2)}, u32[]{:S(2)}) collective-permute-start(f32[272,128]{1,0:T(8,128)S(1)} %get-tuple-element.73), channel_id=1, source_target_pairs={{0,48},{48,0},{96,144},{144,96},{192,240},{240,192},{288,336},{336... | collective-permute-start | bytes 417800 | tf_op jit(solution)/shard_map/ppermute | solution.py:294
  150.6 13.6 %collective-permute-start.21 = (f32[136,128]{1,0:T(8,128)S(1)}, f32[136,128]{1,0:T(8,128)S(1)}, u32[]{:S(2)}, u32[]{:S(2)}) collective-permute-start(f32[136,128]{1,0:T(8,128)S(1)} %get-tuple-element.92), channel_id=1, source_target_pairs={{0,96},{48,720},{96,192},{144,48},{192,288},{240,144},{288,384},{3... | collective-permute-start | bytes 208904 | tf_op jit(solution)/shard_map/ppermute | solution.py:300
  154.7 5.5 %collective-permute-start.19 = (f32[72,128]{1,0:T(8,128)S(1)}, f32[72,128]{1,0:T(8,128)S(1)}, u32[]{:S(2)}, u32[]{:S(2)}) collective-permute-start(f32[72,128]{1,0:T(8,128)S(1)} %get-tuple-element.74), channel_id=1, source_target_pairs={{0,12},{12,24},{24,36},{1,13},{13,25},{25,37},{2,14},{14,26},{26,3... | collective-permute-start | bytes 110600 | tf_op jit(solution)/shard_map/ppermute | solution.py:297
  157.8 5.9 %collective-permute-start.20 = (f32[72,128]{1,0:T(8,128)S(1)}, f32[72,128]{1,0:T(8,128)S(1)}, u32[]{:S(2)}, u32[]{:S(2)}) collective-permute-start(f32[72,128]{1,0:T(8,128)S(1)} %get-tuple-element.75), channel_id=1, source_target_pairs={{12,0},{24,12},{36,24},{13,1},{25,13},{37,25},{14,2},{26,14},{38,2... | collective-permute-start | bytes 110600 | tf_op jit(solution)/shard_map/ppermute | solution.py:298
  164.5 15.4 %collective-permute-start.22 = (f32[256,128]{1,0:T(8,128)S(1)}, f32[256,128]{1,0:T(8,128)S(1)}, u32[]{:S(2)}, u32[]{:S(2)}) collective-permute-start(f32[256,128]{1,0:T(8,128)S(1)} %get-tuple-element.80), channel_id=1, source_target_pairs={{0,48},{48,0},{96,144},{144,96},{192,240},{240,192},{288,336},{336... | collective-permute-start | bytes 393224 | tf_op jit(solution)/shard_map/ppermute | solution.py:294
  179.9 12.7 %collective-permute-start.25 = (f32[128,128]{1,0:T(8,128)S(1)}, f32[128,128]{1,0:T(8,128)S(1)}, u32[]{:S(2)}, u32[]{:S(2)}) collective-permute-start(f32[128,128]{1,0:T(8,128)S(1)} %get-tuple-element.94), channel_id=1, source_target_pairs={{0,96},{48,720},{96,192},{144,48},{192,288},{240,144},{288,384},{3... | collective-permute-start | bytes 196616 | tf_op jit(solution)/shard_map/ppermute | solution.py:300
  181.8 7.3 %collective-permute-start.23 = (f32[64,128]{1,0:T(8,128)S(1)}, f32[64,128]{1,0:T(8,128)S(1)}, u32[]{:S(2)}, u32[]{:S(2)}) collective-permute-start(f32[64,128]{1,0:T(8,128)S(1)} %get-tuple-element.81), channel_id=1, source_target_pairs={{0,12},{12,24},{24,36},{1,13},{13,25},{25,37},{2,14},{14,26},{26,3... | collective-permute-start | bytes 98312 | tf_op jit(solution)/shard_map/ppermute | solution.py:297
  186.5 5.8 %collective-permute-start.24 = (f32[64,128]{1,0:T(8,128)S(1)}, f32[64,128]{1,0:T(8,128)S(1)}, u32[]{:S(2)}, u32[]{:S(2)}) collective-permute-start(f32[64,128]{1,0:T(8,128)S(1)} %get-tuple-element.82), channel_id=1, source_target_pairs={{12,0},{24,12},{36,24},{13,1},{25,13},{37,25},{14,2},{26,14},{38,2... | collective-permute-start | bytes 98312 | tf_op jit(solution)/shard_map/ppermute | solution.py:298
